TPU v7x, 16 devices: a whole 2x2x2 slice. The times are simulated.
16 devices in a mesh: col: 2 (over z), row: 8 (over y, x, core).
Axes of the slice: x: 2, y: 2, z: 2, core: 2. Of those that a mesh axis runs over, the one named last changes fastest.
Arguments:
- w_gate: float32 [4096, 10240], P('row', 'col')
- w_up: float32 [4096, 10240], P('row', 'col')
- w_down: float32 [10240, 4096], P('row', 'col')
- x_norm: bfloat16 [4096, 4096], P(None, 'row')
- x_act: bfloat16 [4096, 10240], P(None, 'row')
- dy_gate: bfloat16 [4096, 10240], P(None, 'col')
- dy_up: bfloat16 [4096, 10240], P(None, 'col')
- dy_down: bfloat16 [4096, 4096], P(None, 'col')
- r_gate: float32 [4096], P('row')
- c_gate: float32 [10240], P('col')
- r_up: float32 [4096], P('row')
- c_up: float32 [10240], P('col')
- r_down: float32 [10240], P('row')
- c_down: float32 [4096], P('col')
- hyper_params: float32 [3], replicated
Outputs:
- output 1: float32 [4096, 10240], P('row', 'col')
- output 2: float32 [4096, 10240], P('row', 'col')
- output 3: float32 [10240, 4096], P('row', 'col')
- output 4: float32 [4096], P('row')
- output 5: float32 [10240], P('col')
- output 6: float32 [4096], P('row')
- output 7: float32 [10240], P('col')
- output 8: float32 [10240], P('row')
- output 9: float32 [4096], P('col')
- output 10: bfloat16 [4096, 4096], P(None, 'row')
- output 11: bfloat16 [4096, 10240], P(None, 'row')
All inputs are finite; a program needn't handle non-finite values.
Results may differ from a plain program's by a relative error of at most 0.001.
Values are sent between devices in bfloat16 or wider.
A program may use at most 1 GiB of HBM per device.

v0:
```python
import jax
import jax.numpy as jnp
from jax import lax
from jax.sharding import PartitionSpec as P

EPS_ONE = 1e-30
EPS_TWO = 1e-3


def factored_step(w_loc, grad_loc, r_loc, c_loc, hyper_params, m_total, n_total):
    beta_two = hyper_params[0]
    grad_sq = grad_loc * grad_loc + EPS_ONE
    row_sum = lax.psum(jnp.sum(grad_sq, axis=1), 'col')
    col_sum = lax.psum(jnp.sum(grad_sq, axis=0), 'row')
    r_new = beta_two * r_loc + (1.0 - beta_two) * (row_sum / n_total)
    c_new = beta_two * c_loc + (1.0 - beta_two) * (col_sum / m_total)
    r_mean = lax.psum(jnp.sum(r_new), 'row') / m_total
    update = grad_loc * lax.rsqrt(r_new[:, None] * c_new[None, :] / r_mean)
    u_sq = lax.psum(jnp.sum(update * update), ('row', 'col'))
    rms_u = jnp.sqrt(u_sq / (m_total * n_total))
    update_hat = update / jnp.maximum(1.0, rms_u / hyper_params[2])
    w_sq = lax.psum(jnp.sum(w_loc * w_loc), ('row', 'col'))
    step_size = hyper_params[1] * jnp.maximum(EPS_TWO, jnp.sqrt(w_sq / (m_total * n_total)))
    return w_loc - step_size * update_hat, r_new, c_new


def weight_grad(activations, grad_out):
    return lax.dot_general(activations, grad_out, (((0,), (0,)), ((), ())), preferred_element_type=jnp.float32)


def input_grad(grad_out, weight):
    return lax.dot_general(grad_out, weight.astype(jnp.bfloat16), (((1,), (1,)), ((), ())), preferred_element_type=jnp.float32)


def solution(mesh):
    row_size = mesh.shape['row']
    col_size = mesh.shape['col']
    weight_spec = P('row', 'col')
    act_spec = P(None, 'row')
    grad_spec = P(None, 'col')
    in_specs = (weight_spec,) * 3 + (act_spec, act_spec) + (grad_spec,) * 3 + (P('row'), P('col')) * 3 + (P(),)
    out_specs = (weight_spec,) * 3 + (P('row'), P('col')) * 3 + (act_spec, act_spec)

    def body(w_gate, w_up, w_down, x_norm, x_act, dy_gate, dy_up, dy_down, r_gate, c_gate, r_up, c_up, r_down, c_down, hyper_params):
        d_model = w_gate.shape[0] * row_size
        d_ff = w_gate.shape[1] * col_size
        new_gate, r_gate_new, c_gate_new = factored_step(w_gate, weight_grad(x_norm, dy_gate), r_gate, c_gate, hyper_params, d_model, d_ff)
        new_up, r_up_new, c_up_new = factored_step(w_up, weight_grad(x_norm, dy_up), r_up, c_up, hyper_params, d_model, d_ff)
        new_down, r_down_new, c_down_new = factored_step(w_down, weight_grad(x_act, dy_down), r_down, c_down, hyper_params, d_ff, d_model)
        dx_norm = lax.psum(input_grad(dy_gate, w_gate) + input_grad(dy_up, w_up), 'col').astype(jnp.bfloat16)
        dx_act = lax.psum(input_grad(dy_down, w_down), 'col').astype(jnp.bfloat16)
        return (new_gate, new_up, new_down, r_gate_new, c_gate_new, r_up_new, c_up_new, r_down_new, c_down_new, dx_norm, dx_act)

    return jax.shard_map(body, mesh=mesh, in_specs=in_specs, out_specs=out_specs, check_vma=False)
```

profile of v0, /device:TPU:0, one launch (start us, length us, event | category | flops | bytes accessed | tf_op | source)
XLA Modules:
  0.0 1000.3 jit_solution(5983184014509871256)
XLA Ops:
  0.7 30.8 %fusion.2 = (f32[5120]{0:T(1024)}, f32[512]{0:T(512)}, f32[512,5120]{1,0:T(8,128)}) fusion(bf16[4096,512]{1,0:T(8,128)(2,1)} %param.18, bf16[4096,5120]{1,0:T(8,128)(2,1)} %param.21), kind=kOutput, calls=%fused_computation.17 | convolution fusion | flops 21485318144 | bytes 56645632 | tf_op jit(solution)/shard_map/dot_general | solution.py:28
  31.5 29.8 %fusion = (f32[5120]{0:T(1024)}, f32[512]{0:T(512)}, f32[512,5120]{1,0:T(8,128)}) fusion(bf16[4096,512]{1,0:T(8,128)(2,1)S(1)} %copy-done.17, bf16[4096,5120]{1,0:T(8,128)(2,1)} %param.20), kind=kOutput, calls=%fused_computation.15 | convolution fusion | flops 21485318144 | bytes 56645632 | tf_op jit(solution)/shard_map/dot_general | solution.py:28
  61.3 30.8 %fusion.4 = (f32[2048]{0:T(1024)S(1)}, f32[1280]{0:T(1024)S(1)}, f32[1280,2048]{1,0:T(8,128)}) fusion(bf16[4096,1280]{1,0:T(8,128)(2,1)} %param.19, bf16[4096,2048]{1,0:T(8,128)(2,1)} %param.22), kind=kOutput, calls=%fused_computation.19 | convolution fusion | flops 21485318144 | bytes 37762048 | tf_op jit(solution)/shard_map/dot_general | solution.py:28
  92.1 27.1 %fusion.6 = f32[4096,1280]{1,0:T(8,128)} fusion(bf16[4096,2048]{1,0:T(8,128)(2,1)} %param.22, f32[1280,2048]{1,0:T(8,128)S(1)} %bitcast.13), kind=kOutput, calls=%fused_computation.22 | convolution fusion | flops 21477457920 | bytes 48234496 | tf_op jit(solution)/shard_map/dot_general | solution.py:32
  119.3 30.9 %fusion.9 = f32[4096,512]{1,0:T(8,128)} fusion(bf16[4096,5120]{1,0:T(8,128)(2,1)} %param.20, f32[512,5120]{1,0:T(8,128)} %param.15), kind=kOutput, calls=%fused_computation.25 | convolution fusion | flops 21477457920 | bytes 60817408 | tf_op jit(solution)/shard_map/dot_general | solution.py:32
  150.2 31.3 %convolution_add_fusion = f32[4096,512]{1,0:T(8,128)} fusion(f32[4096,512]{1,0:T(8,128)} %fusion.9, bf16[4096,5120]{1,0:T(8,128)(2,1)} %param.21, f32[512,5120]{1,0:T(8,128)} %param.16), kind=kOutput, calls=%fused_computation.21 | convolution fusion | flops 21479555072 | bytes 69206016 | tf_op jit(solution)/shard_map/dot_general | solution.py:32
  181.5 0.0 copy-start.12
  181.5 0.0 copy-start.15
  181.5 0.0 copy-start.16
  181.5 0.0 copy-start.10
  181.6 0.0 copy-start.5
  181.6 0.0 copy-start.11
  181.6 669.3 %all-reduce.4 = (f32[512]{0:T(512)S(1)}, f32[512]{0:T(512)S(1)}, f32[1280]{0:T(1024)S(1)}, bf16[4096,512]{1,0:T(8,128)(2,1)}, bf16[4096,1280]{1,0:T(8,128)(2,1)}) all-reduce(f32[512]{0:T(512)S(1)} %copy-done.14, f32[512]{0:T(512)S(1)} %copy-done.13, f32[1280]{0:T(1024)S(1)} %get-tuple-element.12, ...), channel_id=1, replica_groups=mesh['col'=2,'row'=8] {'col'}, use_global_device_ids=true, to_apply=%region_3.0 | all-reduce | flops 7342336 | bytes 44058624 | tf_op jit(solution)/shard_map/psum | solution.py:13
  850.8 0.7 fusion.14
  852.2 1.3 fusion.12
  853.4 1.2 fusion.11
  854.7 23.1 %all-reduce.1 = (f32[]{:T(128)}, f32[5120]{0:T(1024)S(1)}, f32[]{:T(128)}, f32[5120]{0:T(1024)S(1)}, f32[]{:T(128)}, /*index=5*/f32[2048]{0:T(1024)S(1)}) all-reduce(f32[]{:T(128)} %get-tuple-element.46, f32[5120]{0:T(1024)S(1)} %copy-done.5, f32[]{:T(128)} %get-tuple-element.36, ...), channel_id=1, replica_groups=mesh['col'=2,'row'=8] {'row'}, use_global_device_ids=true, to_apply=%region_7.0 | all-reduce | flops 12291 | bytes 98328 | tf_op jit(solution)/shard_map/psum | solution.py:17
  877.8 0.6 multiply_add_fusion.5
  878.4 0.0 copy-start.3
  879.1 0.0 copy-start.7
  879.1 6.9 multiply_reduce_fusion
  886.0 0.6 multiply_add_fusion.3
  887.3 7.4 multiply_reduce_fusion.2
  894.7 0.6 multiply_add_fusion.4
  895.3 0.0 copy-start.1
  896.0 7.4 multiply_reduce_fusion.4
  903.4 10.3 %multiply_reduce_fusion.3 = (f32[]{:T(128)}, f32[]{:T(128)}) fusion(f32[512,5120]{1,0:T(8,128)} %param.16, f32[512,5120]{1,0:T(8,128)} %param.15), kind=kLoop, calls=%fused_computation.9 | loop fusion | flops 10485758 | bytes 20971528 | tf_op jit(solution)/shard_map/reduce_sum | solution.py:22
  913.7 7.3 multiply_reduce_fusion.1
  921.0 32.4 %all-reduce = (f32[]{:T(128)}, f32[]{:T(128)}, f32[]{:T(128)}, f32[]{:T(128)}, f32[]{:T(128)}, /*index=5*/f32[]{:T(128)}) all-reduce(f32[]{:T(128)} %multiply_reduce_fusion.4, f32[]{:T(128)} %get-tuple-element.49, f32[]{:T(128)} %multiply_reduce_fusion.2, f32[]{:T(128)} %get-tuple-element.48, ...), channel_id=1, replica_groups=mesh['col'=2,'row'=8] {'row','col'}, use_global_device_ids=true, to_apply=%region_9.0 | all-reduce | flops 6 | bytes 48 | tf_op jit(solution)/shard_map/psum | solution.py:19
  956.1 13.2 %multiply_subtract_fusion = f32[1280,2048]{1,0:T(8,128)} fusion(f32[1280,2048]{1,0:T(8,128)} %param.17, f32[]{:T(128)S(6)} %max.23, f32[]{:T(128)S(6)} %mul.205, f32[1280,2048]{1,0:T(8,128)} %get-tuple-element.45, f32[]{:T(128)S(6)} %div.97, f32[2048]{0:T(1024)S(1)} %multiply_add_fusion.5, f32[1280]{0:T(1024)S(1)} %get-tuple-element.35), kind=kLoop, calls=%fused_computation | loop fusion | flops 15728640 | bytes 31470604 | tf_op jit(solution)/shard_map/sub | solution.py:24
  972.0 12.7 %multiply_subtract_fusion.1 = f32[512,5120]{1,0:T(8,128)} fusion(f32[512,5120]{1,0:T(8,128)} %param.16, f32[]{:T(128)S(6)} %max.21, f32[]{:T(128)S(6)} %mul.191, f32[512,5120]{1,0:T(8,128)} %get-tuple-element.44, f32[]{:T(128)S(6)} %div.89, f32[5120]{0:T(1024)S(1)} %multiply_add_fusion.3, f32[512]{0:T(512)S(1)} %get-tuple-element.37), kind=kLoop, calls=%fused_computation.5 | loop fusion | flops 15728640 | bytes 31479820 | tf_op jit(solution)/shard_map/sub | solution.py:24
  987.2 12.7 %multiply_subtract_fusion.2 = f32[512,5120]{1,0:T(8,128)} fusion(f32[512,5120]{1,0:T(8,128)} %param.15, f32[]{:T(128)S(6)} %max.19, f32[]{:T(128)S(6)} %mul.171, f32[512,5120]{1,0:T(8,128)} %get-tuple-element.43, f32[]{:T(128)S(6)} %div.81, f32[5120]{0:T(1024)S(1)} %multiply_add_fusion.4, f32[512]{0:T(512)S(1)} %get-tuple-element.47), kind=kLoop, calls=%fused_computation.10 | loop fusion | flops 15728640 | bytes 31479820 | tf_op jit(solution)/shard_map/sub | solution.py:24
  (34 shorter events, 0.1 us)
Async XLA Ops:
  0.6 30.9 %copy-start.17 = (bf16[4096,512]{1,0:T(8,128)(2,1)S(1)}, bf16[4096,512]{1,0:T(8,128)(2,1)}, u32[]{:S(2)}) copy-start(bf16[4096,512]{1,0:T(8,128)(2,1)} %param.18) | copy-start | bytes 12582916
  31.5 60.6 %slice-start = ((s8[10485760]{0:T(1024)(128)(4,1)}), s8[4194304]{0:T(1024)(128)(4,1)S(1)}, s32[]{:S(2)}) async-start(s8[10485760]{0:T(1024)(128)(4,1)} %bitcast.12), calls=%async_computation | async-start | bytes 8388608
  31.5 60.6 %slice-start.1 = ((s8[10485760]{0:T(1024)(128)(4,1)}), s8[4194304]{0:T(1024)(128)(4,1)S(1)}, s32[]{:S(2)}) async-start(s8[10485760]{0:T(1024)(128)(4,1)} %bitcast.12), calls=%async_computation.1 | async-start | bytes 8388608
  61.3 30.8 %slice-start.2 = ((s8[10485760]{0:T(1024)(128)(4,1)}), s8[2097152]{0:T(1024)(128)(4,1)S(1)}, s32[]{:S(2)}) async-start(s8[10485760]{0:T(1024)(128)(4,1)} %bitcast.12), calls=%async_computation.2 | async-start | bytes 4194304
  150.2 31.3 %copy-start.13 = (f32[512]{0:T(512)S(1)}, f32[512]{0:T(512)}, u32[]{:S(2)}) copy-start(f32[512]{0:T(512)} %get-tuple-element.14) | copy-start | bytes 6148
  150.2 31.3 %copy-start.14 = (f32[512]{0:T(512)S(1)}, f32[512]{0:T(512)}, u32[]{:S(2)}) copy-start(f32[512]{0:T(512)} %get-tuple-element.16) | copy-start | bytes 6148
  181.5 669.3 %copy-start.12 = (f32[3]{0:T(128)S(1)}, f32[3]{0:T(128)}, u32[]{:S(2)}) copy-start(f32[3]{0:T(128)} %param.29) | copy-start | bytes 40
  181.5 670.6 %copy-start.15 = (f32[512]{0:T(512)S(1)}, f32[512]{0:T(512)}, u32[]{:S(2)}) copy-start(f32[512]{0:T(512)} %param.25) | copy-start | bytes 6148
  181.5 670.6 %copy-start.16 = (f32[512]{0:T(512)S(1)}, f32[512]{0:T(512)}, u32[]{:S(2)}) copy-start(f32[512]{0:T(512)} %param.23) | copy-start | bytes 6148
  181.5 671.9 %copy-start.10 = (f32[1280]{0:T(1024)S(1)}, f32[1280]{0:T(1024)}, u32[]{:S(2)}) copy-start(f32[1280]{0:T(1024)} %param.27) | copy-start | bytes 15364
  181.5 673.1 %copy-start.4 = (f32[5120]{0:T(1024)S(1)}, f32[5120]{0:T(1024)}, u32[]{:S(2)}) copy-start(f32[5120]{0:T(1024)} %get-tuple-element.13) | copy-start | bytes 61444
  181.6 673.1 %copy-start.5 = (f32[5120]{0:T(1024)S(1)}, f32[5120]{0:T(1024)}, u32[]{:S(2)}) copy-start(f32[5120]{0:T(1024)} %get-tuple-element.15) | copy-start | bytes 61444
  181.6 696.2 %copy-start.11 = (f32[2048]{0:T(1024)S(1)}, f32[2048]{0:T(1024)}, u32[]{:S(2)}) copy-start(f32[2048]{0:T(1024)} %param.28) | copy-start | bytes 24580
  850.8 35.2 %copy-start.6 = (f32[5120]{0:T(1024)S(1)}, f32[5120]{0:T(1024)}, u32[]{:S(2)}) copy-start(f32[5120]{0:T(1024)} %param.26) | copy-start | bytes 61444
  853.4 118.5 %copy-start.8 = (f32[512]{0:T(512)}, f32[512]{0:T(512)S(1)}, u32[]{:S(2)}) copy-start(f32[512]{0:T(512)S(1)} %get-tuple-element.37) | copy-start | bytes 6148
  853.4 133.8 %copy-start.9 = (f32[512]{0:T(512)}, f32[512]{0:T(512)S(1)}, u32[]{:S(2)}) copy-start(f32[512]{0:T(512)S(1)} %get-tuple-element.47) | copy-start | bytes 6148
  854.7 101.4 %copy-start.2 = (f32[1280]{0:T(1024)}, f32[1280]{0:T(1024)S(1)}, u32[]{:S(2)}) copy-start(f32[1280]{0:T(1024)S(1)} %get-tuple-element.35) | copy-start | bytes 15364
  878.4 77.7 %copy-start.3 = (f32[2048]{0:T(1024)}, f32[2048]{0:T(1024)S(1)}, u32[]{:S(2)}) copy-start(f32[2048]{0:T(1024)S(1)} %multiply_add_fusion.5) | copy-start | bytes 24580
  879.1 15.6 %copy-start.7 = (f32[5120]{0:T(1024)S(1)}, f32[5120]{0:T(1024)}, u32[]{:S(2)}) copy-start(f32[5120]{0:T(1024)} %param.24) | copy-start | bytes 61444
  886.6 85.3 %copy-start = (f32[5120]{0:T(1024)}, f32[5120]{0:T(1024)S(1)}, u32[]{:S(2)}) copy-start(f32[5120]{0:T(1024)S(1)} %multiply_add_fusion.3) | copy-start | bytes 61444
  895.3 91.9 %copy-start.1 = (f32[5120]{0:T(1024)}, f32[5120]{0:T(1024)S(1)}, u32[]{:S(2)}) copy-start(f32[5120]{0:T(1024)S(1)} %multiply_add_fusion.4) | copy-start | bytes 61444
where the time goes:
time: 1010 us; the launch traced here: 1000 us
  blocking collectives  725 us (72%)
  matrix products  181 us (18%)
  other arithmetic  82.3 us (8%)
  between operations  11.7 us (1%)
    psum x1, blocking collectives, factored_step(): row_sum = lax.psum(jnp.sum(grad_sq, axis=1), 'col')  669 us
    dot_general x3, matrix products, weight_grad(): lax.dot_general(activations, grad_out, (((0,), (0,)), ((), ())), preferre...  91.5 us
    dot_general x3, matrix products, input_grad(): lax.dot_general(grad_out, weight.astype(jnp.bfloat16), (((1,), (1,)), (()...  89.3 us
    sub x3, other arithmetic, factored_step(): return (w_loc - step_size * update_hat, r_new, c_new)  38.5 us
    psum x1, blocking collectives, factored_step(): u_sq = lax.psum(jnp.sum(update * update), ('row', 'col'))  32.4 us
    psum x1, blocking collectives, factored_step(): r_mean = lax.psum(jnp.sum(r_new), 'row') / m_total  23.1 us
    reduce_sum x3, other arithmetic, factored_step(): u_sq = lax.psum(jnp.sum(update * update), ('row', 'col'))  21.7 us

commit v1 on v0

v1 whole, which is shorter than its diff:
```python
import jax
import jax.numpy as jnp
from jax import lax
from jax.experimental import pallas as pl
from jax.experimental.pallas import tpu as pltpu
from jax.sharding import PartitionSpec as P

EPS_ONE = 1e-30
EPS_TWO = 1e-3
F32 = jnp.float32
BF16 = jnp.bfloat16
VMEM_LIMIT = 60 * 1024 * 1024
NT = (((1,), (1,)), ((), ()))


def params(*semantics):
    return pltpu.CompilerParams(dimension_semantics=semantics, vmem_limit_bytes=VMEM_LIMIT)


def cost(flops, nbytes):
    return pl.CostEstimate(flops=int(flops), bytes_accessed=int(nbytes), transcendentals=0)


def cast_kernel(w_ref, b_ref, s_ref):
    w = w_ref[...]
    b_ref[...] = w.astype(BF16)

    @pl.when(pl.program_id(0) == 0)
    def _():
        s_ref[...] = jnp.zeros_like(s_ref)

    s_ref[...] += jnp.sum((w * w).reshape(w.shape[0] // 8, 8, w.shape[1]), axis=0)


def cast_weight(w):
    rows, cols = w.shape
    tile = 128
    b, s = pl.pallas_call(
        cast_kernel,
        grid=(rows // tile,),
        in_specs=[pl.BlockSpec((tile, cols), lambda i: (i, 0))],
        out_specs=[pl.BlockSpec((tile, cols), lambda i: (i, 0)), pl.BlockSpec((8, cols), lambda i: (0, 0))],
        out_shape=[jax.ShapeDtypeStruct((rows, cols), BF16), jax.ShapeDtypeStruct((8, cols), F32)],
        compiler_params=params('arbitrary'),
        cost_estimate=cost(w.size * 3, w.size * 6),
        name='cast_weight',
    )(w)
    return b, jnp.sum(s)


def grad_kernel(x_ref, dy_ref, g_ref, row_ref, col_ref, xt_ref):
    step = pl.program_id(0)

    @pl.when(step == 0)
    def _():
        row_ref[...] = jnp.zeros_like(row_ref)
        xt_ref[...] = x_ref[...].T

    g = jnp.dot(xt_ref[...], dy_ref[...], preferred_element_type=F32)
    g_ref[...] = g
    q = g * g + EPS_ONE
    col_ref[...] = jnp.sum(q, axis=0, keepdims=True)
    part = q[:, :128]
    for k in range(1, q.shape[1] // 128):
        part += q[:, k * 128:(k + 1) * 128]
    row_ref[...] += part


def weight_grad(x, dy, tile):
    tokens, m = x.shape
    n = dy.shape[1]
    g, row, col = pl.pallas_call(
        grad_kernel,
        grid=(n // tile,),
        in_specs=[
            pl.BlockSpec((tokens, m), lambda j: (0, 0), pipeline_mode=pl.Buffered(1)),
            pl.BlockSpec((tokens, tile), lambda j: (0, j)),
        ],
        out_specs=[
            pl.BlockSpec((m, tile), lambda j: (0, j)),
            pl.BlockSpec((m, 128), lambda j: (0, 0)),
            pl.BlockSpec((1, tile), lambda j: (0, j)),
        ],
        out_shape=[
            jax.ShapeDtypeStruct((m, n), F32),
            jax.ShapeDtypeStruct((m, 128), F32),
            jax.ShapeDtypeStruct((1, n), F32),
        ],
        scratch_shapes=[pltpu.VMEM((m, tokens), BF16)],
        compiler_params=params('arbitrary'),
        cost_estimate=cost(2 * tokens * m * n, 2 * tokens * (m + n) + 4 * m * n),
        name='weight_grad',
    )(x, dy)
    return g, jnp.sum(row, axis=1), col[0]


def norm_kernel(off_ref, dyg_ref, dyu_ref, wg_ref, wu_ref, out_ref):
    out_ref[...] = lax.dot_general(dyg_ref[...], wg_ref[...], NT, preferred_element_type=F32) + lax.dot_general(
        dyu_ref[...], wu_ref[...], NT, preferred_element_type=F32)


def norm_partial(offset, tokens, dyg, dyu, wg, wu):
    tile = 512
    m, n = wg.shape
    dy_spec = pl.BlockSpec((tile, n), lambda i, off: (off[0] + i, 0))
    w_spec = pl.BlockSpec((m, n), lambda i, off: (0, 0), pipeline_mode=pl.Buffered(1))
    return pl.pallas_call(
        norm_kernel,
        grid_spec=pltpu.PrefetchScalarGridSpec(
            num_scalar_prefetch=1,
            grid=(tokens // tile,),
            in_specs=[dy_spec, dy_spec, w_spec, w_spec],
            out_specs=pl.BlockSpec((tile, m), lambda i, off: (i, 0)),
        ),
        out_shape=jax.ShapeDtypeStruct((tokens, m), F32),
        compiler_params=params('arbitrary'),
        cost_estimate=cost(4 * tokens * m * n, 4 * tokens * n + 4 * m * n + 4 * tokens * m),
        name='norm_partial',
    )((offset // tile).astype(jnp.int32).reshape(1), dyg, dyu, wg, wu)


def act_kernel(dya_ref, dyb_ref, wa_ref, wb_ref, out_ref, acc_ref):
    step = pl.program_id(1)

    @pl.when(step == 0)
    def _():
        acc_ref[...] = lax.dot_general(dya_ref[...], wa_ref[...], NT, preferred_element_type=F32)

    @pl.when(step == 1)
    def _():
        other = lax.dot_general(dyb_ref[...], wb_ref[...], NT, preferred_element_type=F32)
        out_ref[...] = (acc_ref[...] + other).astype(BF16)


def act_grad(dya, dyb, wa, wb):
    tile = 512
    tokens, n = dya.shape
    m = wa.shape[0]
    dy_spec = pl.BlockSpec((tile, n), lambda i, k: (i, 0))
    w_spec = pl.BlockSpec((m, n), lambda i, k: (0, 0), pipeline_mode=pl.Buffered(1))
    return pl.pallas_call(
        act_kernel,
        grid=(tokens // tile, 2),
        in_specs=[dy_spec, dy_spec, w_spec, w_spec],
        out_specs=pl.BlockSpec((tile, m), lambda i, k: (i, 0)),
        out_shape=jax.ShapeDtypeStruct((tokens, m), BF16),
        scratch_shapes=[pltpu.VMEM((tile, m), F32)],
        compiler_params=params('arbitrary', 'arbitrary'),
        cost_estimate=cost(4 * tokens * m * n, 4 * tokens * n + 4 * m * n + 2 * tokens * m),
        name='act_grad',
    )(dya, dyb, wa, wb)


def swap_col(v):
    return lax.ppermute(v, 'col', [(0, 1), (1, 0)])


def sum_row(v, row_size):
    step = 1
    while step < row_size:
        v = v + lax.ppermute(v, 'row', [(i, i ^ step) for i in range(row_size)])
        step *= 2
    return v


def solution(mesh):
    row_size = mesh.shape['row']
    col_size = mesh.shape['col']
    weight_spec = P('row', 'col')
    act_spec = P(None, 'row')
    grad_spec = P(None, 'col')
    in_specs = (weight_spec,) * 3 + (act_spec, act_spec) + (grad_spec,) * 3 + (P('row'), P('col')) * 3 + (P(),)
    out_specs = (weight_spec,) * 3 + (P('row'), P('col')) * 3 + (act_spec, act_spec)

    def body(w_gate, w_up, w_down, x_norm, x_act, dy_gate, dy_up, dy_down, r_gate, c_gate, r_up, c_up, r_down, c_down, hyper_params):
        row = lax.axis_index('row')
        col = lax.axis_index('col')
        tokens = x_norm.shape[0]
        half = tokens // col_size
        beta_two = hyper_params[0]

        share = tokens // row_size
        piece = swap_col(lax.dynamic_slice_in_dim(dy_down, row * share, share, axis=0))
        dy_down_other = lax.all_gather(piece, 'row', axis=0, tiled=True)

        b_gate, w_sq_gate = cast_weight(w_gate)
        b_up, w_sq_up = cast_weight(w_up)
        sent = norm_partial((1 - col) * half, half, dy_gate, dy_up, b_gate, b_up)
        got = swap_col(sent)

        b_down, w_sq_down = cast_weight(w_down)
        cut = 768
        b_down_other = [swap_col(b_down[:cut]), swap_col(b_down[cut:])]

        own = norm_partial(col * half, half, dy_gate, dy_up, b_gate, b_up)
        g_gate, row_gate, col_gate = weight_grad(x_norm, dy_gate, 512)
        g_up, row_up, col_up = weight_grad(x_norm, dy_up, 512)
        g_down, row_down, col_down = weight_grad(x_act, dy_down, 256)

        mine = (own + got).astype(BF16)
        theirs = swap_col(mine)
        dx_norm = jnp.where(col == 0, jnp.concatenate([mine, theirs]), jnp.concatenate([theirs, mine]))

        sizes_r = [r_gate.shape[0], r_up.shape[0], r_down.shape[0]]
        sizes_c = [c_gate.shape[0], c_up.shape[0], c_down.shape[0]]
        totals = [(sizes_r[k] * row_size, sizes_c[k] * col_size) for k in range(3)]
        row_all = jnp.concatenate([row_gate, row_up, row_down])
        row_all = row_all + swap_col(row_all)
        row_sums = jnp.split(row_all, [sizes_r[0], sizes_r[0] + sizes_r[1]])
        r_old = [r_gate, r_up, r_down]
        c_old = [c_gate, c_up, c_down]
        r_new = [beta_two * r_old[k] + (1.0 - beta_two) * (row_sums[k] / totals[k][1]) for k in range(3)]
        r_part = jnp.zeros((128,), F32).at[:3].set(jnp.stack([jnp.sum(r) for r in r_new]))
        col_all = sum_row(jnp.concatenate([col_gate, col_up, col_down, r_part]), row_size)
        offs = [0, sizes_c[0], sizes_c[0] + sizes_c[1], sum(sizes_c)]
        c_new = [
            beta_two * c_old[k] + (1.0 - beta_two) * (col_all[offs[k]:offs[k + 1]] / totals[k][0]) for k in range(3)
        ]
        r_mean = [col_all[offs[3] + k] / totals[k][0] for k in range(3)]
        grads = [g_gate, g_up, g_down]
        updates = [grads[k] * lax.rsqrt(r_new[k][:, None] * c_new[k][None, :] / r_mean[k]) for k in range(3)]
        scalars = jnp.stack([jnp.sum(u * u) for u in updates] + [w_sq_gate, w_sq_up, w_sq_down])
        scalars = sum_row(jnp.zeros((128,), F32).at[:6].set(scalars), row_size)
        scalars = scalars + swap_col(scalars)
        weights = [w_gate, w_up, w_down]
        new = []
        for k in range(3):
            size = totals[k][0] * totals[k][1]
            rms_u = jnp.sqrt(scalars[k] / size)
            step_size = hyper_params[1] * jnp.maximum(EPS_TWO, jnp.sqrt(scalars[3 + k] / size))
            new.append(weights[k] - step_size * (updates[k] / jnp.maximum(1.0, rms_u / hyper_params[2])))

        dx_act = jnp.concatenate(
            [
                act_grad(dy_down, dy_down_other, b_down[:cut], b_down_other[0]),
                act_grad(dy_down, dy_down_other, b_down[cut:], b_down_other[1]),
            ],
            axis=1,
        )
        return (*new, r_new[0], c_new[0], r_new[1], c_new[1], r_new[2], c_new[2], dx_norm, dx_act)

    return jax.shard_map(body, mesh=mesh, in_specs=in_specs, out_specs=out_specs, check_vma=False)
```

time: 1010 us -> 567 us (0.56)
  blocking collectives: 725 us -> 0 us
  Pallas kernels: 0 us -> 247 us
  matrix products: 181 us -> 0 us
  waiting for transfers between devices: 0 us -> 170 us
  starting transfers between devices: 0 us -> 16.3 us
  between operations: 11.7 us -> 25.5 us
  local copies, waits for them, and re-layouts: 0.77 us -> 14.3 us
    psum x3 -> x0, blocking collectives: 725 us -> none  [the longest x1 669 us: factored_step(): row_sum = lax.psum(jnp.sum(grad_sq, axis=1), 'col')]
    pallas_call x0 -> x10, Pallas kernels: none -> 247 us  [the longest x3 93.4 us: weight_grad(): pl.pallas_call(grad_kernel, grid=(n // tile,), in_specs=[pl.BlockSpec((to...]
    dot_general x6 -> x0, matrix products: 181 us -> none  [the longest x3 91.5 us: weight_grad(): lax.dot_general(activations, grad_out, (((0,), (0,)), ((), ())), preferre...]
    ppermute x0 -> x13, waiting for transfers between devices: none -> 170 us  [the longest x7 162 us: swap_col(): return lax.ppermute(v, 'col', [(0, 1), (1, 0)])]
    ppermute x0 -> x13, starting transfers between devices: none -> 16.2 us  [the longest x7 10.8 us: swap_col(): return lax.ppermute(v, 'col', [(0, 1), (1, 0)])]
    reduce_sum x7 -> x11, other arithmetic: 41.8 us -> 29.2 us  [the longest x3 19 us: body(): jnp.sum(u * u)]
    concatenate x0 -> x3, other arithmetic: none -> 10.4 us  [the longest x1 9.67 us: body(): jnp.concatenate([act_grad(dy_down, dy_down_other, b_down[:cut], b_down_ot...]
    sub x3 -> x2, other arithmetic: 38.5 us -> 34.7 us  [body(): weights[k]]
  transfers between devices with their start and end apart: 0 -> 14, of which waited for: 0 -> 8; matrix products, arithmetic and copies ran while one was open for 0% -> 15% of each run, Pallas kernels for 0% -> 38%
where the time goes in v1:
time: 567 us; the launch traced here: 557 us
  Pallas kernels  247 us (44%)
  waiting for transfers between devices  170 us (30%)
  other arithmetic  83.9 us (15%)
  between operations  25.5 us (4%)
  starting transfers between devices  16.3 us (3%)
  local copies, waits for them, and re-layouts  14.3 us (3%)
    ppermute x7, waiting for transfers between devices, swap_col(): return lax.ppermute(v, 'col', [(0, 1), (1, 0)])  162 us
    pallas_call x3, Pallas kernels, weight_grad(): pl.pallas_call(grad_kernel, grid=(n // tile,), in_specs=[pl.BlockSpec((to...  93.4 us
    pallas_call x2, Pallas kernels, act_grad(): pl.pallas_call(act_kernel, grid=(tokens // tile, 2), in_specs=[dy_spec, d...  69.1 us
    pallas_call x2, Pallas kernels, norm_partial(): pl.pallas_call(norm_kernel, grid_spec=pltpu.PrefetchScalarGridSpec(num_sc...  61.3 us
    sub x2, other arithmetic, body(): weights[k]  34.7 us
    pallas_call x3, Pallas kernels, cast_weight(): pl.pallas_call(cast_kernel, grid=(rows // tile,), in_specs=[pl.BlockSpec(...  23.4 us
    reduce_sum x3, other arithmetic, body(): jnp.sum(u * u)  19 us
  transfers between devices with their start and end apart: 14, of which 8 were waited for; matrix products, arithmetic and copies ran while one was open for 15% of the time, Pallas kernels for 38%

profile of v1, /device:TPU:0, one launch (start us, length us, event | category | flops | bytes accessed | tf_op | source)
XLA Modules:
  0.0 557.0 jit_solution(9318272433136721969)
XLA Ops:
  7.2 1.7 constant_dynamic-slice_fusion
  9.0 3.3 collective-permute-start.10
  12.3 45.6 %collective-permute-done.10 = bf16[512,2048]{1,0:T(8,128)(2,1)S(1)} collective-permute-done((bf16[512,2048]{1,0:T(8,128)(2,1)S(1)}, bf16[512,2048]{1,0:T(8,128)(2,1)S(1)}, u32[]{:S(2)}, u32[]{:S(2)}) %collective-permute-start.10) | collective-permute-done | bytes 2097184 | tf_op jit(solution)/shard_map/ppermute | solution.py:155
  59.3 30.3 %weight_grad.4 = (f32[512,5120]{1,0:T(8,128)}, f32[512,128]{1,0:T(8,128)}, f32[1,5120]{1,0:T(1,128)}) custom-call(bf16[4096,512]{1,0:T(8,128)(2,1)} %x_ref.4, bf16[4096,5120]{1,0:T(8,128)(2,1)} %dyu_ref.3), custom_call_target="tpu_custom_call" | custom-call | flops 21474836480 | bytes 56623104 | tf_op jit(solution)/shard_map/weight_grad/pallas_call | solution.py:72
  90.7 30.3 %weight_grad.3 = (f32[512,5120]{1,0:T(8,128)}, f32[512,128]{1,0:T(8,128)}, f32[1,5120]{1,0:T(1,128)}) custom-call(bf16[4096,512]{1,0:T(8,128)(2,1)} %x_ref.4, bf16[4096,5120]{1,0:T(8,128)(2,1)} %dyg_ref.3), custom_call_target="tpu_custom_call" | custom-call | flops 21474836480 | bytes 56623104 | tf_op jit(solution)/shard_map/weight_grad/pallas_call | solution.py:72
  122.2 32.8 %weight_grad.5 = (f32[1280,2048]{1,0:T(8,128)}, f32[1280,128]{1,0:T(8,128)}, f32[1,2048]{1,0:T(1,128)}) custom-call(bf16[4096,1280]{1,0:T(8,128)(2,1)} %x_ref.5, bf16[4096,2048]{1,0:T(8,128)(2,1)} %dya_ref.3), custom_call_target="tpu_custom_call" | custom-call | flops 21474836480 | bytes 37748736 | tf_op jit(solution)/shard_map/weight_grad/pallas_call | solution.py:72
  156.3 1.8 collective-permute-start
  162.5 1.9 select_maximum_fusion
  167.1 1.7 collective-permute-start.2
  168.8 2.5 collective-permute-done.2
  171.3 1.7 collective-permute-start.3
  173.0 9.6 %cast_weight.5 = (bf16[1280,2048]{1,0:T(8,128)(2,1)}, f32[8,2048]{1,0:T(8,128)}) custom-call(f32[1280,2048]{1,0:T(8,128)} %w_ref.5), custom_call_target="tpu_custom_call" | custom-call | flops 7864320 | bytes 15728640 | tf_op jit(solution)/shard_map/cast_weight/pallas_call | solution.py:38
  182.6 3.2 slice.96.wa_ref
  187.3 2.1 slice.95.wa_ref
  191.0 6.8 %cast_weight.3 = (bf16[512,5120]{1,0:T(8,128)(2,1)}, f32[8,5120]{1,0:T(8,128)}) custom-call(f32[512,5120]{1,0:T(8,128)} %w_ref.3), custom_call_target="tpu_custom_call" | custom-call | flops 7864320 | bytes 15728640 | tf_op jit(solution)/shard_map/cast_weight/pallas_call | solution.py:38
  199.4 7.0 %cast_weight.4 = (bf16[512,5120]{1,0:T(8,128)(2,1)}, f32[8,5120]{1,0:T(8,128)}) custom-call(f32[512,5120]{1,0:T(8,128)} %w_ref.4), custom_call_target="tpu_custom_call" | custom-call | flops 7864320 | bytes 15728640 | tf_op jit(solution)/shard_map/cast_weight/pallas_call | solution.py:38
  211.9 7.5 %multiply_reduce_fusion.2 = f32[]{:T(128)} fusion(f32[512,5120]{1,0:T(8,128)} %get-tuple-element.50, f32[]{:T(128)} %bitcast.7, f32[5120]{0:T(1024)S(1)} %get-tuple-element.75, f32[512]{0:T(512)S(1)} %get-tuple-element.66), kind=kLoop, calls=%fused_computation.8 | loop fusion | flops 13107199 | bytes 10508296 | tf_op jit(solution)/shard_map/reduce_sum | solution.py:222
  219.4 7.5 %multiply_reduce_fusion.1 = f32[]{:T(128)} fusion(f32[512,5120]{1,0:T(8,128)} %get-tuple-element.57, f32[]{:T(128)} %bitcast.9, f32[5120]{0:T(1024)S(1)} %get-tuple-element.74, f32[512]{0:T(512)S(1)} %get-tuple-element.77), kind=kLoop, calls=%fused_computation.6 | loop fusion | flops 13107199 | bytes 10508296 | tf_op jit(solution)/shard_map/reduce_sum | solution.py:222
  226.9 4.0 multiply_reduce_fusion
  230.9 3.9 stack.43
  237.5 30.6 %norm_partial.3 = f32[2048,512]{1,0:T(8,128)} custom-call(s32[1]{0:T(128)} %bitcast.23.off_ref, bf16[4096,5120]{1,0:T(8,128)(2,1)} %dyg_ref.3, bf16[4096,5120]{1,0:T(8,128)(2,1)} %dyu_ref.3, bf16[512,5120]{1,0:T(8,128)(2,1)} %get-tuple-element.62.wg_ref, bf16[512,5120]{1,0:T(8,128)(2,1)} %get-tuple-element.63.wu_ref), custom_call_target="tpu_custom_call" | custom-call | flops 21474836480 | bytes 56623104 | tf_op jit(solution)/shard_map/norm_partial/pallas_call | solution.py:107
  269.8 3.1 collective-permute-done.6
  273.6 30.7 %norm_partial.2 = f32[2048,512]{1,0:T(8,128)} custom-call(s32[1]{0:T(128)} %bitcast.22.off_ref, bf16[4096,5120]{1,0:T(8,128)(2,1)} %dyg_ref.3, bf16[4096,5120]{1,0:T(8,128)(2,1)} %dyu_ref.3, bf16[512,5120]{1,0:T(8,128)(2,1)} %get-tuple-element.62.wg_ref, bf16[512,5120]{1,0:T(8,128)(2,1)} %get-tuple-element.63.wu_ref), custom_call_target="tpu_custom_call" | custom-call | flops 21474836480 | bytes 56623104 | tf_op jit(solution)/shard_map/norm_partial/pallas_call | solution.py:107
  304.4 84.9 %collective-permute-done.7 = f32[128]{0:T(128)S(1)} collective-permute-done((f32[128]{0:T(128)S(1)}, f32[128]{0:T(128)S(1)}, u32[]{:S(2)}, u32[]{:S(2)}) %collective-permute-start.7) | collective-permute-done | bytes 544 | tf_op jit(solution)/shard_map/ppermute | solution.py:155
  398.2 21.5 %multiply_subtract_fusion.1 = (f32[512,5120]{1,0:T(8,128)}, f32[512,5120]{1,0:T(8,128)}) fusion(f32[512,5120]{1,0:T(8,128)} %w_ref.4, f32[]{:T(128)} %bitcast.19, f32[]{:T(128)} %bitcast.18, f32[512,5120]{1,0:T(8,128)} %get-tuple-element.57, f32[]{:T(128)} %bitcast.9, f32[5120]{0:T(1024)S(1)} %get-tuple-element.74, f32[512]{0:T(512)S(1)} %get-tuple-element.77, ...), kind=kLoop, calls=%fused_computation.2 | loop fusion | flops 31457280 | bytes 62959640 | tf_op jit(solution)/shard_map/sub | solution.py:231
  419.7 3.0 add_convert_fusion
  424.4 13.1 %multiply_subtract_fusion = f32[1280,2048]{1,0:T(8,128)} fusion(f32[1280,2048]{1,0:T(8,128)} %w_ref.5, f32[]{:T(128)} %bitcast.21, f32[]{:T(128)} %bitcast.20, f32[1280,2048]{1,0:T(8,128)} %get-tuple-element.58, f32[]{:T(128)} %bitcast.11, f32[2048]{0:T(1024)S(1)} %fusion.2, f32[1280]{0:T(1024)S(1)} %get-tuple-element.70), kind=kLoop, calls=%fused_computation.1 | loop fusion | flops 15728640 | bytes 31470604 | tf_op jit(solution)/shard_map/sub | solution.py:231
  437.5 30.8 %collective-permute-done.9 = bf16[2048,512]{1,0:T(8,128)(2,1)S(1)} collective-permute-done((bf16[2048,512]{1,0:T(8,128)(2,1)S(1)}, bf16[2048,512]{1,0:T(8,128)(2,1)S(1)}, u32[]{:S(2)}, u32[]{:S(2)}) %collective-permute-start.9) | collective-permute-done | bytes 2097184 | tf_op jit(solution)/shard_map/ppermute | solution.py:155
  468.3 2.6 maximum_select_fusion
  470.9 31.6 %act_grad.3 = bf16[4096,512]{1,0:T(8,128)(2,1)} custom-call(bf16[4096,2048]{1,0:T(8,128)(2,1)} %dya_ref.3, bf16[4096,2048]{1,0:T(8,128)(2,1)} %all-gather.2.cloned.1.call-done.dyb_ref, bf16[512,2048]{1,0:T(8,128)(2,1)} %slice.96.wa_ref, bf16[512,2048]{1,0:T(8,128)(2,1)} %collective-permute-done.12.wb_ref), custom_call_target="tpu_custom_call" | custom-call | flops 17179869184 | bytes 41943040 | tf_op jit(solution)/shard_map/act_grad/pallas_call | solution.py:141
  502.5 37.5 %act_grad.2 = bf16[4096,768]{1,0:T(8,128)(2,1)} custom-call(bf16[4096,2048]{1,0:T(8,128)(2,1)} %dya_ref.3, bf16[4096,2048]{1,0:T(8,128)(2,1)} %all-gather.2.cloned.1.call-done.dyb_ref, bf16[768,2048]{1,0:T(8,128)(2,1)} %copy-done.1, bf16[768,2048]{1,0:T(8,128)(2,1)} %collective-permute-done.11.wb_ref), custom_call_target="tpu_custom_call" | custom-call | flops 25769803776 | bytes 46137344 | tf_op jit(solution)/shard_map/act_grad/pallas_call | solution.py:141
  540.0 9.7 %pad_maximum_fusion = bf16[4096,1280]{1,0:T(8,128)(2,1)} fusion(bf16[4096,512]{1,0:T(8,128)(2,1)} %act_grad.3, bf16[4096,768]{1,0:T(8,128)(2,1)} %act_grad.2), kind=kLoop, calls=%fused_computation | loop fusion | flops 20971520 | bytes 20971520 | tf_op jit(solution)/shard_map/concatenate | solution.py:233
  (89 shorter events, 27.1 us)
Async XLA Ops:
  7.2 463.8 %all-gather.2.cloned.1.call-start = ((), (), s32[]{:S(2)}) async-start(), calls=%async_computation | async-start | bytes 18874368 | tf_op jit(solution)/shard_map/all_gather | solution.py:184
  9.0 49.0 %collective-permute-start.10 = (bf16[512,2048]{1,0:T(8,128)(2,1)S(1)}, bf16[512,2048]{1,0:T(8,128)(2,1)S(1)}, u32[]{:S(2)}, u32[]{:S(2)}) collective-permute-start(bf16[512,2048]{1,0:T(8,128)(2,1)S(1)} %constant_dynamic-slice_fusion), channel_id=1, source_target_pairs={{0,8},{8,0},{1,9},{9,1},{2,10},{10,2},{3,11},{11,3},{4,12},{12,4},... | collective-permute-start | bytes 6291464 | tf_op jit(solution)/shard_map/ppermute | solution.py:155
  122.1 36.0 %copy-start.16 = (f32[3]{0:T(128)S(1)}, f32[3]{0:T(128)}, u32[]{:S(2)}) copy-start(f32[3]{0:T(128)} %param.33) | copy-start | bytes 40
  122.1 37.9 %copy-start.17 = (f32[512]{0:T(512)S(1)}, f32[512]{0:T(512)}, u32[]{:S(2)}) copy-start(f32[512]{0:T(512)} %param.27) | copy-start | bytes 6148
  122.1 37.9 %copy-start.18 = (f32[512]{0:T(512)S(1)}, f32[512]{0:T(512)}, u32[]{:S(2)}) copy-start(f32[512]{0:T(512)} %param.29) | copy-start | bytes 6148
  122.2 39.1 %copy-start.14 = (f32[1280]{0:T(1024)S(1)}, f32[1280]{0:T(1024)}, u32[]{:S(2)}) copy-start(f32[1280]{0:T(1024)} %param.31) | copy-start | bytes 15364
  122.2 42.3 %copy-start.5 = (f32[1,5120]{1,0:T(1,128)S(1)}, f32[1,5120]{1,0:T(1,128)}, u32[]{:S(2)}) copy-start(f32[1,5120]{1,0:T(1,128)} %get-tuple-element.55) | copy-start | bytes 61444
  122.2 42.3 %copy-start.6 = (f32[1,5120]{1,0:T(1,128)S(1)}, f32[1,5120]{1,0:T(1,128)}, u32[]{:S(2)}) copy-start(f32[1,5120]{1,0:T(1,128)} %get-tuple-element.54) | copy-start | bytes 61444
  156.3 3.7 collective-permute-start
  161.3 236.8 %copy-start.12 = (f32[512]{0:T(512)}, f32[512]{0:T(512)S(1)}, u32[]{:S(2)}) copy-start(f32[512]{0:T(512)S(1)} %get-tuple-element.66) | copy-start | bytes 6148
  161.3 236.8 %copy-start.13 = (f32[512]{0:T(512)}, f32[512]{0:T(512)S(1)}, u32[]{:S(2)}) copy-start(f32[512]{0:T(512)S(1)} %get-tuple-element.77) | copy-start | bytes 6148
  162.5 261.8 %copy-start.7 = (f32[1280]{0:T(1024)}, f32[1280]{0:T(1024)S(1)}, u32[]{:S(2)}) copy-start(f32[1280]{0:T(1024)S(1)} %get-tuple-element.70) | copy-start | bytes 15364
  165.2 1.2 collective-permute-start.1
  167.1 4.1 collective-permute-start.2
  171.3 36.7 %collective-permute-start.3 = (f32[12416]{0:T(1024)S(1)}, f32[12416]{0:T(1024)S(1)}, u32[]{:S(2)}, u32[]{:S(2)}) collective-permute-start(f32[12416]{0:T(1024)S(1)} %add.64), channel_id=1, source_target_pairs={{0,4},{1,5},{2,6},{3,7},{4,0},{5,1},{6,2},{7,3},{8,12},{9,13},{10,... | collective-permute-start | bytes 149000 | tf_op jit(solution)/shard_map/ppermute | solution.py:161
  185.7 285.2 %collective-permute-start.12 = (bf16[512,2048]{1,0:T(8,128)(2,1)}, bf16[512,2048]{1,0:T(8,128)(2,1)}, u32[]{:S(2)}, u32[]{:S(2)}) collective-permute-start(bf16[512,2048]{1,0:T(8,128)(2,1)} %slice.96.wa_ref), channel_id=1, source_target_pairs={{0,8},{8,0},{1,9},{9,1},{2,10},{10,2},{3,11},{11,3},{4,12},{12,4},... | collective-permute-start | bytes 6291464 | tf_op jit(solution)/shard_map/ppermute | solution.py:155
  189.4 16.9 %copy-start.1 = (bf16[768,2048]{1,0:T(8,128)(2,1)}, bf16[768,2048]{1,0:T(8,128)(2,1)S(1)}, u32[]{:S(2)}) copy-start(bf16[768,2048]{1,0:T(8,128)(2,1)S(1)} %slice.95.wa_ref) | copy-start | bytes 9437188
  189.4 313.1 %collective-permute-start.11 = (bf16[768,2048]{1,0:T(8,128)(2,1)S(1)}, bf16[768,2048]{1,0:T(8,128)(2,1)}, u32[]{:S(2)}, u32[]{:S(2)}) collective-permute-start(bf16[768,2048]{1,0:T(8,128)(2,1)S(1)} %slice.95.wa_ref), channel_id=1, source_target_pairs={{0,8},{8,0},{1,9},{9,1},{2,10},{10,2},{3,11},{11,3},{4,12},{12,4},... | collective-permute-start | bytes 9437192 | tf_op jit(solution)/shard_map/ppermute | solution.py:155
  191.0 19.5 %copy-start.15 = (f32[2048]{0:T(1024)S(1)}, f32[2048]{0:T(1024)}, u32[]{:S(2)}) copy-start(f32[2048]{0:T(1024)} %param.32) | copy-start | bytes 24580
  191.0 20.2 %copy-start.10 = (f32[5120]{0:T(1024)S(1)}, f32[5120]{0:T(1024)}, u32[]{:S(2)}) copy-start(f32[5120]{0:T(1024)} %param.30) | copy-start | bytes 61444
  191.0 20.2 %copy-start.11 = (f32[5120]{0:T(1024)S(1)}, f32[5120]{0:T(1024)}, u32[]{:S(2)}) copy-start(f32[5120]{0:T(1024)} %param.28) | copy-start | bytes 61444
  211.2 213.2 %copy-start.8 = (f32[2048]{0:T(1024)}, f32[2048]{0:T(1024)S(1)}, u32[]{:S(2)}) copy-start(f32[2048]{0:T(1024)S(1)} %fusion.2) | copy-start | bytes 24580
  211.8 186.3 %copy-start.3 = (f32[5120]{0:T(1024)}, f32[5120]{0:T(1024)S(1)}, u32[]{:S(2)}) copy-start(f32[5120]{0:T(1024)S(1)} %get-tuple-element.74) | copy-start | bytes 61444
  211.8 186.3 %copy-start.4 = (f32[5120]{0:T(1024)}, f32[5120]{0:T(1024)S(1)}, u32[]{:S(2)}) copy-start(f32[5120]{0:T(1024)S(1)} %get-tuple-element.75) | copy-start | bytes 61444
  211.9 15.1 %slice-start = ((s8[10485760]{0:T(1024)(128)(4,1)}), s8[4194304]{0:T(1024)(128)(4,1)S(1)}, s32[]{:S(2)}) async-start(s8[10485760]{0:T(1024)(128)(4,1)} %bitcast.24), calls=%async_computation.1 | async-start | bytes 8388608
  234.8 1.2 collective-permute-start.4
  236.0 33.3 %collective-permute-start.5 = (f32[128]{0:T(128)S(1)}, f32[128]{0:T(128)S(1)}, u32[]{:S(2)}, u32[]{:S(2)}) collective-permute-start(f32[128]{0:T(128)S(1)} %constant_dynamic-update-slice_fusion), channel_id=1, source_target_pairs={{0,2},{1,3},{2,0},{3,1},{4,6},{5,7},{6,4},{7,5},{8,10},{9,11},{10,... | collective-permute-start | bytes 1544 | tf_op jit(solution)/shard_map/ppermute | solution.py:161
  268.0 151.7 %collective-permute-start.8 = (f32[2048,512]{1,0:T(8,128)}, f32[2048,512]{1,0:T(8,128)}, u32[]{:S(2)}, u32[]{:S(2)}) collective-permute-start(f32[2048,512]{1,0:T(8,128)} %norm_partial.3), channel_id=1, source_target_pairs={{0,8},{8,0},{1,9},{9,1},{2,10},{10,2},{3,11},{11,3},{4,12},{12,4},... | collective-permute-start | bytes 12582920 | tf_op jit(solution)/shard_map/ppermute | solution.py:155
  269.3 3.6 collective-permute-start.6
  272.9 116.4 %collective-permute-start.7 = (f32[128]{0:T(128)S(1)}, f32[128]{0:T(128)S(1)}, u32[]{:S(2)}, u32[]{:S(2)}) collective-permute-start(f32[128]{0:T(128)S(1)} %add.71), channel_id=1, source_target_pairs={{0,8},{8,0},{1,9},{9,1},{2,10},{10,2},{3,11},{11,3},{4,12},{12,4},... | collective-permute-start | bytes 1544 | tf_op jit(solution)/shard_map/ppermute | solution.py:155
  398.2 21.6 %copy-start = (f32[2048,512]{1,0:T(8,128)S(1)}, f32[2048,512]{1,0:T(8,128)}, u32[]{:S(2)}) copy-start(f32[2048,512]{1,0:T(8,128)} %norm_partial.2) | copy-start | bytes 12582916
  422.7 45.6 %collective-permute-start.9 = (bf16[2048,512]{1,0:T(8,128)(2,1)S(1)}, bf16[2048,512]{1,0:T(8,128)(2,1)S(1)}, u32[]{:S(2)}, u32[]{:S(2)}) collective-permute-start(bf16[2048,512]{1,0:T(8,128)(2,1)S(1)} %add_convert_fusion), channel_id=1, source_target_pairs={{0,8},{8,0},{1,9},{9,1},{2,10},{10,2},{3,11},{11,3},{4,12},{12,4},... | collective-permute-start | bytes 6291464 | tf_op jit(solution)/shard_map/ppermute | solution.py:155
  (4 other events, 31.3 us)
Sparse Core Ops, SparseCore 0:
  59.4 87.1 all-gather.1

commit v2 on v1

v2 whole, which is shorter than its diff:
```python
import functools

import jax
import jax.numpy as jnp
from jax import lax
from jax.experimental import pallas as pl
from jax.experimental.pallas import tpu as pltpu
from jax.sharding import PartitionSpec as P

EPS_ONE = 1e-30
EPS_TWO = 1e-3
F32 = jnp.float32
BF16 = jnp.bfloat16
VMEM_LIMIT = 60 * 1024 * 1024
NT = (((1,), (1,)), ((), ()))


def params(*semantics):
    return pltpu.CompilerParams(dimension_semantics=semantics, vmem_limit_bytes=VMEM_LIMIT)


def cost(flops, nbytes):
    return pl.CostEstimate(flops=int(flops), bytes_accessed=int(nbytes), transcendentals=0)


def fold_squares(v):
    return jnp.sum((v * v).reshape(v.shape[0] // 8, 8, v.shape[1]), axis=0)


def cast_kernel(first, w_ref, a_ref, b_ref, s_ref):
    step = pl.program_id(0)
    w = w_ref[...]

    @pl.when(step < first)
    def _():
        a_ref[...] = w.astype(BF16)

    @pl.when(step >= first)
    def _():
        b_ref[...] = w.astype(BF16)

    @pl.when(step == 0)
    def _():
        s_ref[...] = jnp.zeros_like(s_ref)

    s_ref[...] += fold_squares(w)


def cast_weight(w, cut):
    rows, cols = w.shape
    tile = 256
    first = cut // tile
    a, b, s = pl.pallas_call(
        functools.partial(cast_kernel, first),
        grid=(rows // tile,),
        in_specs=[pl.BlockSpec((tile, cols), lambda i: (i, 0))],
        out_specs=[
            pl.BlockSpec((tile, cols), lambda i: (jnp.minimum(i, first - 1), 0)),
            pl.BlockSpec((tile, cols), lambda i: (jnp.maximum(i - first, 0), 0)),
            pl.BlockSpec((8, cols), lambda i: (0, 0)),
        ],
        out_shape=[
            jax.ShapeDtypeStruct((cut, cols), BF16),
            jax.ShapeDtypeStruct((rows - cut, cols), BF16),
            jax.ShapeDtypeStruct((8, cols), F32),
        ],
        compiler_params=params('arbitrary'),
        cost_estimate=cost(w.size * 1000, w.size * 6),
        name='cast_weight',
    )(w)
    return a, b, jnp.sum(s)


def grad_block(xt_ref, dy_ref, g_ref, row_ref, col_ref):
    g = jnp.dot(xt_ref[...], dy_ref[...], preferred_element_type=F32)
    g_ref[...] = g
    q = g * g + EPS_ONE
    col_ref[...] = jnp.sum(q, axis=0, keepdims=True)
    part = q[:, :128]
    for k in range(1, q.shape[1] // 128):
        part += q[:, k * 128:(k + 1) * 128]
    row_ref[...] += part


def grad_kernel(count, steps, x_ref, *refs):
    dy, out, xt_ref = refs[:count], refs[count:-1], refs[-1]
    step = pl.program_id(0)

    @pl.when(step == 0)
    def _():
        for k in range(count):
            out[3 * k + 1][...] = jnp.zeros_like(out[3 * k + 1])
        xt_ref[...] = x_ref[...].T

    for k in range(count):
        @pl.when((step >= k * steps) & (step < (k + 1) * steps))
        def _():
            grad_block(xt_ref, dy[k], *out[3 * k:3 * k + 3])


def weight_grads(x, dys, tile):
    tokens, m = x.shape
    n = dys[0].shape[1]
    steps = n // tile
    count = len(dys)

    def block(k):
        return lambda j: (0, jnp.clip(j - k * steps, 0, steps - 1))

    out_specs, out_shape = [], []
    for k in range(count):
        out_specs += [
            pl.BlockSpec((m, tile), block(k)),
            pl.BlockSpec((m, 128), lambda j: (0, 0)),
            pl.BlockSpec((1, tile), block(k)),
        ]
        out_shape += [
            jax.ShapeDtypeStruct((m, n), F32),
            jax.ShapeDtypeStruct((m, 128), F32),
            jax.ShapeDtypeStruct((1, n), F32),
        ]
    out = pl.pallas_call(
        functools.partial(grad_kernel, count, steps),
        grid=(steps * count,),
        in_specs=[pl.BlockSpec((tokens, m), lambda j: (0, 0), pipeline_mode=pl.Buffered(1))]
        + [pl.BlockSpec((tokens, tile), block(k)) for k in range(count)],
        out_specs=out_specs,
        out_shape=out_shape,
        scratch_shapes=[pltpu.VMEM((m, tokens), BF16)],
        compiler_params=params('arbitrary'),
        cost_estimate=cost(2 * count * tokens * m * n, count * (2 * tokens * (m + n) + 4 * m * n)),
        name='weight_grads',
    )(x, *dys)
    return [(out[3 * k], jnp.sum(out[3 * k + 1], axis=1), out[3 * k + 2][0]) for k in range(count)]


def norm_kernel(steps, squares, off_ref, dyg_ref, dyu_ref, wg_ref, wu_ref, *out):
    step = pl.program_id(0)

    def add(dy_ref, w_ref, k):
        w = w_ref[...]
        b = w.astype(BF16)
        half = dy_ref.shape[0] // 2
        for i in range(2):
            part = lax.dot_general(dy_ref[i * half:(i + 1) * half, :], b, NT, preferred_element_type=F32)
            out[i][...] += part
        if squares:
            out[2 + k][...] += fold_squares(w)

    @pl.when(step == 0)
    def _():
        for ref in out:
            ref[...] = jnp.zeros_like(ref)

    @pl.when(step < steps)
    def _():
        add(dyg_ref, wg_ref, 0)

    @pl.when(step >= steps)
    def _():
        add(dyu_ref, wu_ref, 1)


def norm_partial(offset, tokens, dyg, dyu, wg, wu, squares):
    tile = 1024
    m, n = wg.shape
    steps = n // tile

    def block(row, k):
        return lambda j, off: (off[0] if row else 0, jnp.clip(j - k * steps, 0, steps - 1))

    out_specs = [pl.BlockSpec((tokens // 2, m), lambda j, off: (0, 0))] * 2
    out_shape = [jax.ShapeDtypeStruct((tokens // 2, m), F32)] * 2
    if squares:
        out_specs += [pl.BlockSpec((8, tile), lambda j, off: (0, 0))] * 2
        out_shape += [jax.ShapeDtypeStruct((8, tile), F32)] * 2
    out = pl.pallas_call(
        functools.partial(norm_kernel, steps, squares),
        grid_spec=pltpu.PrefetchScalarGridSpec(
            num_scalar_prefetch=1,
            grid=(2 * steps,),
            in_specs=[
                pl.BlockSpec((tokens, tile), block(True, 0)),
                pl.BlockSpec((tokens, tile), block(True, 1)),
                pl.BlockSpec((m, tile), block(False, 0)),
                pl.BlockSpec((m, tile), block(False, 1)),
            ],
            out_specs=out_specs,
        ),
        out_shape=out_shape,
        compiler_params=params('arbitrary'),
        cost_estimate=cost(4 * tokens * m * n, 4 * tokens * n + 8 * m * n + 4 * tokens * m),
        name='norm_partial',
    )((offset // tokens).astype(jnp.int32).reshape(1), dyg, dyu, wg, wu)
    return [*out[:2], *[jnp.sum(s) for s in out[2:]]]


def act_kernel(block, parts, dya_ref, dyb_ref, *refs):
    out_ref, acc_ref = refs[-2:]
    done = 0
    for wa_ref, wb_ref in zip(refs[:parts], refs[parts:2 * parts]):
        count = wa_ref.shape[0] // block

        @pl.loop(0, count)
        def _(k):
            rows = pl.ds(pl.multiple_of(k * block, block), block)
            acc_ref[k] = lax.dot_general(dya_ref[...], wa_ref[rows, :], NT, preferred_element_type=F32)

        @pl.loop(0, count)
        def _(k):
            rows = pl.ds(pl.multiple_of(k * block, block), block)
            cols = pl.ds(pl.multiple_of(done + k * block, block), block)
            other = lax.dot_general(dyb_ref[...], wb_ref[rows, :], NT, preferred_element_type=F32)
            out_ref[:, cols] = (acc_ref[k] + other).astype(BF16)

        done += wa_ref.shape[0]


def act_grad(dya, dyb, wa, wb):
    tile, block = 512, 256
    tokens, n = dya.shape
    m = sum(w.shape[0] for w in wa)
    dy_spec = pl.BlockSpec((tile, n), lambda i: (i, 0))
    w_specs = [pl.BlockSpec(w.shape, lambda i: (0, 0), pipeline_mode=pl.Buffered(1)) for w in (*wa, *wb)]
    return pl.pallas_call(
        functools.partial(act_kernel, block, len(wa)),
        grid=(tokens // tile,),
        in_specs=[dy_spec, dy_spec, *w_specs],
        out_specs=pl.BlockSpec((tile, m), lambda i: (i, 0)),
        out_shape=jax.ShapeDtypeStruct((tokens, m), BF16),
        scratch_shapes=[pltpu.VMEM((max(w.shape[0] for w in wa) // block, tile, block), F32)],
        compiler_params=params('arbitrary'),
        cost_estimate=cost(4 * tokens * m * n, 4 * tokens * n + 4 * m * n + 2 * tokens * m),
        name='act_grad',
    )(dya, dyb, *wa, *wb)


def swap_col(v):
    return lax.ppermute(v, 'col', [(0, 1), (1, 0)])


def sum_row(v, row_size):
    step = 1
    while step < row_size:
        v = v + lax.ppermute(v, 'row', [(i, i ^ step) for i in range(row_size)])
        step *= 2
    return v


def solution(mesh):
    row_size = mesh.shape['row']
    col_size = mesh.shape['col']
    weight_spec = P('row', 'col')
    act_spec = P(None, 'row')
    grad_spec = P(None, 'col')
    in_specs = (weight_spec,) * 3 + (act_spec, act_spec) + (grad_spec,) * 3 + (P('row'), P('col')) * 3 + (P(),)
    out_specs = (weight_spec,) * 3 + (P('row'), P('col')) * 3 + (act_spec, act_spec)

    def body(w_gate, w_up, w_down, x_norm, x_act, dy_gate, dy_up, dy_down, r_gate, c_gate, r_up, c_up, r_down, c_down, hyper_params):
        row = lax.axis_index('row')
        col = lax.axis_index('col')
        tokens = x_norm.shape[0]
        half = tokens // col_size
        beta_two = hyper_params[0]

        share = tokens // row_size
        piece = lax.dynamic_slice_in_dim(dy_down, row * share, share, axis=0)
        piece = swap_col(piece)
        dy_down_other = lax.all_gather(piece, 'row', axis=0, tiled=True)
        b_down_a, b_down_b, w_sq_down = cast_weight(w_down, 768)
        o_down_a = swap_col(b_down_a)

        (g_gate, row_gate, col_gate), (g_up, row_up, col_up) = weight_grads(x_norm, [dy_gate, dy_up], 512)
        ((g_down, row_down, col_down),) = weight_grads(x_act, [dy_down], 256)
        row_all = jnp.concatenate([row_gate, row_up, row_down])
        row_peer = swap_col(row_all)
        o_down_b = swap_col(b_down_b)
        sent = norm_partial((1 - col) * half, half, dy_gate, dy_up, w_gate, w_up, False)
        got0 = swap_col(sent[0])
        own0, own1, w_sq_gate, w_sq_up = norm_partial(col * half, half, dy_gate, dy_up, w_gate, w_up, True)

        sizes_r = [r_gate.shape[0], r_up.shape[0], r_down.shape[0]]
        sizes_c = [c_gate.shape[0], c_up.shape[0], c_down.shape[0]]
        totals = [(sizes_r[k] * row_size, sizes_c[k] * col_size) for k in range(3)]
        row_all = row_all + row_peer
        row_sums = jnp.split(row_all, [sizes_r[0], sizes_r[0] + sizes_r[1]])
        r_old = [r_gate, r_up, r_down]
        c_old = [c_gate, c_up, c_down]
        r_new = [beta_two * r_old[k] + (1.0 - beta_two) * (row_sums[k] / totals[k][1]) for k in range(3)]
        r_part = jnp.zeros((128,), F32).at[:3].set(jnp.stack([jnp.sum(r) for r in r_new]))
        col_all = sum_row(jnp.concatenate([col_gate, col_up, col_down, r_part]), row_size)
        offs = [0, sizes_c[0], sizes_c[0] + sizes_c[1], sum(sizes_c)]
        c_new = [
            beta_two * c_old[k] + (1.0 - beta_two) * (col_all[offs[k]:offs[k + 1]] / totals[k][0]) for k in range(3)
        ]
        r_mean = [col_all[offs[3] + k] / totals[k][0] for k in range(3)]
        grads = [g_gate, g_up, g_down]
        updates = [grads[k] * lax.rsqrt(r_new[k][:, None] * c_new[k][None, :] / r_mean[k]) for k in range(3)]
        scalars = jnp.stack([jnp.sum(u * u) for u in updates] + [w_sq_gate, w_sq_up, w_sq_down])
        scalars = sum_row(jnp.zeros((128,), F32).at[:6].set(scalars), row_size)
        scalars_peer = swap_col(scalars)
        got1 = swap_col(sent[1])
        dx_act = act_grad(dy_down, dy_down_other, [b_down_a, b_down_b], [o_down_a, o_down_b])
        scalars = scalars + scalars_peer
        weights = [w_gate, w_up, w_down]
        new = []
        for k in range(3):
            size = totals[k][0] * totals[k][1]
            rms_u = jnp.sqrt(scalars[k] / size)
            step_size = hyper_params[1] * jnp.maximum(EPS_TWO, jnp.sqrt(scalars[3 + k] / size))
            new.append(weights[k] - step_size * (updates[k] / jnp.maximum(1.0, rms_u / hyper_params[2])))

        mine0 = (own0 + got0).astype(BF16)
        theirs0 = swap_col(mine0)
        mine1 = (own1 + got1).astype(BF16)
        theirs1 = swap_col(mine1)
        dx_norm = jnp.where(
            col == 0,
            jnp.concatenate([mine0, mine1, theirs0, theirs1]),
            jnp.concatenate([theirs0, theirs1, mine0, mine1]),
        )
        return (*new, r_new[0], c_new[0], r_new[1], c_new[1], r_new[2], c_new[2], dx_norm, dx_act)

    return jax.shard_map(body, mesh=mesh, in_specs=in_specs, out_specs=out_specs, check_vma=False)
```

time: 567 us -> 607 us (1.071); the launches traced: 557 us -> 606 us
  waiting for transfers between devices: 170 us -> 253 us
  other arithmetic: 83.9 us -> 68.4 us
  Pallas kernels: 247 us -> 232 us
    ppermute x7 -> x9, waiting for transfers between devices: 162 us -> 245 us  [swap_col(): return lax.ppermute(v, 'col', [(0, 1), (1, 0)])]
    pallas_call x10 -> x6, Pallas kernels: 247 us -> 232 us  [the longest x2 91.4 us: weight_grads(): pl.pallas_call(functools.partial(grad_kernel, count, steps), grid=(steps...]
    concatenate x1 -> x0, other arithmetic: 9.67 us -> none  [body(): jnp.concatenate([act_grad(dy_down, dy_down_other, b_down[:cut], b_down_ot...]
    sub x2, other arithmetic: 34.7 us -> 28.1 us  [body(): weights[k]]
  transfers between devices with their start and end apart: 14 -> 16, of which waited for: 8 -> 10; matrix products, arithmetic and copies ran while one was open for 15% -> 12% of each run, Pallas kernels for 38% -> 27%
where the time goes in v2:
time: 607 us; the launch traced here: 606 us
  waiting for transfers between devices  253 us (42%)
  Pallas kernels  232 us (38%)
  other arithmetic  68.4 us (11%)
  between operations  27.7 us (5%)
  starting transfers between devices  15.7 us (3%)
  local copies, waits for them, and re-layouts  8.97 us (1%)
    ppermute x9, waiting for transfers between devices, swap_col(): return lax.ppermute(v, 'col', [(0, 1), (1, 0)])  245 us
    pallas_call x2, Pallas kernels, weight_grads(): pl.pallas_call(functools.partial(grad_kernel, count, steps), grid=(steps...  91.4 us
    pallas_call x1, Pallas kernels, act_grad(): pl.pallas_call(functools.partial(act_kernel, block, len(wa)), grid=(token...  66.3 us
    pallas_call x2, Pallas kernels, norm_partial(): pl.pallas_call(functools.partial(norm_kernel, steps, squares), grid_spec=...  66 us
    sub x2, other arithmetic, body(): weights[k]  28.1 us
    reduce_sum x3, other arithmetic, body(): jnp.sum(u * u)  19.2 us
  transfers between devices with their start and end apart: 16, of which 10 were waited for; matrix products, arithmetic and copies ran while one was open for 12% of the time, Pallas kernels for 27%

profile of v2, /device:TPU:0, one launch (start us, length us, event | category | flops | bytes accessed | tf_op | source)
XLA Modules:
  0.0 605.9 jit_solution(3077513464932787445)
XLA Ops:
  7.2 1.7 constant_dynamic-slice_fusion
  9.0 3.3 collective-permute-start.12
  12.3 45.6 %collective-permute-done.12 = bf16[512,2048]{1,0:T(8,128)(2,1)S(1)} collective-permute-done((bf16[512,2048]{1,0:T(8,128)(2,1)S(1)}, bf16[512,2048]{1,0:T(8,128)(2,1)S(1)}, u32[]{:S(2)}, u32[]{:S(2)}) %collective-permute-start.12) | collective-permute-done | bytes 2097184 | tf_op jit(solution)/shard_map/ppermute | solution.py:239
  59.2 32.9 %weight_grads.3 = (f32[1280,2048]{1,0:T(8,128)}, f32[1280,128]{1,0:T(8,128)}, f32[1,2048]{1,0:T(1,128)}) custom-call(bf16[4096,1280]{1,0:T(8,128)(2,1)} %x_ref.3, bf16[4096,2048]{1,0:T(8,128)(2,1)} %dya_ref.1), custom_call_target="tpu_custom_call" | custom-call | flops 21474836480 | bytes 37748736 | tf_op jit(solution)/shard_map/weight_grads/pallas_call | solution.py:122
  93.5 58.5 %weight_grads.2 = (f32[512,5120]{1,0:T(8,128)}, f32[512,128]{1,0:T(8,128)}, f32[1,5120]{1,0:T(1,128)}, f32[512,5120]{1,0:T(8,128)}, f32[512,128]{1,0:T(8,128)}, /*index=5*/f32[1,5120]{1,0:T(1,128)}) custom-call(bf16[4096,512]{1,0:T(8,128)(2,1)} %x_ref.2, bf16[4096,5120]{1,0:T(8,128)(2,1)} %dyg_ref.3, bf16[4096,5120]{1,0:T(8,128)(2,1)} %dyu_ref.3), custom_call_target="tpu_custom_call" | custom-call | flops 42949672960 | bytes 113246208 | tf_op jit(solution)/shard_map/weight_grads/pallas_call | solution.py:122
  154.2 1.6 collective-permute-start
  160.5 2.0 select_maximum_fusion
  165.3 1.4 collective-permute-start.2
  166.6 33.1 %norm_partial.2 = (f32[1024,512]{1,0:T(8,128)}, f32[1024,512]{1,0:T(8,128)}, f32[8,1024]{1,0:T(8,128)}, f32[8,1024]{1,0:T(8,128)}) custom-call(s32[1]{0:T(128)} %bitcast.13.off_ref, bf16[4096,5120]{1,0:T(8,128)(2,1)} %dyg_ref.3, bf16[4096,5120]{1,0:T(8,128)(2,1)} %dyu_ref.3, f32[512,5120]{1,0:T(8,128)} %wg_ref.3, f32[512,5120]{1,0:T(8,128)} %wu_ref.3), custom_call_target="tpu_custom_call" | custom-call | flops 21474836480 | bytes 67108864 | tf_op jit(solution)/shard_map/norm_partial/pallas_call | solution.py:177
  199.8 1.5 collective-permute-start.3
  201.3 8.2 %cast_weight.1 = (bf16[768,2048]{1,0:T(8,128)(2,1)}, bf16[512,2048]{1,0:T(8,128)(2,1)}, f32[8,2048]{1,0:T(8,128)}) custom-call(f32[1280,2048]{1,0:T(8,128)} %w_ref.1), custom_call_target="tpu_custom_call" | custom-call | flops 2621440000 | bytes 15728640 | tf_op jit(solution)/shard_map/cast_weight/pallas_call | solution.py:53
  210.9 1.5 reduce_sum.119
  216.3 7.5 %multiply_reduce_fusion.2 = f32[]{:T(128)} fusion(f32[512,5120]{1,0:T(8,128)} %get-tuple-element.53, f32[]{:T(128)} %bitcast.7, f32[5120]{0:T(1024)S(1)} %get-tuple-element.81, f32[512]{0:T(512)S(1)} %get-tuple-element.72), kind=kLoop, calls=%fused_computation.7 | loop fusion | flops 13107199 | bytes 10508296 | tf_op jit(solution)/shard_map/reduce_sum | solution.py:299
  223.8 7.5 %multiply_reduce_fusion.1 = f32[]{:T(128)} fusion(f32[512,5120]{1,0:T(8,128)} %get-tuple-element.60, f32[]{:T(128)} %bitcast.9, f32[5120]{0:T(1024)S(1)} %get-tuple-element.80, f32[512]{0:T(512)S(1)} %get-tuple-element.83), kind=kLoop, calls=%fused_computation.5 | loop fusion | flops 13107199 | bytes 10508296 | tf_op jit(solution)/shard_map/reduce_sum | solution.py:299
  231.3 4.2 multiply_reduce_fusion
  235.5 3.9 stack.43
  241.0 3.2 collective-permute-done.5
  244.8 3.0 collective-permute-done.6
  247.8 1.5 collective-permute-start.7
  249.3 32.9 %norm_partial.3 = (f32[1024,512]{1,0:T(8,128)}, f32[1024,512]{1,0:T(8,128)}) custom-call(s32[1]{0:T(128)} %bitcast.23.off_ref, bf16[4096,5120]{1,0:T(8,128)(2,1)} %dyg_ref.3, bf16[4096,5120]{1,0:T(8,128)(2,1)} %dyu_ref.3, f32[512,5120]{1,0:T(8,128)} %wg_ref.3, f32[512,5120]{1,0:T(8,128)} %wu_ref.3), custom_call_target="tpu_custom_call" | custom-call | flops 21474836480 | bytes 67108864 | tf_op jit(solution)/shard_map/norm_partial/pallas_call | solution.py:177
  282.8 1.4 collective-permute-start.9
  284.9 1.4 collective-permute-start.13
  292.4 22.2 %multiply_subtract_fusion.1 = (f32[512,5120]{1,0:T(8,128)}, f32[512,5120]{1,0:T(8,128)}) fusion(f32[512,5120]{1,0:T(8,128)} %wu_ref.3, f32[]{:T(128)} %bitcast.20, f32[]{:T(128)} %bitcast.19, f32[512,5120]{1,0:T(8,128)} %get-tuple-element.60, f32[]{:T(128)} %bitcast.9, f32[5120]{0:T(1024)S(1)} %get-tuple-element.80, f32[512]{0:T(512)S(1)} %get-tuple-element.83, ...), kind=kLoop, calls=%fused_computation.1 | loop fusion | flops 31457280 | bytes 62959640 | tf_op jit(solution)/shard_map/sub | solution.py:311
  319.9 11.1 %collective-permute-done.8 = f32[1024,512]{1,0:T(8,128)} collective-permute-done((f32[1024,512]{1,0:T(8,128)}, f32[1024,512]{1,0:T(8,128)}, u32[]{:S(2)}, u32[]{:S(2)}) %collective-permute-start.8) | collective-permute-done | bytes 2097184 | tf_op jit(solution)/shard_map/ppermute | solution.py:239
  331.1 2.6 add_convert_fusion.1
  334.3 41.7 %collective-permute-done.9 = f32[1024,512]{1,0:T(8,128)} collective-permute-done((f32[1024,512]{1,0:T(8,128)}, f32[1024,512]{1,0:T(8,128)}, u32[]{:S(2)}, u32[]{:S(2)}) %collective-permute-start.9) | collective-permute-done | bytes 2097184 | tf_op jit(solution)/shard_map/ppermute | solution.py:239
  376.0 2.0 add_convert_fusion
  378.7 5.9 multiply_subtract_fusion
  384.6 126.1 %collective-permute-done.10 = bf16[1024,512]{1,0:T(8,128)(2,1)S(1)} collective-permute-done((bf16[1024,512]{1,0:T(8,128)(2,1)S(1)}, bf16[1024,512]{1,0:T(8,128)(2,1)S(1)}, u32[]{:S(2)}, u32[]{:S(2)}) %collective-permute-start.10) | collective-permute-done | bytes 1048608 | tf_op jit(solution)/shard_map/ppermute | solution.py:239
  510.7 19.1 %collective-permute-done.11 = bf16[1024,512]{1,0:T(8,128)(2,1)S(1)} collective-permute-done((bf16[1024,512]{1,0:T(8,128)(2,1)S(1)}, bf16[1024,512]{1,0:T(8,128)(2,1)S(1)}, u32[]{:S(2)}, u32[]{:S(2)}) %collective-permute-start.11) | collective-permute-done | bytes 1048608 | tf_op jit(solution)/shard_map/ppermute | solution.py:239
  529.8 2.8 maximum_select_fusion
  532.7 66.3 %act_grad.1 = bf16[4096,1280]{1,0:T(8,128)(2,1)} custom-call(bf16[4096,2048]{1,0:T(8,128)(2,1)} %dya_ref.1, bf16[4096,2048]{1,0:T(8,128)(2,1)} %all-gather.2.cloned.1.call-done.dyb_ref, bf16[768,2048]{1,0:T(8,128)(2,1)} %get-tuple-element.69.refs_0_, bf16[512,2048]{1,0:T(8,128)(2,1)} %get-tuple-element.70.refs_1_, ...), custom_call_target="tpu_custom_call" | custom-call | flops 42949672960 | bytes 54525952 | tf_op jit(solution)/shard_map/act_grad/pallas_call | solution.py:225
  (99 shorter events, 20.3 us)
Async XLA Ops:
  7.2 525.5 %all-gather.2.cloned.1.call-start = ((), (), s32[]{:S(2)}) async-start(), calls=%async_computation | async-start | bytes 18874368 | tf_op jit(solution)/shard_map/all_gather | solution.py:269
  9.0 48.9 %collective-permute-start.12 = (bf16[512,2048]{1,0:T(8,128)(2,1)S(1)}, bf16[512,2048]{1,0:T(8,128)(2,1)S(1)}, u32[]{:S(2)}, u32[]{:S(2)}) collective-permute-start(bf16[512,2048]{1,0:T(8,128)(2,1)S(1)} %constant_dynamic-slice_fusion), channel_id=1, source_target_pairs={{0,8},{8,0},{1,9},{9,1},{2,10},{10,2},{3,11},{11,3},{4,12},{12,4},... | collective-permute-start | bytes 6291464 | tf_op jit(solution)/shard_map/ppermute | solution.py:239
  93.4 64.6 %copy-start.16 = (f32[512]{0:T(512)S(1)}, f32[512]{0:T(512)}, u32[]{:S(2)}) copy-start(f32[512]{0:T(512)} %param.27) | copy-start | bytes 6148
  93.5 65.8 %copy-start.13 = (f32[1280]{0:T(1024)S(1)}, f32[1280]{0:T(1024)}, u32[]{:S(2)}) copy-start(f32[1280]{0:T(1024)} %param.31) | copy-start | bytes 15364
  93.5 69.0 %copy-start.6 = (f32[1,2048]{1,0:T(1,128)S(1)}, f32[1,2048]{1,0:T(1,128)}, u32[]{:S(2)}) copy-start(f32[1,2048]{1,0:T(1,128)} %get-tuple-element.59) | copy-start | bytes 24580
  154.2 3.7 collective-permute-start
  159.2 133.1 %copy-start.11 = (f32[512]{0:T(512)}, f32[512]{0:T(512)S(1)}, u32[]{:S(2)}) copy-start(f32[512]{0:T(512)S(1)} %get-tuple-element.72) | copy-start | bytes 6148
  159.2 133.1 %copy-start.12 = (f32[512]{0:T(512)}, f32[512]{0:T(512)S(1)}, u32[]{:S(2)}) copy-start(f32[512]{0:T(512)S(1)} %get-tuple-element.83) | copy-start | bytes 6148
  160.5 218.2 %copy-start.4 = (f32[1280]{0:T(1024)}, f32[1280]{0:T(1024)S(1)}, u32[]{:S(2)}) copy-start(f32[1280]{0:T(1024)S(1)} %get-tuple-element.76) | copy-start | bytes 15364
  163.3 1.2 collective-permute-start.1
  165.3 34.5 %collective-permute-start.2 = (f32[12416]{0:T(1024)S(1)}, f32[12416]{0:T(1024)S(1)}, u32[]{:S(2)}, u32[]{:S(2)}) collective-permute-start(f32[12416]{0:T(1024)S(1)} %fusion.7), channel_id=1, source_target_pairs={{0,2},{1,3},{2,0},{3,1},{4,6},{5,7},{6,4},{7,5},{8,10},{9,11},{10,... | collective-permute-start | bytes 149000 | tf_op jit(solution)/shard_map/ppermute | solution.py:245
  199.8 12.6 %collective-permute-start.3 = (f32[12416]{0:T(1024)S(1)}, f32[12416]{0:T(1024)S(1)}, u32[]{:S(2)}, u32[]{:S(2)}) collective-permute-start(f32[12416]{0:T(1024)S(1)} %add.67), channel_id=1, source_target_pairs={{0,4},{1,5},{2,6},{3,7},{4,0},{5,1},{6,2},{7,3},{8,12},{9,13},{10,... | collective-permute-start | bytes 149000 | tf_op jit(solution)/shard_map/ppermute | solution.py:245
  215.6 163.1 %copy-start.5 = (f32[2048]{0:T(1024)}, f32[2048]{0:T(1024)S(1)}, u32[]{:S(2)}) copy-start(f32[2048]{0:T(1024)S(1)} %fusion.2) | copy-start | bytes 24580
  216.3 76.1 %copy-start.2 = (f32[5120]{0:T(1024)}, f32[5120]{0:T(1024)S(1)}, u32[]{:S(2)}) copy-start(f32[5120]{0:T(1024)S(1)} %get-tuple-element.80) | copy-start | bytes 61444
  216.3 76.1 %copy-start.3 = (f32[5120]{0:T(1024)}, f32[5120]{0:T(1024)S(1)}, u32[]{:S(2)}) copy-start(f32[5120]{0:T(1024)S(1)} %get-tuple-element.81) | copy-start | bytes 61444
  239.4 1.2 collective-permute-start.4
  240.6 3.6 collective-permute-start.5
  244.2 3.6 collective-permute-start.6
  247.8 38.5 %collective-permute-start.7 = (f32[128]{0:T(128)S(1)}, f32[128]{0:T(128)S(1)}, u32[]{:S(2)}, u32[]{:S(2)}) collective-permute-start(f32[128]{0:T(128)S(1)} %add.74), channel_id=1, source_target_pairs={{0,8},{8,0},{1,9},{9,1},{2,10},{10,2},{3,11},{11,3},{4,12},{12,4},... | collective-permute-start | bytes 1544 | tf_op jit(solution)/shard_map/ppermute | solution.py:239
  282.2 48.8 %collective-permute-start.8 = (f32[1024,512]{1,0:T(8,128)}, f32[1024,512]{1,0:T(8,128)}, u32[]{:S(2)}, u32[]{:S(2)}) collective-permute-start(f32[1024,512]{1,0:T(8,128)} %get-tuple-element.66), channel_id=1, source_target_pairs={{0,8},{8,0},{1,9},{9,1},{2,10},{10,2},{3,11},{11,3},{4,12},{12,4},... | collective-permute-start | bytes 6291464 | tf_op jit(solution)/shard_map/ppermute | solution.py:239
  282.8 93.1 %collective-permute-start.9 = (f32[1024,512]{1,0:T(8,128)}, f32[1024,512]{1,0:T(8,128)}, u32[]{:S(2)}, u32[]{:S(2)}) collective-permute-start(f32[1024,512]{1,0:T(8,128)} %get-tuple-element.68), channel_id=1, source_target_pairs={{0,8},{8,0},{1,9},{9,1},{2,10},{10,2},{3,11},{11,3},{4,12},{12,4},... | collective-permute-start | bytes 6291464 | tf_op jit(solution)/shard_map/ppermute | solution.py:239
  284.3 248.4 %collective-permute-start.14 = (bf16[512,2048]{1,0:T(8,128)(2,1)}, bf16[512,2048]{1,0:T(8,128)(2,1)}, u32[]{:S(2)}, u32[]{:S(2)}) collective-permute-start(bf16[512,2048]{1,0:T(8,128)(2,1)} %get-tuple-element.70.refs_1_), channel_id=1, source_target_pairs={{0,8},{8,0},{1,9},{9,1},{2,10},{10,2},{3,11},{11,3},{4,12},{12,4},... | collective-permute-start | bytes 6291464 | tf_op jit(solution)/shard_map/ppermute | solution.py:239
  284.9 247.8 %collective-permute-start.13 = (bf16[768,2048]{1,0:T(8,128)(2,1)}, bf16[768,2048]{1,0:T(8,128)(2,1)}, u32[]{:S(2)}, u32[]{:S(2)}) collective-permute-start(bf16[768,2048]{1,0:T(8,128)(2,1)} %get-tuple-element.69.refs_0_), channel_id=1, source_target_pairs={{0,8},{8,0},{1,9},{9,1},{2,10},{10,2},{3,11},{11,3},{4,12},{12,4},... | collective-permute-start | bytes 9437192 | tf_op jit(solution)/shard_map/ppermute | solution.py:239
  292.3 86.3 %slice-start = ((s8[10485760]{0:T(1024)(128)(4,1)}), s8[4194304]{0:T(1024)(128)(4,1)S(1)}, s32[]{:S(2)}) async-start(s8[10485760]{0:T(1024)(128)(4,1)} %bitcast.24), calls=%async_computation.1 | async-start | bytes 8388608
  292.3 86.3 %slice-start.6 = ((s8[10485760]{0:T(1024)(128)(4,1)}), s8[4194304]{0:T(1024)(128)(4,1)S(1)}, s32[]{:S(2)}) async-start(s8[10485760]{0:T(1024)(128)(4,1)} %bitcast.28), calls=%async_computation.7 | async-start | bytes 8388608
  292.4 83.6 %copy-start.1 = (f32[1024,512]{1,0:T(8,128)S(1)}, f32[1024,512]{1,0:T(8,128)}, u32[]{:S(2)}) copy-start(f32[1024,512]{1,0:T(8,128)} %get-tuple-element.67) | copy-start | bytes 6291460
  292.4 86.3 %slice-start.1 = ((s8[10485760]{0:T(1024)(128)(4,1)}), s8[4194304]{0:T(1024)(128)(4,1)S(1)}, s32[]{:S(2)}) async-start(s8[10485760]{0:T(1024)(128)(4,1)} %bitcast.24), calls=%async_computation.2 | async-start | bytes 8388608
  292.4 86.3 %slice-start.2 = ((s8[10485760]{0:T(1024)(128)(4,1)}), s8[2097152]{0:T(1024)(128)(4,1)S(1)}, s32[]{:S(2)}) async-start(s8[10485760]{0:T(1024)(128)(4,1)} %bitcast.24), calls=%async_computation.3 | async-start | bytes 4194304
  292.4 86.3 %slice-start.7 = ((s8[10485760]{0:T(1024)(128)(4,1)}), s8[4194304]{0:T(1024)(128)(4,1)S(1)}, s32[]{:S(2)}) async-start(s8[10485760]{0:T(1024)(128)(4,1)} %bitcast.28), calls=%async_computation.8 | async-start | bytes 8388608
  292.4 86.3 %slice-start.8 = ((s8[10485760]{0:T(1024)(128)(4,1)}), s8[2097152]{0:T(1024)(128)(4,1)S(1)}, s32[]{:S(2)}) async-start(s8[10485760]{0:T(1024)(128)(4,1)} %bitcast.28), calls=%async_computation.9 | async-start | bytes 4194304
  333.6 177.1 %collective-permute-start.10 = (bf16[1024,512]{1,0:T(8,128)(2,1)S(1)}, bf16[1024,512]{1,0:T(8,128)(2,1)S(1)}, u32[]{:S(2)}, u32[]{:S(2)}) collective-permute-start(bf16[1024,512]{1,0:T(8,128)(2,1)S(1)} %add_convert_fusion.1), channel_id=1, source_target_pairs={{0,8},{8,0},{1,9},{9,1},{2,10},{10,2},{3,11},{11,3},{4,12},{12,4},... | collective-permute-start | bytes 3145736 | tf_op jit(solution)/shard_map/ppermute | solution.py:239
  378.0 151.8 %collective-permute-start.11 = (bf16[1024,512]{1,0:T(8,128)(2,1)S(1)}, bf16[1024,512]{1,0:T(8,128)(2,1)S(1)}, u32[]{:S(2)}, u32[]{:S(2)}) collective-permute-start(bf16[1024,512]{1,0:T(8,128)(2,1)S(1)} %add_convert_fusion), channel_id=1, source_target_pairs={{0,8},{8,0},{1,9},{9,1},{2,10},{10,2},{3,11},{11,3},{4,12},{12,4},... | collective-permute-start | bytes 3145736 | tf_op jit(solution)/shard_map/ppermute | solution.py:239
  (11 other events, 233.1 us)
Sparse Core Ops, SparseCore 0:
  59.3 87.2 all-gather.1

commit v3 on v2

--- a/solution.py
+++ b/solution.py
@@ -134,105 +134,136 @@
     return [(out[3 * k], jnp.sum(out[3 * k + 1], axis=1), out[3 * k + 2][0]) for k in range(count)]
 
 
-def norm_kernel(steps, squares, off_ref, dyg_ref, dyu_ref, wg_ref, wu_ref, *out):
+def norm_kernel(chunk, start_ref, dyg_ref, dyu_ref, wg_ref, wu_ref, *refs):
+    out, squares, (acc_ref, wb_ref, stage_ref, sems) = refs[:4], refs[4:6], refs[6:]
     step = pl.program_id(0)
-
-    def add(dy_ref, w_ref, k):
-        w = w_ref[...]
-        b = w.astype(BF16)
-        half = dy_ref.shape[0] // 2
-        for i in range(2):
-            part = lax.dot_general(dy_ref[i * half:(i + 1) * half, :], b, NT, preferred_element_type=F32)
-            out[i][...] += part
-        if squares:
-            out[2 + k][...] += fold_squares(w)
+    weights = (wg_ref, wu_ref)
+    chunks = wg_ref.shape[1] // chunk
+    slots = stage_ref.shape[0]
+    per_out = pl.num_programs(0) // 4
+
+    def fetch(matrix, c):
+        slot = lax.rem(matrix * chunks + c, slots)
+        cols = pl.ds(pl.multiple_of(c * chunk, chunk), chunk)
+        return pltpu.make_async_copy(weights[matrix].at[:, cols], stage_ref.at[slot], sems.at[slot])
 
     @pl.when(step == 0)
     def _():
-        for ref in out:
-            ref[...] = jnp.zeros_like(ref)
-
-    @pl.when(step < steps)
-    def _():
-        add(dyg_ref, wg_ref, 0)
-
-    @pl.when(step >= steps)
-    def _():
-        add(dyu_ref, wu_ref, 1)
-
-
-def norm_partial(offset, tokens, dyg, dyu, wg, wu, squares):
-    tile = 1024
-    m, n = wg.shape
-    steps = n // tile
-
-    def block(row, k):
-        return lambda j, off: (off[0] if row else 0, jnp.clip(j - k * steps, 0, steps - 1))
-
-    out_specs = [pl.BlockSpec((tokens // 2, m), lambda j, off: (0, 0))] * 2
-    out_shape = [jax.ShapeDtypeStruct((tokens // 2, m), F32)] * 2
-    if squares:
-        out_specs += [pl.BlockSpec((8, tile), lambda j, off: (0, 0))] * 2
-        out_shape += [jax.ShapeDtypeStruct((8, tile), F32)] * 2
+        for c in range(slots):
+            fetch(0, c).start()
+        acc_ref[...] = jnp.zeros_like(acc_ref)
+        for k, dy_ref in enumerate((dyg_ref, dyu_ref)):
+            squares[k][...] = jnp.zeros_like(squares[k])
+
+            @pl.loop(0, chunks)
+            def _(c):
+                fetch(k, c).wait()
+                slot = lax.rem(k * chunks + c, slots)
+                cols = pl.ds(pl.multiple_of(c * chunk, chunk), chunk)
+                w = stage_ref[slot]
+                wb_ref[k, :, cols] = w.astype(BF16)
+                squares[k][...] += fold_squares(w)
+
+                @pl.when(c + slots < chunks)
+                def _():
+                    fetch(k, c + slots).start()
+
+                if k == 0:
+                    @pl.when(c + slots >= chunks)
+                    def _():
+                        fetch(1, c + slots - chunks).start()
+
+                acc_ref[...] += lax.dot_general(dy_ref[:, cols], wb_ref[k, :, cols], NT, preferred_element_type=F32)
+
+    @pl.when(step > 0)
+    def _():
+        acc_ref[...] = lax.dot_general(dyg_ref[...], wb_ref[0], NT, preferred_element_type=F32) + lax.dot_general(
+            dyu_ref[...], wb_ref[1], NT, preferred_element_type=F32)
+
+    for k in range(4):
+        @pl.when((step >= k * per_out) & (step < (k + 1) * per_out))
+        def _():
+            out[k][...] = acc_ref[...]
+
+
+def norm_partial(first, dyg, dyu, wg, wu):
+    tile, chunk, slots = 512, 1024, 3
+    tokens, n = dyg.shape
+    m = wg.shape[0]
+    tiles = tokens // tile
+    per_out = tiles // 4
+    dy_spec = pl.BlockSpec((tile, n), lambda i, start: (lax.rem(i + start[0], tiles), 0))
+    any_spec = pl.BlockSpec(memory_space=pl.ANY)
+
+    def block(k):
+        return lambda i, start: (jnp.clip(i - k * per_out, 0, per_out - 1), 0)
+
     out = pl.pallas_call(
-        functools.partial(norm_kernel, steps, squares),
+        functools.partial(norm_kernel, chunk),
         grid_spec=pltpu.PrefetchScalarGridSpec(
             num_scalar_prefetch=1,
-            grid=(2 * steps,),
-            in_specs=[
-                pl.BlockSpec((tokens, tile), block(True, 0)),
-                pl.BlockSpec((tokens, tile), block(True, 1)),
-                pl.BlockSpec((m, tile), block(False, 0)),
-                pl.BlockSpec((m, tile), block(False, 1)),
+            grid=(tiles,),
+            in_specs=[dy_spec, dy_spec, any_spec, any_spec],
+            out_specs=[pl.BlockSpec((tile, m), block(k)) for k in range(4)]
+            + [pl.BlockSpec((8, chunk), lambda i, start: (0, 0))] * 2,
+            scratch_shapes=[
+                pltpu.VMEM((tile, m), F32),
+                pltpu.VMEM((2, m, n), BF16),
+                pltpu.VMEM((slots, m, chunk), F32),
+                pltpu.SemaphoreType.DMA((slots,)),
             ],
-            out_specs=out_specs,
         ),
-        out_shape=out_shape,
+        out_shape=[jax.ShapeDtypeStruct((tokens // 4, m), F32)] * 4 + [jax.ShapeDtypeStruct((8, chunk), F32)] * 2,
         compiler_params=params('arbitrary'),
         cost_estimate=cost(4 * tokens * m * n, 4 * tokens * n + 8 * m * n + 4 * tokens * m),
         name='norm_partial',
-    )((offset // tokens).astype(jnp.int32).reshape(1), dyg, dyu, wg, wu)
-    return [*out[:2], *[jnp.sum(s) for s in out[2:]]]
-
-
-def act_kernel(block, parts, dya_ref, dyb_ref, *refs):
+    )((first * (tiles // 2)).astype(jnp.int32).reshape(1), dyg, dyu, wg, wu)
+    return [*out[:4], *[jnp.sum(v) for v in out[4:]]]
+
+
+def act_kernel(parts, dya_ref, dyb_ref, *refs):
     out_ref, acc_ref = refs[-2:]
-    done = 0
-    for wa_ref, wb_ref in zip(refs[:parts], refs[parts:2 * parts]):
-        count = wa_ref.shape[0] // block
-
-        @pl.loop(0, count)
-        def _(k):
-            rows = pl.ds(pl.multiple_of(k * block, block), block)
-            acc_ref[k] = lax.dot_general(dya_ref[...], wa_ref[rows, :], NT, preferred_element_type=F32)
-
-        @pl.loop(0, count)
-        def _(k):
-            rows = pl.ds(pl.multiple_of(k * block, block), block)
-            cols = pl.ds(pl.multiple_of(done + k * block, block), block)
-            other = lax.dot_general(dyb_ref[...], wb_ref[rows, :], NT, preferred_element_type=F32)
-            out_ref[:, cols] = (acc_ref[k] + other).astype(BF16)
-
-        done += wa_ref.shape[0]
+
+    def halves(dy_ref, w_refs):
+        done = 0
+        for w_ref in w_refs:
+            yield slice(done, done + w_ref.shape[0]), lax.dot_general(
+                dy_ref[...], w_ref[...], NT, preferred_element_type=F32)
+            done += w_ref.shape[0]
+
+    @pl.when(pl.program_id(0) >= 0)
+    def _():
+        for cols, part in halves(dya_ref, refs[:parts]):
+            acc_ref[:, cols] = part
+
+    @pl.when(pl.program_id(0) < pl.num_programs(0))
+    def _():
+        for cols, part in halves(dyb_ref, refs[parts:2 * parts]):
+            out_ref[:, cols] = (acc_ref[:, cols] + part).astype(BF16)
 
 
 def act_grad(dya, dyb, wa, wb):
-    tile, block = 512, 256
+    tile = 512
     tokens, n = dya.shape
     m = sum(w.shape[0] for w in wa)
     dy_spec = pl.BlockSpec((tile, n), lambda i: (i, 0))
     w_specs = [pl.BlockSpec(w.shape, lambda i: (0, 0), pipeline_mode=pl.Buffered(1)) for w in (*wa, *wb)]
     return pl.pallas_call(
-        functools.partial(act_kernel, block, len(wa)),
+        functools.partial(act_kernel, len(wa)),
         grid=(tokens // tile,),
         in_specs=[dy_spec, dy_spec, *w_specs],
         out_specs=pl.BlockSpec((tile, m), lambda i: (i, 0)),
         out_shape=jax.ShapeDtypeStruct((tokens, m), BF16),
-        scratch_shapes=[pltpu.VMEM((max(w.shape[0] for w in wa) // block, tile, block), F32)],
+        scratch_shapes=[pltpu.VMEM((tile, m), F32)],
         compiler_params=params('arbitrary'),
         cost_estimate=cost(4 * tokens * m * n, 4 * tokens * n + 4 * m * n + 2 * tokens * m),
         name='act_grad',
     )(dya, dyb, *wa, *wb)
+
+
+def lanes(values):
+    index = lax.iota(jnp.int32, 128)
+    return sum(jnp.where(index == k, v, 0.0) for k, v in enumerate(values))
 
 
 def swap_col(v):
@@ -275,9 +306,8 @@
         row_all = jnp.concatenate([row_gate, row_up, row_down])
         row_peer = swap_col(row_all)
         o_down_b = swap_col(b_down_b)
-        sent = norm_partial((1 - col) * half, half, dy_gate, dy_up, w_gate, w_up, False)
-        got0 = swap_col(sent[0])
-        own0, own1, w_sq_gate, w_sq_up = norm_partial(col * half, half, dy_gate, dy_up, w_gate, w_up, True)
+        sent0, sent1, own0, own1, w_sq_gate, w_sq_up = norm_partial(1 - col, dy_gate, dy_up, w_gate, w_up)
+        got0 = swap_col(sent0)
 
         sizes_r = [r_gate.shape[0], r_up.shape[0], r_down.shape[0]]
         sizes_c = [c_gate.shape[0], c_up.shape[0], c_down.shape[0]]
@@ -287,28 +317,27 @@
         r_old = [r_gate, r_up, r_down]
         c_old = [c_gate, c_up, c_down]
         r_new = [beta_two * r_old[k] + (1.0 - beta_two) * (row_sums[k] / totals[k][1]) for k in range(3)]
-        r_part = jnp.zeros((128,), F32).at[:3].set(jnp.stack([jnp.sum(r) for r in r_new]))
+        r_part = lanes([jnp.sum(r) for r in r_new])
         col_all = sum_row(jnp.concatenate([col_gate, col_up, col_down, r_part]), row_size)
         offs = [0, sizes_c[0], sizes_c[0] + sizes_c[1], sum(sizes_c)]
         c_new = [
             beta_two * c_old[k] + (1.0 - beta_two) * (col_all[offs[k]:offs[k + 1]] / totals[k][0]) for k in range(3)
         ]
-        r_mean = [col_all[offs[3] + k] / totals[k][0] for k in range(3)]
+        r_mean = [col_all[offs[3] + k:offs[3] + k + 1] / totals[k][0] for k in range(3)]
         grads = [g_gate, g_up, g_down]
-        updates = [grads[k] * lax.rsqrt(r_new[k][:, None] * c_new[k][None, :] / r_mean[k]) for k in range(3)]
-        scalars = jnp.stack([jnp.sum(u * u) for u in updates] + [w_sq_gate, w_sq_up, w_sq_down])
-        scalars = sum_row(jnp.zeros((128,), F32).at[:6].set(scalars), row_size)
+        updates = [grads[k] * lax.rsqrt((r_new[k] / r_mean[k])[:, None] * c_new[k][None, :]) for k in range(3)]
+        scalars = lanes([jnp.sum(u * u) for u in updates] + [w_sq_gate, w_sq_up, w_sq_down])
+        scalars = sum_row(scalars, row_size)
         scalars_peer = swap_col(scalars)
-        got1 = swap_col(sent[1])
+        got1 = swap_col(sent1)
         dx_act = act_grad(dy_down, dy_down_other, [b_down_a, b_down_b], [o_down_a, o_down_b])
         scalars = scalars + scalars_peer
+        size = float(totals[0][0] * totals[0][1])
+        rms_u = jnp.sqrt(scalars[:3] / size)
+        rms_w = jnp.sqrt(scalars[3:6] / size)
+        scale = hyper_params[1:2] * jnp.maximum(EPS_TWO, rms_w) / jnp.maximum(1.0, rms_u / hyper_params[2:3])
         weights = [w_gate, w_up, w_down]
-        new = []
-        for k in range(3):
-            size = totals[k][0] * totals[k][1]
-            rms_u = jnp.sqrt(scalars[k] / size)
-            step_size = hyper_params[1] * jnp.maximum(EPS_TWO, jnp.sqrt(scalars[3 + k] / size))
-            new.append(weights[k] - step_size * (updates[k] / jnp.maximum(1.0, rms_u / hyper_params[2])))
+        new = [weights[k] - scale[k:k + 1, None] * updates[k] for k in range(3)]
 
         mine0 = (own0 + got0).astype(BF16)
         theirs0 = swap_col(mine0)
@@ -316,9 +345,10 @@
         theirs1 = swap_col(mine1)
         dx_norm = jnp.where(
             col == 0,
-            jnp.concatenate([mine0, mine1, theirs0, theirs1]),
-            jnp.concatenate([theirs0, theirs1, mine0, mine1]),
+            jnp.concatenate([mine0, mine1, theirs0, theirs0]),
+            jnp.concatenate([theirs0, theirs0, mine0, mine1]),
         )
+        dx_norm = lax.dynamic_update_slice_in_dim(dx_norm, theirs1, (1 - col) * half + half // 2, axis=0)
         return (*new, r_new[0], c_new[0], r_new[1], c_new[1], r_new[2], c_new[2], dx_norm, dx_act)
 
     return jax.shard_map(body, mesh=mesh, in_specs=in_specs, out_specs=out_specs, check_vma=False)

time: 607 us -> 590 us (0.972)
  other arithmetic: 68.4 us -> 92.3 us
  Pallas kernels: 232 us -> 211 us
  between operations: 27.7 us -> 17 us
  waiting for transfers between devices: 253 us -> 244 us
    pallas_call x3 -> x2, Pallas kernels: 132 us -> 112 us  [the longest x1 58.6 us: norm_partial(): pl.pallas_call(functools.partial(norm_kernel, chunk), grid_spec=pltpu.Pre...]
    sub x2, other arithmetic: 28.1 us -> 38 us  [body(): new = [weights[k] - scale[k:k + 1, None] * updates[k] for k in range(3)]]
    add x6, other arithmetic: 0.79 us -> 8.42 us  [sum_row(): v = v + lax.ppermute(v, 'row', [(i, i ^ step) for i in range(row_size)])]
    ppermute x9, waiting for transfers between devices: 245 us -> 238 us  [swap_col(): return lax.ppermute(v, 'col', [(0, 1), (1, 0)])]
  transfers between devices with their start and end apart: 16 -> 16, of which waited for: 10 -> 9; matrix products, arithmetic and copies ran while one was open for 12% -> 16% of each run, Pallas kernels for 27% -> 27%
where the time goes in v3:
time: 590 us; the launch traced here: 589 us
  waiting for transfers between devices  244 us (41%)
  Pallas kernels  211 us (36%)
  other arithmetic  92.3 us (16%)
  starting transfers between devices  18.3 us (3%)
  between operations  17 us (3%)
  local copies, waits for them, and re-layouts  6.09 us (1%)
    ppermute x9, waiting for transfers between devices, swap_col(): return lax.ppermute(v, 'col', [(0, 1), (1, 0)])  238 us
    pallas_call x2, Pallas kernels, weight_grads(): pl.pallas_call(functools.partial(grad_kernel, count, steps), grid=(steps...  91.4 us
    pallas_call x1, Pallas kernels, norm_partial(): pl.pallas_call(functools.partial(norm_kernel, chunk), grid_spec=pltpu.Pre...  58.6 us
    pallas_call x1, Pallas kernels, act_grad(): pl.pallas_call(functools.partial(act_kernel, len(wa)), grid=(tokens // ti...  53.1 us
    sub x2, other arithmetic, body(): new = [weights[k] - scale[k:k + 1, None] * updates[k] for k in range(3)]  38 us
    reduce_sum x3, other arithmetic, body(): jnp.sum(u * u)  20.6 us
    ppermute x9, starting transfers between devices, swap_col(): return lax.ppermute(v, 'col', [(0, 1), (1, 0)])  14.4 us
  transfers between devices with their start and end apart: 16, of which 9 were waited for; matrix products, arithmetic and copies ran while one was open for 16% of the time, Pallas kernels for 27%

profile of v3, /device:TPU:0, one launch (start us, length us, event | category | flops | bytes accessed | tf_op | source)
XLA Modules:
  0.0 588.9 jit_solution(12958448641698407273)
XLA Ops:
  7.2 1.7 constant_dynamic-slice_fusion
  9.0 3.3 collective-permute-start.12
  12.3 45.6 %collective-permute-done.12 = bf16[512,2048]{1,0:T(8,128)(2,1)S(1)} collective-permute-done((bf16[512,2048]{1,0:T(8,128)(2,1)S(1)}, bf16[512,2048]{1,0:T(8,128)(2,1)S(1)}, u32[]{:S(2)}, u32[]{:S(2)}) %collective-permute-start.12) | collective-permute-done | bytes 2097184 | tf_op jit(solution)/shard_map/ppermute | solution.py:270
  59.2 32.9 %weight_grads.3 = (f32[1280,2048]{1,0:T(8,128)}, f32[1280,128]{1,0:T(8,128)}, f32[1,2048]{1,0:T(1,128)}) custom-call(bf16[4096,1280]{1,0:T(8,128)(2,1)} %x_ref.3, bf16[4096,2048]{1,0:T(8,128)(2,1)} %dya_ref.1), custom_call_target="tpu_custom_call" | custom-call | flops 21474836480 | bytes 37748736 | tf_op jit(solution)/shard_map/weight_grads/pallas_call | solution.py:122
  93.5 58.6 %weight_grads.2 = (f32[512,5120]{1,0:T(8,128)}, f32[512,128]{1,0:T(8,128)}, f32[1,5120]{1,0:T(1,128)}, f32[512,5120]{1,0:T(8,128)}, f32[512,128]{1,0:T(8,128)}, /*index=5*/f32[1,5120]{1,0:T(1,128)}) custom-call(bf16[4096,512]{1,0:T(8,128)(2,1)} %x_ref.2, bf16[4096,5120]{1,0:T(8,128)(2,1)} %dyg_ref.1, bf16[4096,5120]{1,0:T(8,128)(2,1)} %dyu_ref.1), custom_call_target="tpu_custom_call" | custom-call | flops 42949672960 | bytes 113246208 | tf_op jit(solution)/shard_map/weight_grads/pallas_call | solution.py:122
  154.3 1.6 collective-permute-start
  160.5 1.9 fusion.7
  166.6 58.6 %norm_partial.1 = (f32[1024,512]{1,0:T(8,128)}, f32[1024,512]{1,0:T(8,128)}, f32[1024,512]{1,0:T(8,128)}, f32[1024,512]{1,0:T(8,128)}, f32[8,1024]{1,0:T(8,128)}, /*index=5*/f32[8,1024]{1,0:T(8,128)}) custom-call(s32[1]{0:T(128)} %bitcast.8.start_ref, bf16[4096,5120]{1,0:T(8,128)(2,1)} %dyg_ref.1, bf16[4096,5120]{1,0:T(8,128)(2,1)} %dyu_ref.1, ...), custom_call_target="tpu_custom_call" | custom-call | flops 42949672960 | bytes 113246208 | tf_op jit(solution)/shard_map/norm_partial/pallas_call | solution.py:201
  225.3 1.5 collective-permute-start.3
  226.8 8.2 %cast_weight.1 = (bf16[768,2048]{1,0:T(8,128)(2,1)}, bf16[512,2048]{1,0:T(8,128)(2,1)}, f32[8,2048]{1,0:T(8,128)}) custom-call(f32[1280,2048]{1,0:T(8,128)} %w_ref.1), custom_call_target="tpu_custom_call" | custom-call | flops 2621440000 | bytes 15728640 | tf_op jit(solution)/shard_map/cast_weight/pallas_call | solution.py:53
  235.0 1.4 reduce_sum.119
  241.7 8.3 %multiply_reduce_fusion = f32[]{:T(128)} fusion(f32[1280,2048]{1,0:T(8,128)} %get-tuple-element.37, f32[2048]{0:T(1024)S(1)} %fusion.2, f32[1280]{0:T(1024)S(1)} %broadcast_divide_fusion), kind=kLoop, calls=%fused_computation.3 | loop fusion | flops 10485759 | bytes 10499076 | tf_op jit(solution)/shard_map/reduce_sum | solution.py:329
  250.0 7.5 %multiply_reduce_fusion.1 = f32[]{:T(128)} fusion(f32[512,5120]{1,0:T(8,128)} %get-tuple-element.36, f32[5120]{0:T(1024)S(1)} %get-tuple-element.57, f32[512]{0:T(512)S(1)} %broadcast_divide_fusion.1), kind=kLoop, calls=%fused_computation.5 | loop fusion | flops 10485759 | bytes 10508292 | tf_op jit(solution)/shard_map/reduce_sum | solution.py:329
  257.5 4.8 multiply_reduce_fusion.2
  262.3 3.8 fusion.12
  267.3 3.8 fusion.24
  271.6 3.2 collective-permute-done.5
  274.8 3.8 fusion.25
  279.2 1.8 collective-permute-start.14
  281.2 1.8 collective-permute-start.8
  285.0 155.3 %collective-permute-done.7 = f32[128]{0:T(128)S(1)} collective-permute-done((f32[128]{0:T(128)S(1)}, f32[128]{0:T(128)S(1)}, u32[]{:S(2)}, u32[]{:S(2)}) %collective-permute-start.7) | collective-permute-done | bytes 544 | tf_op jit(solution)/shard_map/ppermute | solution.py:270
  442.4 26.5 %multiply_subtract_fusion.1 = (f32[512,5120]{1,0:T(8,128)}, f32[512,5120]{1,0:T(8,128)}) fusion(f32[512,5120]{1,0:T(8,128)} %wu_ref.1, f32[512,5120]{1,0:T(8,128)} %get-tuple-element.36, f32[]{:T(128)} %bitcast.11, f32[5120]{0:T(1024)S(1)} %get-tuple-element.57, f32[512]{0:T(512)S(1)} %broadcast_divide_fusion.1, f32[512,5120]{1,0:T(8,128)} %wg_ref.1, ...), kind=kLoop, calls=%fused_computation.1 | loop fusion | flops 20971520 | bytes 62959624 | tf_op jit(solution)/shard_map/sub | solution.py:340
  468.9 2.6 add_convert_fusion.1
  471.5 1.8 collective-permute-start.10
  473.3 12.0 %collective-permute-done.9 = f32[1024,512]{1,0:T(8,128)} collective-permute-done((f32[1024,512]{1,0:T(8,128)}, f32[1024,512]{1,0:T(8,128)}, u32[]{:S(2)}, u32[]{:S(2)}) %collective-permute-start.9) | collective-permute-done | bytes 2097184 | tf_op jit(solution)/shard_map/ppermute | solution.py:270
  485.3 1.9 add_convert_fusion
  487.2 1.8 collective-permute-start.11
  489.1 11.5 %multiply_subtract_fusion = f32[1280,2048]{1,0:T(8,128)} fusion(f32[1280,2048]{1,0:T(8,128)S(1)} %bitcast.14, f32[1280,2048]{1,0:T(8,128)} %get-tuple-element.37, f32[]{:T(128)} %bitcast.12, f32[2048]{0:T(1024)S(1)} %fusion.2, f32[1280]{0:T(1024)S(1)} %broadcast_divide_fusion), kind=kLoop, calls=%fused_computation | loop fusion | flops 10485760 | bytes 31470596 | tf_op jit(solution)/shard_map/sub | solution.py:340
  500.6 7.1 %collective-permute-done.10 = bf16[1024,512]{1,0:T(8,128)(2,1)S(1)} collective-permute-done((bf16[1024,512]{1,0:T(8,128)(2,1)S(1)}, bf16[1024,512]{1,0:T(8,128)(2,1)S(1)}, u32[]{:S(2)}, u32[]{:S(2)}) %collective-permute-start.10) | collective-permute-done | bytes 1048608 | tf_op jit(solution)/shard_map/ppermute | solution.py:270
  507.7 2.8 maximum_select_fusion
  510.5 17.4 %collective-permute-done.11 = bf16[1024,512]{1,0:T(8,128)(2,1)S(1)} collective-permute-done((bf16[1024,512]{1,0:T(8,128)(2,1)S(1)}, bf16[1024,512]{1,0:T(8,128)(2,1)S(1)}, u32[]{:S(2)}, u32[]{:S(2)}) %collective-permute-start.11) | collective-permute-done | bytes 1048608 | tf_op jit(solution)/shard_map/ppermute | solution.py:270
  529.0 53.1 %act_grad.1 = bf16[4096,1280]{1,0:T(8,128)(2,1)} custom-call(bf16[4096,2048]{1,0:T(8,128)(2,1)} %dya_ref.1, bf16[4096,2048]{1,0:T(8,128)(2,1)} %all-gather.2.cloned.1.call-done.dyb_ref, bf16[768,2048]{1,0:T(8,128)(2,1)} %get-tuple-element.45.refs_0_, bf16[512,2048]{1,0:T(8,128)(2,1)} %get-tuple-element.46.refs_1_, ...), custom_call_target="tpu_custom_call" | custom-call | flops 42949672960 | bytes 54525952 | tf_op jit(solution)/shard_map/act_grad/pallas_call | solution.py:251
  (95 shorter events, 23.7 us)
Async XLA Ops:
  7.2 521.8 %all-gather.2.cloned.1.call-start = ((), (), s32[]{:S(2)}) async-start(), calls=%async_computation | async-start | bytes 18874368 | tf_op jit(solution)/shard_map/all_gather | solution.py:300
  9.0 48.9 %collective-permute-start.12 = (bf16[512,2048]{1,0:T(8,128)(2,1)S(1)}, bf16[512,2048]{1,0:T(8,128)(2,1)S(1)}, u32[]{:S(2)}, u32[]{:S(2)}) collective-permute-start(bf16[512,2048]{1,0:T(8,128)(2,1)S(1)} %constant_dynamic-slice_fusion), channel_id=1, source_target_pairs={{0,8},{8,0},{1,9},{9,1},{2,10},{10,2},{3,11},{11,3},{4,12},{12,4},... | collective-permute-start | bytes 6291464 | tf_op jit(solution)/shard_map/ppermute | solution.py:270
  93.4 62.5 %copy-start.15 = (f32[3]{0:T(128)S(1)}, f32[3]{0:T(128)}, u32[]{:S(2)}) copy-start(f32[3]{0:T(128)} %param.29) | copy-start | bytes 40
  93.4 64.6 %copy-start.16 = (f32[512]{0:T(512)S(1)}, f32[512]{0:T(512)}, u32[]{:S(2)}) copy-start(f32[512]{0:T(512)} %param.23) | copy-start | bytes 6148
  93.5 64.6 %copy-start.17 = (f32[512]{0:T(512)S(1)}, f32[512]{0:T(512)}, u32[]{:S(2)}) copy-start(f32[512]{0:T(512)} %param.25) | copy-start | bytes 6148
  93.5 65.8 %copy-start.11 = (f32[1280]{0:T(1024)S(1)}, f32[1280]{0:T(1024)}, u32[]{:S(2)}) copy-start(f32[1280]{0:T(1024)} %param.27) | copy-start | bytes 15364
  93.5 69.0 %copy-start.5 = (f32[1,2048]{1,0:T(1,128)S(1)}, f32[1,2048]{1,0:T(1,128)}, u32[]{:S(2)}) copy-start(f32[1,2048]{1,0:T(1,128)} %get-tuple-element.35) | copy-start | bytes 24580
  154.3 3.7 collective-permute-start
  159.3 81.0 %copy-start.13 = (f32[512]{0:T(512)}, f32[512]{0:T(512)S(1)}, u32[]{:S(2)}) copy-start(f32[512]{0:T(512)S(1)} %get-tuple-element.48) | copy-start | bytes 6148
  159.3 81.0 %copy-start.14 = (f32[512]{0:T(512)}, f32[512]{0:T(512)S(1)}, u32[]{:S(2)}) copy-start(f32[512]{0:T(512)S(1)} %get-tuple-element.59) | copy-start | bytes 6148
  160.5 79.8 %copy-start.6 = (f32[1280]{0:T(1024)}, f32[1280]{0:T(1024)S(1)}, u32[]{:S(2)}) copy-start(f32[1280]{0:T(1024)S(1)} %get-tuple-element.52) | copy-start | bytes 15364
  163.2 1.2 collective-permute-start.1
  165.2 60.0 %collective-permute-start.2 = (f32[12416]{0:T(1024)S(1)}, f32[12416]{0:T(1024)S(1)}, u32[]{:S(2)}, u32[]{:S(2)}) collective-permute-start(f32[12416]{0:T(1024)S(1)} %fusion.14), channel_id=1, source_target_pairs={{0,2},{1,3},{2,0},{3,1},{4,6},{5,7},{6,4},{7,5},{8,10},{9,11},{10,... | collective-permute-start | bytes 149000 | tf_op jit(solution)/shard_map/ppermute | solution.py:276
  225.3 12.4 %collective-permute-start.3 = (f32[12416]{0:T(1024)S(1)}, f32[12416]{0:T(1024)S(1)}, u32[]{:S(2)}, u32[]{:S(2)}) collective-permute-start(f32[12416]{0:T(1024)S(1)} %add.87), channel_id=1, source_target_pairs={{0,4},{1,5},{2,6},{3,7},{4,0},{5,1},{6,2},{7,3},{8,12},{9,13},{10,... | collective-permute-start | bytes 149000 | tf_op jit(solution)/shard_map/ppermute | solution.py:276
  241.0 248.1 %copy-start.4 = (f32[2048]{0:T(1024)}, f32[2048]{0:T(1024)S(1)}, u32[]{:S(2)}) copy-start(f32[2048]{0:T(1024)S(1)} %fusion.2) | copy-start | bytes 24580
  241.6 200.7 %copy-start.2 = (f32[5120]{0:T(1024)}, f32[5120]{0:T(1024)S(1)}, u32[]{:S(2)}) copy-start(f32[5120]{0:T(1024)S(1)} %get-tuple-element.56) | copy-start | bytes 61444
  241.7 200.7 %copy-start.3 = (f32[5120]{0:T(1024)}, f32[5120]{0:T(1024)S(1)}, u32[]{:S(2)}) copy-start(f32[5120]{0:T(1024)S(1)} %get-tuple-element.57) | copy-start | bytes 61444
  241.7 15.8 %slice-start.3 = ((s8[10485760]{0:T(1024)(128)(4,1)}), s8[4194304]{0:T(1024)(128)(4,1)S(1)}, s32[]{:S(2)}) async-start(s8[10485760]{0:T(1024)(128)(4,1)} %bitcast.15), calls=%async_computation.4 | async-start | bytes 8388608
  266.1 1.2 collective-permute-start.4
  271.2 3.6 collective-permute-start.5
  278.6 4.4 collective-permute-start.6
  279.2 249.8 %collective-permute-start.14 = (bf16[512,2048]{1,0:T(8,128)(2,1)}, bf16[512,2048]{1,0:T(8,128)(2,1)}, u32[]{:S(2)}, u32[]{:S(2)}) collective-permute-start(bf16[512,2048]{1,0:T(8,128)(2,1)} %get-tuple-element.46.refs_1_), channel_id=1, source_target_pairs={{0,8},{8,0},{1,9},{9,1},{2,10},{10,2},{3,11},{11,3},{4,12},{12,4},... | collective-permute-start | bytes 6291464 | tf_op jit(solution)/shard_map/ppermute | solution.py:270
  280.9 248.0 %collective-permute-start.13 = (bf16[768,2048]{1,0:T(8,128)(2,1)}, bf16[768,2048]{1,0:T(8,128)(2,1)}, u32[]{:S(2)}, u32[]{:S(2)}) collective-permute-start(bf16[768,2048]{1,0:T(8,128)(2,1)} %get-tuple-element.45.refs_0_), channel_id=1, source_target_pairs={{0,8},{8,0},{1,9},{9,1},{2,10},{10,2},{3,11},{11,3},{4,12},{12,4},... | collective-permute-start | bytes 9437192 | tf_op jit(solution)/shard_map/ppermute | solution.py:270
  281.2 187.7 %collective-permute-start.8 = (f32[1024,512]{1,0:T(8,128)}, f32[1024,512]{1,0:T(8,128)}, u32[]{:S(2)}, u32[]{:S(2)}) collective-permute-start(f32[1024,512]{1,0:T(8,128)} %get-tuple-element.42), channel_id=1, source_target_pairs={{0,8},{8,0},{1,9},{9,1},{2,10},{10,2},{3,11},{11,3},{4,12},{12,4},... | collective-permute-start | bytes 6291464 | tf_op jit(solution)/shard_map/ppermute | solution.py:270
  283.0 157.4 %collective-permute-start.7 = (f32[128]{0:T(128)S(1)}, f32[128]{0:T(128)S(1)}, u32[]{:S(2)}, u32[]{:S(2)}) collective-permute-start(f32[128]{0:T(128)S(1)} %add.99), channel_id=1, source_target_pairs={{0,8},{8,0},{1,9},{9,1},{2,10},{10,2},{3,11},{11,3},{4,12},{12,4},... | collective-permute-start | bytes 1544 | tf_op jit(solution)/shard_map/ppermute | solution.py:270
  283.8 201.5 %collective-permute-start.9 = (f32[1024,512]{1,0:T(8,128)}, f32[1024,512]{1,0:T(8,128)}, u32[]{:S(2)}, u32[]{:S(2)}) collective-permute-start(f32[1024,512]{1,0:T(8,128)} %get-tuple-element.44), channel_id=1, source_target_pairs={{0,8},{8,0},{1,9},{9,1},{2,10},{10,2},{3,11},{11,3},{4,12},{12,4},... | collective-permute-start | bytes 6291464 | tf_op jit(solution)/shard_map/ppermute | solution.py:270
  442.4 46.7 %slice-start = ((s8[10485760]{0:T(1024)(128)(4,1)}), s8[4194304]{0:T(1024)(128)(4,1)S(1)}, s32[]{:S(2)}) async-start(s8[10485760]{0:T(1024)(128)(4,1)} %bitcast.13), calls=%async_computation.1 | async-start | bytes 8388608
  442.4 42.9 %copy-start.1 = (f32[1024,512]{1,0:T(8,128)S(1)}, f32[1024,512]{1,0:T(8,128)}, u32[]{:S(2)}) copy-start(f32[1024,512]{1,0:T(8,128)} %get-tuple-element.43) | copy-start | bytes 6291460
  442.4 46.7 %slice-start.1 = ((s8[10485760]{0:T(1024)(128)(4,1)}), s8[4194304]{0:T(1024)(128)(4,1)S(1)}, s32[]{:S(2)}) async-start(s8[10485760]{0:T(1024)(128)(4,1)} %bitcast.13), calls=%async_computation.2 | async-start | bytes 8388608
  442.4 46.7 %slice-start.2 = ((s8[10485760]{0:T(1024)(128)(4,1)}), s8[2097152]{0:T(1024)(128)(4,1)S(1)}, s32[]{:S(2)}) async-start(s8[10485760]{0:T(1024)(128)(4,1)} %bitcast.13), calls=%async_computation.3 | async-start | bytes 4194304
  471.5 36.2 %collective-permute-start.10 = (bf16[1024,512]{1,0:T(8,128)(2,1)S(1)}, bf16[1024,512]{1,0:T(8,128)(2,1)S(1)}, u32[]{:S(2)}, u32[]{:S(2)}) collective-permute-start(bf16[1024,512]{1,0:T(8,128)(2,1)S(1)} %add_convert_fusion.1), channel_id=1, source_target_pairs={{0,8},{8,0},{1,9},{9,1},{2,10},{10,2},{3,11},{11,3},{4,12},{12,4},... | collective-permute-start | bytes 3145736 | tf_op jit(solution)/shard_map/ppermute | solution.py:270
  487.2 40.7 %collective-permute-start.11 = (bf16[1024,512]{1,0:T(8,128)(2,1)S(1)}, bf16[1024,512]{1,0:T(8,128)(2,1)S(1)}, u32[]{:S(2)}, u32[]{:S(2)}) collective-permute-start(bf16[1024,512]{1,0:T(8,128)(2,1)S(1)} %add_convert_fusion), channel_id=1, source_target_pairs={{0,8},{8,0},{1,9},{9,1},{2,10},{10,2},{3,11},{11,3},{4,12},{12,4},... | collective-permute-start | bytes 3145736 | tf_op jit(solution)/shard_map/ppermute | solution.py:270
  (8 other events, 94.5 us)
Sparse Core Ops, SparseCore 0:
  59.3 87.2 all-gather.1

commit v4 on v3

--- a/solution.py
+++ b/solution.py
@@ -68,7 +68,7 @@
         cost_estimate=cost(w.size * 1000, w.size * 6),
         name='cast_weight',
     )(w)
-    return a, b, jnp.sum(s)
+    return a, b, s
 
 
 def grad_block(xt_ref, dy_ref, g_ref, row_ref, col_ref):
@@ -83,19 +83,25 @@
 
 
 def grad_kernel(count, steps, x_ref, *refs):
-    dy, out, xt_ref = refs[:count], refs[count:-1], refs[-1]
+    dy, out, xt_ref, part_ref = refs[:count], refs[count:-2], refs[-2], refs[-1]
     step = pl.program_id(0)
 
     @pl.when(step == 0)
     def _():
-        for k in range(count):
-            out[3 * k + 1][...] = jnp.zeros_like(out[3 * k + 1])
         xt_ref[...] = x_ref[...].T
 
     for k in range(count):
+        @pl.when(step == k * steps)
+        def _():
+            part_ref[...] = jnp.zeros_like(part_ref)
+
         @pl.when((step >= k * steps) & (step < (k + 1) * steps))
         def _():
-            grad_block(xt_ref, dy[k], *out[3 * k:3 * k + 3])
+            grad_block(xt_ref, dy[k], out[3 * k], part_ref, out[3 * k + 2])
+
+        @pl.when(step == (k + 1) * steps - 1)
+        def _():
+            out[3 * k + 1][...] = jnp.sum(part_ref[...].T, axis=0, keepdims=True)
 
 
 def weight_grads(x, dys, tile):
@@ -111,12 +117,12 @@
     for k in range(count):
         out_specs += [
             pl.BlockSpec((m, tile), block(k)),
-            pl.BlockSpec((m, 128), lambda j: (0, 0)),
+            pl.BlockSpec((1, m), lambda j: (0, 0)),
             pl.BlockSpec((1, tile), block(k)),
         ]
         out_shape += [
             jax.ShapeDtypeStruct((m, n), F32),
-            jax.ShapeDtypeStruct((m, 128), F32),
+            jax.ShapeDtypeStruct((1, m), F32),
             jax.ShapeDtypeStruct((1, n), F32),
         ]
     out = pl.pallas_call(
@@ -126,12 +132,12 @@
         + [pl.BlockSpec((tokens, tile), block(k)) for k in range(count)],
         out_specs=out_specs,
         out_shape=out_shape,
-        scratch_shapes=[pltpu.VMEM((m, tokens), BF16)],
+        scratch_shapes=[pltpu.VMEM((m, tokens), BF16), pltpu.VMEM((m, 128), F32)],
         compiler_params=params('arbitrary'),
         cost_estimate=cost(2 * count * tokens * m * n, count * (2 * tokens * (m + n) + 4 * m * n)),
         name='weight_grads',
     )(x, *dys)
-    return [(out[3 * k], jnp.sum(out[3 * k + 1], axis=1), out[3 * k + 2][0]) for k in range(count)]
+    return [tuple(out[3 * k:3 * k + 3]) for k in range(count)]
 
 
 def norm_kernel(chunk, start_ref, dyg_ref, dyu_ref, wg_ref, wu_ref, *refs):
@@ -218,52 +224,155 @@
         cost_estimate=cost(4 * tokens * m * n, 4 * tokens * n + 8 * m * n + 4 * tokens * m),
         name='norm_partial',
     )((first * (tiles // 2)).astype(jnp.int32).reshape(1), dyg, dyu, wg, wu)
-    return [*out[:4], *[jnp.sum(v) for v in out[4:]]]
-
-
-def act_kernel(parts, dya_ref, dyb_ref, *refs):
-    out_ref, acc_ref = refs[-2:]
-
-    def halves(dy_ref, w_refs):
+    return out
+
+
+def lane_fold(v):
+    return functools.reduce(lambda p, q: p + q, [v[:, k:k + 128] for k in range(0, v.shape[1], 128)])
+
+
+def direction(g, r_ref, rows, c_ref):
+    r = r_ref[rows, :]
+    r = jnp.concatenate([r] * (g.shape[1] // 128), axis=1)
+    return g * lax.rsqrt(r * c_ref[...])
+
+
+def square_kernel(row_total, sizes, hyper_ref, g0, g1, g2, all_ref, r_ref,
+                  c0, c1, c2, w0, w1, w2, n0, n1, n2, ratio_ref, part_ref, acc_ref):
+    step = pl.program_id(0)
+    beta_two = hyper_ref[0]
+    grads, c_new = (g0, g1, g2), (n0, n1, n2)
+    starts = [0, sizes[0], sizes[0] + sizes[1]]
+
+    @pl.when(step == 0)
+    def _():
+        off = 0
+        for c_old, new, total in zip((c0, c1, c2), c_new, row_total):
+            size = c_old.shape[1]
+            new[...] = beta_two * c_old[...] + (1.0 - beta_two) * (all_ref[:, off:off + size] / total)
+            off += size
+        for k in range(3):
+            mean = jnp.sum(all_ref[:, off + 128 * k:off + 128 * k + 128], axis=1, keepdims=True) / row_total[k]
+            for i in range(starts[k], starts[k] + sizes[k], 128):
+                ratio_ref[i:i + 128, :] = jnp.broadcast_to(r_ref[:, i:i + 128] / mean, (128, 128)).T
+        acc_ref[...] = jnp.zeros_like(acc_ref)
+
+    for k in range(3):
+        tile = grads[k].shape[0]
+
+        @pl.loop(0, tile // 8)
+        def _(i):
+            g = grads[k][pl.ds(pl.multiple_of(i * 8, 8), 8), :]
+            rows = pl.ds(pl.multiple_of(starts[k] + step * tile + i * 8, 8), 8)
+            u = direction(g, ratio_ref, rows, c_new[k])
+            acc_ref[k] += lane_fold(u * u)
+
+    @pl.when(step == pl.num_programs(0) - 1)
+    def _():
+        part_ref[...] = jnp.zeros_like(part_ref)
+        for k in range(3):
+            part_ref[k:k + 1, :] = jnp.sum(acc_ref[k], axis=0, keepdims=True)
+        for k, w in enumerate((w0, w1, w2)):
+            part_ref[3 + k:4 + k, :] = jnp.sum(lane_fold(w[...]), axis=0, keepdims=True)
+
+
+def square_sums(hyper_params, grads, all_sums, r_new, c_old, w_sq, row_total):
+    steps = 8
+    whole = lambda v: pl.BlockSpec(v.shape, lambda i: (0, 0))
+    in_specs = (
+        [pl.BlockSpec(memory_space=pltpu.SMEM)]
+        + [pl.BlockSpec((g.shape[0] // steps, g.shape[1]), lambda i: (i, 0)) for g in grads]
+        + [whole(v) for v in (all_sums, r_new, *c_old, *w_sq)]
+    )
+    out_shape = [jax.ShapeDtypeStruct(c.shape, F32) for c in c_old] + [
+        jax.ShapeDtypeStruct((r_new.shape[1], 128), F32),
+        jax.ShapeDtypeStruct((8, 128), F32),
+    ]
+    size = sum(g.size for g in grads)
+    out = pl.pallas_call(
+        functools.partial(square_kernel, row_total, [g.shape[0] for g in grads]),
+        grid=(steps,),
+        in_specs=in_specs,
+        out_specs=[whole(v) for v in out_shape],
+        out_shape=out_shape,
+        scratch_shapes=[pltpu.VMEM((3, 8, 128), F32)],
+        compiler_params=params('arbitrary'),
+        cost_estimate=cost(1000 * size, 4 * size),
+        name='square_sums',
+    )(hyper_params, *grads, all_sums, r_new, *c_old, *w_sq)
+    return out[:3], out[3], out[4]
+
+
+def act_kernel(parts, total, hyper_ref, dya_ref, dyb_ref, *refs):
+    w_refs, refs = refs[:2 * parts], refs[2 * parts:]
+    weights, grads, c_new, (ratio_ref, sum_ref) = refs[:3], refs[3:6], refs[6:9], refs[9:11]
+    out_ref, new, (acc_ref, scale_ref) = refs[11], refs[12:15], refs[15:]
+    step = pl.program_id(0)
+
+    @pl.when(step == 0)
+    def _():
+        mean = jnp.sum(sum_ref[...], axis=1, keepdims=True) / total
+        for k in range(3):
+            rms_u, rms_w = jnp.sqrt(mean[k:k + 1]), jnp.sqrt(mean[3 + k:4 + k])
+            scale = hyper_ref[1] * jnp.maximum(EPS_TWO, rms_w) / jnp.maximum(1.0, rms_u / hyper_ref[2])
+            scale_ref[k] = jnp.broadcast_to(scale, (8, 128))
+
+    def halves(dy_ref, refs):
         done = 0
-        for w_ref in w_refs:
+        for w_ref in refs:
             yield slice(done, done + w_ref.shape[0]), lax.dot_general(
                 dy_ref[...], w_ref[...], NT, preferred_element_type=F32)
             done += w_ref.shape[0]
 
-    @pl.when(pl.program_id(0) >= 0)
-    def _():
-        for cols, part in halves(dya_ref, refs[:parts]):
+    @pl.when(step >= 0)
+    def _():
+        for cols, part in halves(dya_ref, w_refs[:parts]):
             acc_ref[:, cols] = part
 
-    @pl.when(pl.program_id(0) < pl.num_programs(0))
-    def _():
-        for cols, part in halves(dyb_ref, refs[parts:2 * parts]):
+    @pl.when(step < pl.num_programs(0))
+    def _():
+        for cols, part in halves(dyb_ref, w_refs[parts:]):
             out_ref[:, cols] = (acc_ref[:, cols] + part).astype(BF16)
 
-
-def act_grad(dya, dyb, wa, wb):
+    start = 0
+    for k in range(3):
+        tile, n = weights[k].shape
+
+        @pl.loop(0, tile // 8)
+        def _(i):
+            slab = pl.ds(pl.multiple_of(i * 8, 8), 8)
+            rows = pl.ds(pl.multiple_of(start + step * tile + i * 8, 8), 8)
+            u = direction(grads[k][slab, :], ratio_ref, rows, c_new[k])
+            scale = jnp.concatenate([scale_ref[k]] * (n // 128), axis=1)
+            new[k][slab, :] = weights[k][slab, :] - scale * u
+
+        start += tile * pl.num_programs(0)
+
+
+def act_and_update(hyper_params, dya, dyb, wa, wb, weights, grads, c_new, ratio, sums, total):
     tile = 512
     tokens, n = dya.shape
+    steps = tokens // tile
     m = sum(w.shape[0] for w in wa)
     dy_spec = pl.BlockSpec((tile, n), lambda i: (i, 0))
-    w_specs = [pl.BlockSpec(w.shape, lambda i: (0, 0), pipeline_mode=pl.Buffered(1)) for w in (*wa, *wb)]
-    return pl.pallas_call(
-        functools.partial(act_kernel, len(wa)),
-        grid=(tokens // tile,),
-        in_specs=[dy_spec, dy_spec, *w_specs],
-        out_specs=pl.BlockSpec((tile, m), lambda i: (i, 0)),
-        out_shape=jax.ShapeDtypeStruct((tokens, m), BF16),
-        scratch_shapes=[pltpu.VMEM((tile, m), F32)],
+    fixed = lambda v: pl.BlockSpec(v.shape, lambda i: (0, 0), pipeline_mode=pl.Buffered(1))
+    rows = lambda v: pl.BlockSpec((v.shape[0] // steps, v.shape[1]), lambda i: (i, 0))
+    size = sum(w.size for w in weights)
+    out = pl.pallas_call(
+        functools.partial(act_kernel, len(wa), total),
+        grid=(steps,),
+        in_specs=[pl.BlockSpec(memory_space=pltpu.SMEM), dy_spec, dy_spec]
+        + [fixed(w) for w in (*wa, *wb)]
+        + [rows(v) for v in (*weights, *grads)]
+        + [fixed(v) for v in (*c_new, ratio, sums)],
+        out_specs=[pl.BlockSpec((tile, m), lambda i: (i, 0))] + [rows(w) for w in weights],
+        out_shape=[jax.ShapeDtypeStruct((tokens, m), BF16)] + [jax.ShapeDtypeStruct(w.shape, F32) for w in weights],
+        scratch_shapes=[pltpu.VMEM((tile, m), F32), pltpu.VMEM((3, 8, 128), F32)],
         compiler_params=params('arbitrary'),
-        cost_estimate=cost(4 * tokens * m * n, 4 * tokens * n + 4 * m * n + 2 * tokens * m),
-        name='act_grad',
-    )(dya, dyb, *wa, *wb)
-
-
-def lanes(values):
-    index = lax.iota(jnp.int32, 128)
-    return sum(jnp.where(index == k, v, 0.0) for k, v in enumerate(values))
+        cost_estimate=cost(4 * tokens * m * n, 4 * tokens * n + 4 * m * n + 2 * tokens * m + 12 * size),
+        name='act_and_update',
+    )(hyper_params, dya, dyb, *wa, *wb, *weights, *grads, *c_new, ratio, sums)
+    return out[0], out[1:]
 
 
 def swap_col(v):
@@ -303,41 +412,35 @@
 
         (g_gate, row_gate, col_gate), (g_up, row_up, col_up) = weight_grads(x_norm, [dy_gate, dy_up], 512)
         ((g_down, row_down, col_down),) = weight_grads(x_act, [dy_down], 256)
-        row_all = jnp.concatenate([row_gate, row_up, row_down])
+        row_all = jnp.concatenate([row_gate, row_up, row_down], axis=1)
         row_peer = swap_col(row_all)
         o_down_b = swap_col(b_down_b)
         sent0, sent1, own0, own1, w_sq_gate, w_sq_up = norm_partial(1 - col, dy_gate, dy_up, w_gate, w_up)
         got0 = swap_col(sent0)
 
-        sizes_r = [r_gate.shape[0], r_up.shape[0], r_down.shape[0]]
-        sizes_c = [c_gate.shape[0], c_up.shape[0], c_down.shape[0]]
-        totals = [(sizes_r[k] * row_size, sizes_c[k] * col_size) for k in range(3)]
-        row_all = row_all + row_peer
-        row_sums = jnp.split(row_all, [sizes_r[0], sizes_r[0] + sizes_r[1]])
-        r_old = [r_gate, r_up, r_down]
-        c_old = [c_gate, c_up, c_down]
-        r_new = [beta_two * r_old[k] + (1.0 - beta_two) * (row_sums[k] / totals[k][1]) for k in range(3)]
-        r_part = lanes([jnp.sum(r) for r in r_new])
-        col_all = sum_row(jnp.concatenate([col_gate, col_up, col_down, r_part]), row_size)
-        offs = [0, sizes_c[0], sizes_c[0] + sizes_c[1], sum(sizes_c)]
-        c_new = [
-            beta_two * c_old[k] + (1.0 - beta_two) * (col_all[offs[k]:offs[k + 1]] / totals[k][0]) for k in range(3)
-        ]
-        r_mean = [col_all[offs[3] + k:offs[3] + k + 1] / totals[k][0] for k in range(3)]
+        got1 = swap_col(sent1)
+
+        sizes = [r_gate.shape[0], r_up.shape[0], r_down.shape[0]]
+        bounds = [0, sizes[0], sizes[0] + sizes[1], sum(sizes)]
+        row_total = [v * row_size for v in sizes]
+        col_total = [v.shape[0] * col_size for v in (c_gate, c_up, c_down)]
+        index = lax.broadcasted_iota(jnp.int32, row_all.shape, 1)
+        length = jnp.where(index < bounds[1], col_total[0], jnp.where(index < bounds[2], col_total[1], col_total[2]))
+        r_old = jnp.concatenate([r_gate, r_up, r_down])[None]
+        r_new = beta_two * r_old + (1.0 - beta_two) * ((row_all + row_peer) / length.astype(F32))
+        r_part = [lane_fold(r_new[:, bounds[k]:bounds[k + 1]]) for k in range(3)]
+        all_sums = sum_row(jnp.concatenate([col_gate, col_up, col_down, *r_part], axis=1), row_size)
         grads = [g_gate, g_up, g_down]
-        updates = [grads[k] * lax.rsqrt((r_new[k] / r_mean[k])[:, None] * c_new[k][None, :]) for k in range(3)]
-        scalars = lanes([jnp.sum(u * u) for u in updates] + [w_sq_gate, w_sq_up, w_sq_down])
-        scalars = sum_row(scalars, row_size)
-        scalars_peer = swap_col(scalars)
-        got1 = swap_col(sent1)
-        dx_act = act_grad(dy_down, dy_down_other, [b_down_a, b_down_b], [o_down_a, o_down_b])
-        scalars = scalars + scalars_peer
-        size = float(totals[0][0] * totals[0][1])
-        rms_u = jnp.sqrt(scalars[:3] / size)
-        rms_w = jnp.sqrt(scalars[3:6] / size)
-        scale = hyper_params[1:2] * jnp.maximum(EPS_TWO, rms_w) / jnp.maximum(1.0, rms_u / hyper_params[2:3])
-        weights = [w_gate, w_up, w_down]
-        new = [weights[k] - scale[k:k + 1, None] * updates[k] for k in range(3)]
+        c_new, ratio, sums = square_sums(
+            hyper_params, grads, all_sums, r_new, [c_gate[None], c_up[None], c_down[None]],
+            [w_sq_gate, w_sq_up, w_sq_down], row_total)
+        sums = sum_row(sums, row_size)
+        sums_peer = swap_col(sums)
+        dx_act, new = act_and_update(
+            hyper_params, dy_down, dy_down_other, [b_down_a, b_down_b], [o_down_a, o_down_b],
+            [w_gate, w_up, w_down], grads, c_new, ratio, sums + sums_peer, float(row_total[0] * col_total[0]))
+        r_new = [r_new[0, bounds[k]:bounds[k + 1]] for k in range(3)]
+        c_new = [c[0] for c in c_new]
 
         mine0 = (own0 + got0).astype(BF16)
         theirs0 = swap_col(mine0)

time: 590 us -> 409 us (0.69)
  waiting for transfers between devices: 244 us -> 109 us
  other arithmetic: 92.3 us -> 10.5 us
  Pallas kernels: 211 us -> 245 us
    ppermute x9, waiting for transfers between devices: 238 us -> 101 us  [swap_col(): return lax.ppermute(v, 'col', [(0, 1), (1, 0)])]
    sub x2 -> x0, other arithmetic: 38 us -> none  [body(): new = [weights[k] - scale[k:k + 1, None] * updates[k] for k in range(3)]]
    pallas_call x1 -> x2, Pallas kernels: 53.1 us -> 87 us  [the longest x1 68.4 us: act_and_update(): pl.pallas_call(functools.partial(act_kernel, len(wa), total), grid=(steps...]
    reduce_sum x11 -> x0, other arithmetic: 29.3 us -> none  [the longest x3 20.6 us: body(): jnp.sum(u * u)]
    add x6, other arithmetic: 8.42 us -> 1.47 us  [sum_row(): v = v + lax.ppermute(v, 'row', [(i, i ^ step) for i in range(row_size)])]
    add x6 -> x2, other arithmetic: 7.07 us -> 0.65 us  [the longest x1 0.6 us: body(): sums + sums_peer]
  transfers between devices with their start and end apart: 16 -> 16, of which waited for: 9 -> 8; matrix products, arithmetic and copies ran while one was open for 16% -> 4% of each run, Pallas kernels for 27% -> 43%
where the time goes in v4:
time: 409 us; the launch traced here: 407 us
  Pallas kernels  245 us (60%)
  waiting for transfers between devices  109 us (27%)
  starting transfers between devices  20.2 us (5%)
  between operations  14.2 us (3%)
  other arithmetic  10.5 us (3%)
  local copies, waits for them, and re-layouts  8.13 us (2%)
    ppermute x9, waiting for transfers between devices, swap_col(): return lax.ppermute(v, 'col', [(0, 1), (1, 0)])  101 us
    pallas_call x2, Pallas kernels, weight_grads(): pl.pallas_call(functools.partial(grad_kernel, count, steps), grid=(steps...  90.9 us
    pallas_call x1, Pallas kernels, act_and_update(): pl.pallas_call(functools.partial(act_kernel, len(wa), total), grid=(steps...  68.4 us
    pallas_call x1, Pallas kernels, norm_partial(): pl.pallas_call(functools.partial(norm_kernel, chunk), grid_spec=pltpu.Pre...  58.9 us
    pallas_call x1, Pallas kernels, square_sums(): pl.pallas_call(functools.partial(square_kernel, row_total, [g.shape[0] fo...  18.5 us
    ppermute x9, starting transfers between devices, swap_col(): return lax.ppermute(v, 'col', [(0, 1), (1, 0)])  13.9 us
    pallas_call x1, Pallas kernels, cast_weight(): pl.pallas_call(functools.partial(cast_kernel, first), grid=(rows // tile,...  8.51 us
    ppermute x6, waiting for transfers between devices, sum_row(): v = v + lax.ppermute(v, 'row', [(i, i ^ step) for i in range(row_size)])  8.25 us
  transfers between devices with their start and end apart: 16, of which 8 were waited for; matrix products, arithmetic and copies ran while one was open for 4% of the time, Pallas kernels for 43%

profile of v4, /device:TPU:0, one launch (start us, length us, event | category | flops | bytes accessed | tf_op | source)
XLA Modules:
  0.0 407.3 jit_solution(17362351365448253804)
XLA Ops:
  7.2 1.7 constant_dynamic-slice_fusion
  9.0 3.3 collective-permute-start
  12.3 45.6 %collective-permute-done = bf16[512,2048]{1,0:T(8,128)(2,1)S(1)} collective-permute-done((bf16[512,2048]{1,0:T(8,128)(2,1)S(1)}, bf16[512,2048]{1,0:T(8,128)(2,1)S(1)}, u32[]{:S(2)}, u32[]{:S(2)}) %collective-permute-start) | collective-permute-done | bytes 2097184 | tf_op jit(solution)/shard_map/ppermute | solution.py:379
  57.9 1.3 copy-done
  59.3 8.5 %cast_weight.1 = (bf16[768,2048]{1,0:T(8,128)(2,1)}, bf16[512,2048]{1,0:T(8,128)(2,1)}, f32[8,2048]{1,0:T(8,128)}) custom-call(f32[1280,2048]{1,0:T(8,128)} %refs_6_.1), custom_call_target="tpu_custom_call" | custom-call | flops 2621440000 | bytes 15728640 | tf_op jit(solution)/shard_map/cast_weight/pallas_call | solution.py:53
  67.8 1.6 collective-permute-start.1
  69.4 58.9 %norm_partial.1 = (f32[1024,512]{1,0:T(8,128)}, f32[1024,512]{1,0:T(8,128)}, f32[1024,512]{1,0:T(8,128)}, f32[1024,512]{1,0:T(8,128)}, f32[8,1024]{1,0:T(8,128)}, /*index=5*/f32[8,1024]{1,0:T(8,128)}) custom-call(s32[1]{0:T(128)} %bitcast.6.start_ref, bf16[4096,5120]{1,0:T(8,128)(2,1)} %dyg_ref.1, bf16[4096,5120]{1,0:T(8,128)(2,1)} %dyu_ref.1, ...), custom_call_target="tpu_custom_call" | custom-call | flops 42949672960 | bytes 113246208 | tf_op jit(solution)/shard_map/norm_partial/pallas_call | solution.py:207
  128.3 1.9 collective-permute-start.11
  130.4 57.6 %weight_grads.2 = (f32[512,5120]{1,0:T(8,128)}, f32[1,512]{1,0:T(1,128)}, f32[1,5120]{1,0:T(1,128)}, f32[512,5120]{1,0:T(8,128)}, f32[1,512]{1,0:T(1,128)}, /*index=5*/f32[1,5120]{1,0:T(1,128)}) custom-call(bf16[4096,512]{1,0:T(8,128)(2,1)} %x_ref.2, bf16[4096,5120]{1,0:T(8,128)(2,1)} %dyg_ref.1, bf16[4096,5120]{1,0:T(8,128)(2,1)} %dyu_ref.1), custom_call_target="tpu_custom_call" | custom-call | flops 42949672960 | bytes 113246208 | tf_op jit(solution)/shard_map/weight_grads/pallas_call | solution.py:128
  189.3 33.3 %weight_grads.3 = (f32[1280,2048]{1,0:T(8,128)}, f32[1,1280]{1,0:T(1,128)}, f32[1,2048]{1,0:T(1,128)}) custom-call(bf16[4096,1280]{1,0:T(8,128)(2,1)} %x_ref.3, bf16[4096,2048]{1,0:T(8,128)(2,1)} %dya_ref.1), custom_call_target="tpu_custom_call" | custom-call | flops 21474836480 | bytes 37748736 | tf_op jit(solution)/shard_map/weight_grads/pallas_call | solution.py:128
  223.4 1.7 collective-permute-start.3
  225.1 0.7 constant_dynamic-update-slice_fusion.6
  225.9 1.3 collective-permute-done.3
  227.3 1.2 collective-permute-done.4
  228.6 1.7 collective-permute-start.5
  230.3 2.5 collective-permute-done.5
  232.8 1.7 collective-permute-start.6
  234.5 1.4 collective-permute-start.2
  235.9 1.1 collective-permute-done.6
  237.6 1.9 add_convert_fusion.1
  239.5 1.6 collective-permute-start.13
  241.2 18.5 %square_sums.1 = (f32[1,5120]{1,0:T(1,128)}, f32[1,5120]{1,0:T(1,128)}, f32[1,2048]{1,0:T(1,128)}, f32[2304,128]{1,0:T(8,128)}, f32[8,128]{1,0:T(8,128)}) custom-call(f32[3]{0:T(128)} %hyper_ref.3, f32[512,5120]{1,0:T(8,128)} %get-tuple-element.40.g0.refs_7_, f32[512,5120]{1,0:T(8,128)} %get-tuple-element.41.g1.refs_8_, ...), custom_call_target="tpu_custom_call" | custom-call | flops 7864320000 | bytes 31457280 | tf_op jit(solution)/shard_map/square_sums/pallas_call | solution.py:292
  259.8 1.4 collective-permute-done.7
  261.9 1.5 collective-permute-start.8
  263.3 2.1 collective-permute-done.8
  265.5 1.4 collective-permute-start.9
  266.9 2.0 add_convert_fusion
  270.2 1.4 collective-permute-start.10
  272.2 53.8 %collective-permute-done.10 = f32[8,128]{1,0:T(8,128)S(1)} collective-permute-done((f32[8,128]{1,0:T(8,128)S(1)}, f32[8,128]{1,0:T(8,128)S(1)}, u32[]{:S(2)}, u32[]{:S(2)}) %collective-permute-start.10) | collective-permute-done | bytes 4128 | tf_op jit(solution)/shard_map/ppermute | solution.py:379
  326.6 4.4 %maximum_select_fusion = bf16[4096,512]{1,0:T(8,128)(2,1)} fusion(bf16[1024,512]{1,0:T(8,128)(2,1)} %collective-permute-done.13, bf16[1024,512]{1,0:T(8,128)(2,1)S(1)} %add_convert_fusion, bf16[1024,512]{1,0:T(8,128)(2,1)S(1)} %add_convert_fusion.1, pred[]{:T(512)S(6)} %eq.3), kind=kLoop, calls=%fused_computation | loop fusion | flops 35651584 | bytes 7340033 | tf_op jit(solution)/shard_map/jit(_where)/select_n | solution.py:449
  331.0 1.0 constant_dynamic-update-slice_fusion.9
  332.1 68.4 %act_and_update.1 = (bf16[4096,1280]{1,0:T(8,128)(2,1)}, f32[512,5120]{1,0:T(8,128)}, f32[512,5120]{1,0:T(8,128)}, f32[1280,2048]{1,0:T(8,128)}) custom-call(f32[3]{0:T(128)} %hyper_ref.3, bf16[4096,2048]{1,0:T(8,128)(2,1)} %dya_ref.1, bf16[4096,2048]{1,0:T(8,128)(2,1)} %all-gather.2.cloned.1.call-done.dyb_ref, bf16[768,2048]{1,0:T(8,128)(2,1)} %get-tuple-element.38.refs_0_, ...), custom_call_target="tpu_custom_call" | custom-call | flops 42949672960 | bytes 148897792 | tf_op jit(solution)/shard_map/act_and_update/pallas_call | solution.py:361
  (54 shorter events, 6.5 us)
Async XLA Ops:
  7.2 324.9 %all-gather.2.cloned.1.call-start = ((), (), s32[]{:S(2)}) async-start(), calls=%async_computation | async-start | bytes 18874368 | tf_op jit(solution)/shard_map/all_gather | solution.py:409
  9.0 48.9 %collective-permute-start = (bf16[512,2048]{1,0:T(8,128)(2,1)S(1)}, bf16[512,2048]{1,0:T(8,128)(2,1)S(1)}, u32[]{:S(2)}, u32[]{:S(2)}) collective-permute-start(bf16[512,2048]{1,0:T(8,128)(2,1)S(1)} %constant_dynamic-slice_fusion), channel_id=1, source_target_pairs={{0,8},{8,0},{1,9},{9,1},{2,10},{10,2},{3,11},{11,3},{4,12},{12,4},... | collective-permute-start | bytes 6291464 | tf_op jit(solution)/shard_map/ppermute | solution.py:379
  57.9 1.3 copy-start
  67.8 264.3 %collective-permute-start.1 = (bf16[768,2048]{1,0:T(8,128)(2,1)}, bf16[768,2048]{1,0:T(8,128)(2,1)}, u32[]{:S(2)}, u32[]{:S(2)}) collective-permute-start(bf16[768,2048]{1,0:T(8,128)(2,1)} %get-tuple-element.38.refs_0_), channel_id=1, source_target_pairs={{0,8},{8,0},{1,9},{9,1},{2,10},{10,2},{3,11},{11,3},{4,12},{12,4},... | collective-permute-start | bytes 9437192 | tf_op jit(solution)/shard_map/ppermute | solution.py:379
  128.3 109.3 %collective-permute-start.11 = (f32[1024,512]{1,0:T(8,128)}, f32[1024,512]{1,0:T(8,128)}, u32[]{:S(2)}, u32[]{:S(2)}) collective-permute-start(f32[1024,512]{1,0:T(8,128)} %get-tuple-element.61), channel_id=1, source_target_pairs={{0,8},{8,0},{1,9},{9,1},{2,10},{10,2},{3,11},{11,3},{4,12},{12,4},... | collective-permute-start | bytes 6291464 | tf_op jit(solution)/shard_map/ppermute | solution.py:379
  130.2 136.7 %collective-permute-start.12 = (f32[1024,512]{1,0:T(8,128)}, f32[1024,512]{1,0:T(8,128)}, u32[]{:S(2)}, u32[]{:S(2)}) collective-permute-start(f32[1024,512]{1,0:T(8,128)} %get-tuple-element.63), channel_id=1, source_target_pairs={{0,8},{8,0},{1,9},{9,1},{2,10},{10,2},{3,11},{11,3},{4,12},{12,4},... | collective-permute-start | bytes 6291464 | tf_op jit(solution)/shard_map/ppermute | solution.py:379
  189.3 35.8 %copy-start.6 = (f32[1,5120]{1,0:T(1,128)S(1)}, f32[1,5120]{1,0:T(1,128)}, u32[]{:S(2)}) copy-start(f32[1,5120]{1,0:T(1,128)} %get-tuple-element.43) | copy-start | bytes 61444
  189.3 35.8 %copy-start.5 = (f32[1,5120]{1,0:T(1,128)S(1)}, f32[1,5120]{1,0:T(1,128)}, u32[]{:S(2)}) copy-start(f32[1,5120]{1,0:T(1,128)} %get-tuple-element.44) | copy-start | bytes 61444
  189.3 36.5 %copy-start.7 = (f32[1280]{0:T(1024)S(1)}, f32[1280]{0:T(1024)}, u32[]{:S(2)}) copy-start(f32[1280]{0:T(1024)} %param.27) | copy-start | bytes 15364
  189.3 36.5 %copy-start.8 = (f32[3]{0:T(128)S(1)}, f32[3]{0:T(128)}, u32[]{:S(2)}) copy-start(f32[3]{0:T(128)} %hyper_ref.3) | copy-start | bytes 40
  189.3 37.8 %copy-start.9 = (f32[512]{0:T(512)S(1)}, f32[512]{0:T(512)}, u32[]{:S(2)}) copy-start(f32[512]{0:T(512)} %param.25) | copy-start | bytes 6148
  189.3 37.8 %copy-start.10 = (f32[512]{0:T(512)S(1)}, f32[512]{0:T(512)}, u32[]{:S(2)}) copy-start(f32[512]{0:T(512)} %param.23) | copy-start | bytes 6148
  189.3 48.3 %copy-start.2 = (f32[1024,512]{1,0:T(8,128)S(1)}, f32[1024,512]{1,0:T(8,128)}, u32[]{:S(2)}) copy-start(f32[1024,512]{1,0:T(8,128)} %get-tuple-element.60) | copy-start | bytes 6291460
  223.4 3.7 collective-permute-start.3
  227.2 14.0 %copy-start.3 = (f32[1,2304]{1,0:T(1,128)}, f32[1,2304]{1,0:T(1,128)S(1)}, u32[]{:S(2)}) copy-start(f32[1,2304]{1,0:T(1,128)S(1)} %fusion.3.r_ref) | copy-start | bytes 27652
  227.3 1.3 collective-permute-start.4
  228.6 4.1 %collective-permute-start.5 = (f32[1,12672]{1,0:T(1,128)S(1)}, f32[1,12672]{1,0:T(1,128)S(1)}, u32[]{:S(2)}, u32[]{:S(2)}) collective-permute-start(f32[1,12672]{1,0:T(1,128)S(1)} %add.107), channel_id=1, source_target_pairs={{0,2},{1,3},{2,0},{3,1},{4,6},{5,7},{6,4},{7,5},{8,10},{9,11},{10,... | collective-permute-start | bytes 152072 | tf_op jit(solution)/shard_map/ppermute | solution.py:385
  232.8 4.1 %collective-permute-start.6 = (f32[1,12672]{1,0:T(1,128)S(1)}, f32[1,12672]{1,0:T(1,128)S(1)}, u32[]{:S(2)}, u32[]{:S(2)}) collective-permute-start(f32[1,12672]{1,0:T(1,128)S(1)} %add.108), channel_id=1, source_target_pairs={{0,4},{1,5},{2,6},{3,7},{4,0},{5,1},{6,2},{7,3},{8,12},{9,13},{10,... | collective-permute-start | bytes 152072 | tf_op jit(solution)/shard_map/ppermute | solution.py:385
  234.5 97.6 %collective-permute-start.2 = (bf16[512,2048]{1,0:T(8,128)(2,1)}, bf16[512,2048]{1,0:T(8,128)(2,1)}, u32[]{:S(2)}, u32[]{:S(2)}) collective-permute-start(bf16[512,2048]{1,0:T(8,128)(2,1)} %get-tuple-element.39.refs_1_), channel_id=1, source_target_pairs={{0,8},{8,0},{1,9},{9,1},{2,10},{10,2},{3,11},{11,3},{4,12},{12,4},... | collective-permute-start | bytes 6291464 | tf_op jit(solution)/shard_map/ppermute | solution.py:379
  239.5 87.0 %collective-permute-start.13 = (bf16[1024,512]{1,0:T(8,128)(2,1)S(1)}, bf16[1024,512]{1,0:T(8,128)(2,1)}, u32[]{:S(2)}, u32[]{:S(2)}) collective-permute-start(bf16[1024,512]{1,0:T(8,128)(2,1)S(1)} %add_convert_fusion.1), channel_id=1, source_target_pairs={{0,8},{8,0},{1,9},{9,1},{2,10},{10,2},{3,11},{11,3},{4,12},{12,4},... | collective-permute-start | bytes 3145736 | tf_op jit(solution)/shard_map/ppermute | solution.py:379
  241.2 25.7 %copy-start.1 = (f32[1024,512]{1,0:T(8,128)S(1)}, f32[1024,512]{1,0:T(8,128)}, u32[]{:S(2)}) copy-start(f32[1024,512]{1,0:T(8,128)} %get-tuple-element.62) | copy-start | bytes 6291460
  259.7 9.8 %copy-start.4 = (f32[1,2304]{1,0:T(1,128)S(1)}, f32[1,2304]{1,0:T(1,128)}, u32[]{:S(2)}) copy-start(f32[1,2304]{1,0:T(1,128)} %copy-done.3) | copy-start | bytes 27652
  259.8 1.4 collective-permute-start.7
  261.9 3.6 collective-permute-start.8
  265.5 4.7 %collective-permute-start.9 = (f32[8,128]{1,0:T(8,128)S(1)}, f32[8,128]{1,0:T(8,128)S(1)}, u32[]{:S(2)}, u32[]{:S(2)}) collective-permute-start(f32[8,128]{1,0:T(8,128)S(1)} %add.111), channel_id=1, source_target_pairs={{0,4},{1,5},{2,6},{3,7},{4,0},{5,1},{6,2},{7,3},{8,12},{9,13},{10,... | collective-permute-start | bytes 12296 | tf_op jit(solution)/shard_map/ppermute | solution.py:385
  268.9 62.1 %collective-permute-start.14 = (bf16[1024,512]{1,0:T(8,128)(2,1)S(1)}, bf16[1024,512]{1,0:T(8,128)(2,1)S(1)}, u32[]{:S(2)}, u32[]{:S(2)}) collective-permute-start(bf16[1024,512]{1,0:T(8,128)(2,1)S(1)} %add_convert_fusion), channel_id=1, source_target_pairs={{0,8},{8,0},{1,9},{9,1},{2,10},{10,2},{3,11},{11,3},{4,12},{12,4},... | collective-permute-start | bytes 3145736 | tf_op jit(solution)/shard_map/ppermute | solution.py:379
  270.2 55.8 %collective-permute-start.10 = (f32[8,128]{1,0:T(8,128)S(1)}, f32[8,128]{1,0:T(8,128)S(1)}, u32[]{:S(2)}, u32[]{:S(2)}) collective-permute-start(f32[8,128]{1,0:T(8,128)S(1)} %add.112), channel_id=1, source_target_pairs={{0,8},{8,0},{1,9},{9,1},{2,10},{10,2},{3,11},{11,3},{4,12},{12,4},... | collective-permute-start | bytes 12296 | tf_op jit(solution)/shard_map/ppermute | solution.py:379
Sparse Core Ops, SparseCore 0:
  59.4 87.2 all-gather.1

commit v5 on v4

--- a/solution.py
+++ b/solution.py
@@ -228,7 +228,10 @@
 
 
 def lane_fold(v):
-    return functools.reduce(lambda p, q: p + q, [v[:, k:k + 128] for k in range(0, v.shape[1], 128)])
+    parts = [v[:, k:k + 128] for k in range(0, v.shape[1], 128)]
+    while len(parts) > 1:
+        parts = [p + q for p, q in zip(parts[::2], parts[1::2])] + parts[len(parts) & ~1:]
+    return parts[0]
 
 
 def direction(g, r_ref, rows, c_ref):
@@ -260,7 +263,7 @@
     for k in range(3):
         tile = grads[k].shape[0]
 
-        @pl.loop(0, tile // 8)
+        @pl.loop(0, tile // 8, unroll=4)
         def _(i):
             g = grads[k][pl.ds(pl.multiple_of(i * 8, 8), 8), :]
             rows = pl.ds(pl.multiple_of(starts[k] + step * tile + i * 8, 8), 8)
@@ -338,7 +341,7 @@
     for k in range(3):
         tile, n = weights[k].shape
 
-        @pl.loop(0, tile // 8)
+        @pl.loop(0, tile // 8, unroll=4)
         def _(i):
             slab = pl.ds(pl.multiple_of(i * 8, 8), 8)
             rows = pl.ds(pl.multiple_of(start + step * tile + i * 8, 8), 8)
@@ -411,7 +414,7 @@
         o_down_a = swap_col(b_down_a)
 
         (g_gate, row_gate, col_gate), (g_up, row_up, col_up) = weight_grads(x_norm, [dy_gate, dy_up], 512)
-        ((g_down, row_down, col_down),) = weight_grads(x_act, [dy_down], 256)
+        ((g_down, row_down, col_down),) = weight_grads(x_act, [dy_down], 512)
         row_all = jnp.concatenate([row_gate, row_up, row_down], axis=1)
         row_peer = swap_col(row_all)
         o_down_b = swap_col(b_down_b)

time: 409 us -> 406 us (level)
  Pallas kernels: 245 us -> 240 us
where the time goes in v5:
time: 406 us; the launch traced here: 405 us
  Pallas kernels  240 us (59%)
  waiting for transfers between devices  112 us (28%)
  starting transfers between devices  20.5 us (5%)
  between operations  14.2 us (3%)
  other arithmetic  10.5 us (3%)
  local copies, waits for them, and re-layouts  8.13 us (2%)
    ppermute x9, waiting for transfers between devices, swap_col(): return lax.ppermute(v, 'col', [(0, 1), (1, 0)])  104 us
    pallas_call x2, Pallas kernels, weight_grads(): pl.pallas_call(functools.partial(grad_kernel, count, steps), grid=(steps...  91.1 us
    pallas_call x1, Pallas kernels, act_and_update(): pl.pallas_call(functools.partial(act_kernel, len(wa), total), grid=(steps...  66.2 us
    pallas_call x1, Pallas kernels, norm_partial(): pl.pallas_call(functools.partial(norm_kernel, chunk), grid_spec=pltpu.Pre...  58.9 us
    pallas_call x1, Pallas kernels, square_sums(): pl.pallas_call(functools.partial(square_kernel, row_total, [g.shape[0] fo...  15.5 us
    ppermute x9, starting transfers between devices, swap_col(): return lax.ppermute(v, 'col', [(0, 1), (1, 0)])  13.9 us
    pallas_call x1, Pallas kernels, cast_weight(): pl.pallas_call(functools.partial(cast_kernel, first), grid=(rows // tile,...  8.51 us
  transfers between devices with their start and end apart: 16, of which 8 were waited for; matrix products, arithmetic and copies ran while one was open for 4% of the time, Pallas kernels for 43%

profile of v5, /device:TPU:0, one launch (start us, length us, event | category | flops | bytes accessed | tf_op | source)
XLA Modules:
  0.0 405.3 jit_solution(13655537293403124554)
XLA Ops:
  7.2 1.7 constant_dynamic-slice_fusion
  9.0 3.3 collective-permute-start
  12.3 45.6 %collective-permute-done = bf16[512,2048]{1,0:T(8,128)(2,1)S(1)} collective-permute-done((bf16[512,2048]{1,0:T(8,128)(2,1)S(1)}, bf16[512,2048]{1,0:T(8,128)(2,1)S(1)}, u32[]{:S(2)}, u32[]{:S(2)}) %collective-permute-start) | collective-permute-done | bytes 2097184 | tf_op jit(solution)/shard_map/ppermute | solution.py:382
  57.9 1.3 copy-done
  59.3 8.5 %cast_weight.1 = (bf16[768,2048]{1,0:T(8,128)(2,1)}, bf16[512,2048]{1,0:T(8,128)(2,1)}, f32[8,2048]{1,0:T(8,128)}) custom-call(f32[1280,2048]{1,0:T(8,128)} %refs_6_.1), custom_call_target="tpu_custom_call" | custom-call | flops 2621440000 | bytes 15728640 | tf_op jit(solution)/shard_map/cast_weight/pallas_call | solution.py:53
  67.8 1.6 collective-permute-start.1
  69.4 58.9 %norm_partial.1 = (f32[1024,512]{1,0:T(8,128)}, f32[1024,512]{1,0:T(8,128)}, f32[1024,512]{1,0:T(8,128)}, f32[1024,512]{1,0:T(8,128)}, f32[8,1024]{1,0:T(8,128)}, /*index=5*/f32[8,1024]{1,0:T(8,128)}) custom-call(s32[1]{0:T(128)} %bitcast.6.start_ref, bf16[4096,5120]{1,0:T(8,128)(2,1)} %dyg_ref.1, bf16[4096,5120]{1,0:T(8,128)(2,1)} %dyu_ref.1, ...), custom_call_target="tpu_custom_call" | custom-call | flops 42949672960 | bytes 113246208 | tf_op jit(solution)/shard_map/norm_partial/pallas_call | solution.py:207
  128.3 1.9 collective-permute-start.11
  130.4 57.6 %weight_grads.2 = (f32[512,5120]{1,0:T(8,128)}, f32[1,512]{1,0:T(1,128)}, f32[1,5120]{1,0:T(1,128)}, f32[512,5120]{1,0:T(8,128)}, f32[1,512]{1,0:T(1,128)}, /*index=5*/f32[1,5120]{1,0:T(1,128)}) custom-call(bf16[4096,512]{1,0:T(8,128)(2,1)} %x_ref.2, bf16[4096,5120]{1,0:T(8,128)(2,1)} %dyg_ref.1, bf16[4096,5120]{1,0:T(8,128)(2,1)} %dyu_ref.1), custom_call_target="tpu_custom_call" | custom-call | flops 42949672960 | bytes 113246208 | tf_op jit(solution)/shard_map/weight_grads/pallas_call | solution.py:128
  189.3 33.5 %weight_grads.3 = (f32[1280,2048]{1,0:T(8,128)}, f32[1,1280]{1,0:T(1,128)}, f32[1,2048]{1,0:T(1,128)}) custom-call(bf16[4096,1280]{1,0:T(8,128)(2,1)} %x_ref.3, bf16[4096,2048]{1,0:T(8,128)(2,1)} %dya_ref.1), custom_call_target="tpu_custom_call" | custom-call | flops 21474836480 | bytes 37748736 | tf_op jit(solution)/shard_map/weight_grads/pallas_call | solution.py:128
  223.5 1.7 collective-permute-start.3
  225.3 0.7 constant_dynamic-update-slice_fusion.6
  226.0 1.2 collective-permute-done.3
  227.4 1.2 collective-permute-done.4
  228.7 1.8 collective-permute-start.5
  230.4 2.4 collective-permute-done.5
  232.9 1.8 collective-permute-start.6
  234.6 1.4 collective-permute-start.2
  236.0 1.0 collective-permute-done.6
  237.7 1.9 add_convert_fusion.1
  239.6 1.7 collective-permute-start.13
  241.4 15.5 %square_sums.1 = (f32[1,5120]{1,0:T(1,128)}, f32[1,5120]{1,0:T(1,128)}, f32[1,2048]{1,0:T(1,128)}, f32[2304,128]{1,0:T(8,128)}, f32[8,128]{1,0:T(8,128)}) custom-call(f32[3]{0:T(128)} %hyper_ref.3, f32[512,5120]{1,0:T(8,128)} %get-tuple-element.40.g0.refs_7_, f32[512,5120]{1,0:T(8,128)} %get-tuple-element.41.g1.refs_8_, ...), custom_call_target="tpu_custom_call" | custom-call | flops 7864320000 | bytes 31457280 | tf_op jit(solution)/shard_map/square_sums/pallas_call | solution.py:295
  256.9 1.4 collective-permute-done.7
  258.9 1.5 collective-permute-start.8
  260.4 2.1 collective-permute-done.8
  262.6 1.4 collective-permute-start.9
  264.0 2.0 add_convert_fusion
  267.2 1.4 collective-permute-start.10
  269.3 56.8 %collective-permute-done.10 = f32[8,128]{1,0:T(8,128)S(1)} collective-permute-done((f32[8,128]{1,0:T(8,128)S(1)}, f32[8,128]{1,0:T(8,128)S(1)}, u32[]{:S(2)}, u32[]{:S(2)}) %collective-permute-start.10) | collective-permute-done | bytes 4128 | tf_op jit(solution)/shard_map/ppermute | solution.py:382
  326.7 4.4 %maximum_select_fusion = bf16[4096,512]{1,0:T(8,128)(2,1)} fusion(bf16[1024,512]{1,0:T(8,128)(2,1)} %collective-permute-done.13, bf16[1024,512]{1,0:T(8,128)(2,1)S(1)} %add_convert_fusion, bf16[1024,512]{1,0:T(8,128)(2,1)S(1)} %add_convert_fusion.1, pred[]{:T(512)S(6)} %eq.3), kind=kLoop, calls=%fused_computation | loop fusion | flops 35651584 | bytes 7340033 | tf_op jit(solution)/shard_map/jit(_where)/select_n | solution.py:452
  331.2 1.0 constant_dynamic-update-slice_fusion.9
  332.2 66.2 %act_and_update.1 = (bf16[4096,1280]{1,0:T(8,128)(2,1)}, f32[512,5120]{1,0:T(8,128)}, f32[512,5120]{1,0:T(8,128)}, f32[1280,2048]{1,0:T(8,128)}) custom-call(f32[3]{0:T(128)} %hyper_ref.3, bf16[4096,2048]{1,0:T(8,128)(2,1)} %dya_ref.1, bf16[4096,2048]{1,0:T(8,128)(2,1)} %all-gather.2.cloned.1.call-done.dyb_ref, bf16[768,2048]{1,0:T(8,128)(2,1)} %get-tuple-element.38.refs_0_, ...), custom_call_target="tpu_custom_call" | custom-call | flops 42949672960 | bytes 148897792 | tf_op jit(solution)/shard_map/act_and_update/pallas_call | solution.py:364
  (54 shorter events, 6.5 us)
Async XLA Ops:
  7.2 325.0 %all-gather.2.cloned.1.call-start = ((), (), s32[]{:S(2)}) async-start(), calls=%async_computation | async-start | bytes 18874368 | tf_op jit(solution)/shard_map/all_gather | solution.py:412
  9.0 48.9 %collective-permute-start = (bf16[512,2048]{1,0:T(8,128)(2,1)S(1)}, bf16[512,2048]{1,0:T(8,128)(2,1)S(1)}, u32[]{:S(2)}, u32[]{:S(2)}) collective-permute-start(bf16[512,2048]{1,0:T(8,128)(2,1)S(1)} %constant_dynamic-slice_fusion), channel_id=1, source_target_pairs={{0,8},{8,0},{1,9},{9,1},{2,10},{10,2},{3,11},{11,3},{4,12},{12,4},... | collective-permute-start | bytes 6291464 | tf_op jit(solution)/shard_map/ppermute | solution.py:382
  57.9 1.3 copy-start
  67.8 264.4 %collective-permute-start.1 = (bf16[768,2048]{1,0:T(8,128)(2,1)}, bf16[768,2048]{1,0:T(8,128)(2,1)}, u32[]{:S(2)}, u32[]{:S(2)}) collective-permute-start(bf16[768,2048]{1,0:T(8,128)(2,1)} %get-tuple-element.38.refs_0_), channel_id=1, source_target_pairs={{0,8},{8,0},{1,9},{9,1},{2,10},{10,2},{3,11},{11,3},{4,12},{12,4},... | collective-permute-start | bytes 9437192 | tf_op jit(solution)/shard_map/ppermute | solution.py:382
  128.3 109.4 %collective-permute-start.11 = (f32[1024,512]{1,0:T(8,128)}, f32[1024,512]{1,0:T(8,128)}, u32[]{:S(2)}, u32[]{:S(2)}) collective-permute-start(f32[1024,512]{1,0:T(8,128)} %get-tuple-element.61), channel_id=1, source_target_pairs={{0,8},{8,0},{1,9},{9,1},{2,10},{10,2},{3,11},{11,3},{4,12},{12,4},... | collective-permute-start | bytes 6291464 | tf_op jit(solution)/shard_map/ppermute | solution.py:382
  130.2 133.8 %collective-permute-start.12 = (f32[1024,512]{1,0:T(8,128)}, f32[1024,512]{1,0:T(8,128)}, u32[]{:S(2)}, u32[]{:S(2)}) collective-permute-start(f32[1024,512]{1,0:T(8,128)} %get-tuple-element.63), channel_id=1, source_target_pairs={{0,8},{8,0},{1,9},{9,1},{2,10},{10,2},{3,11},{11,3},{4,12},{12,4},... | collective-permute-start | bytes 6291464 | tf_op jit(solution)/shard_map/ppermute | solution.py:382
  189.3 35.9 %copy-start.6 = (f32[1,5120]{1,0:T(1,128)S(1)}, f32[1,5120]{1,0:T(1,128)}, u32[]{:S(2)}) copy-start(f32[1,5120]{1,0:T(1,128)} %get-tuple-element.43) | copy-start | bytes 61444
  189.3 35.9 %copy-start.5 = (f32[1,5120]{1,0:T(1,128)S(1)}, f32[1,5120]{1,0:T(1,128)}, u32[]{:S(2)}) copy-start(f32[1,5120]{1,0:T(1,128)} %get-tuple-element.44) | copy-start | bytes 61444
  189.3 36.7 %copy-start.7 = (f32[1280]{0:T(1024)S(1)}, f32[1280]{0:T(1024)}, u32[]{:S(2)}) copy-start(f32[1280]{0:T(1024)} %param.27) | copy-start | bytes 15364
  189.3 36.7 %copy-start.8 = (f32[3]{0:T(128)S(1)}, f32[3]{0:T(128)}, u32[]{:S(2)}) copy-start(f32[3]{0:T(128)} %hyper_ref.3) | copy-start | bytes 40
  189.3 37.9 %copy-start.9 = (f32[512]{0:T(512)S(1)}, f32[512]{0:T(512)}, u32[]{:S(2)}) copy-start(f32[512]{0:T(512)} %param.25) | copy-start | bytes 6148
  189.3 37.9 %copy-start.10 = (f32[512]{0:T(512)S(1)}, f32[512]{0:T(512)}, u32[]{:S(2)}) copy-start(f32[512]{0:T(512)} %param.23) | copy-start | bytes 6148
  189.3 48.3 %copy-start.2 = (f32[1024,512]{1,0:T(8,128)S(1)}, f32[1024,512]{1,0:T(8,128)}, u32[]{:S(2)}) copy-start(f32[1024,512]{1,0:T(8,128)} %get-tuple-element.60) | copy-start | bytes 6291460
  223.5 3.7 collective-permute-start.3
  227.3 14.1 %copy-start.3 = (f32[1,2304]{1,0:T(1,128)}, f32[1,2304]{1,0:T(1,128)S(1)}, u32[]{:S(2)}) copy-start(f32[1,2304]{1,0:T(1,128)S(1)} %fusion.3.r_ref) | copy-start | bytes 27652
  227.3 1.3 collective-permute-start.4
  228.7 4.1 %collective-permute-start.5 = (f32[1,12672]{1,0:T(1,128)S(1)}, f32[1,12672]{1,0:T(1,128)S(1)}, u32[]{:S(2)}, u32[]{:S(2)}) collective-permute-start(f32[1,12672]{1,0:T(1,128)S(1)} %add.107), channel_id=1, source_target_pairs={{0,2},{1,3},{2,0},{3,1},{4,6},{5,7},{6,4},{7,5},{8,10},{9,11},{10,... | collective-permute-start | bytes 152072 | tf_op jit(solution)/shard_map/ppermute | solution.py:388
  232.9 4.1 %collective-permute-start.6 = (f32[1,12672]{1,0:T(1,128)S(1)}, f32[1,12672]{1,0:T(1,128)S(1)}, u32[]{:S(2)}, u32[]{:S(2)}) collective-permute-start(f32[1,12672]{1,0:T(1,128)S(1)} %add.108), channel_id=1, source_target_pairs={{0,4},{1,5},{2,6},{3,7},{4,0},{5,1},{6,2},{7,3},{8,12},{9,13},{10,... | collective-permute-start | bytes 152072 | tf_op jit(solution)/shard_map/ppermute | solution.py:388
  234.6 97.6 %collective-permute-start.2 = (bf16[512,2048]{1,0:T(8,128)(2,1)}, bf16[512,2048]{1,0:T(8,128)(2,1)}, u32[]{:S(2)}, u32[]{:S(2)}) collective-permute-start(bf16[512,2048]{1,0:T(8,128)(2,1)} %get-tuple-element.39.refs_1_), channel_id=1, source_target_pairs={{0,8},{8,0},{1,9},{9,1},{2,10},{10,2},{3,11},{11,3},{4,12},{12,4},... | collective-permute-start | bytes 6291464 | tf_op jit(solution)/shard_map/ppermute | solution.py:382
  239.6 87.1 %collective-permute-start.13 = (bf16[1024,512]{1,0:T(8,128)(2,1)S(1)}, bf16[1024,512]{1,0:T(8,128)(2,1)}, u32[]{:S(2)}, u32[]{:S(2)}) collective-permute-start(bf16[1024,512]{1,0:T(8,128)(2,1)S(1)} %add_convert_fusion.1), channel_id=1, source_target_pairs={{0,8},{8,0},{1,9},{9,1},{2,10},{10,2},{3,11},{11,3},{4,12},{12,4},... | collective-permute-start | bytes 3145736 | tf_op jit(solution)/shard_map/ppermute | solution.py:382
  241.4 22.6 %copy-start.1 = (f32[1024,512]{1,0:T(8,128)S(1)}, f32[1024,512]{1,0:T(8,128)}, u32[]{:S(2)}) copy-start(f32[1024,512]{1,0:T(8,128)} %get-tuple-element.62) | copy-start | bytes 6291460
  256.8 9.8 %copy-start.4 = (f32[1,2304]{1,0:T(1,128)S(1)}, f32[1,2304]{1,0:T(1,128)}, u32[]{:S(2)}) copy-start(f32[1,2304]{1,0:T(1,128)} %copy-done.3) | copy-start | bytes 27652
  256.8 1.4 collective-permute-start.7
  258.9 3.6 collective-permute-start.8
  262.6 4.7 %collective-permute-start.9 = (f32[8,128]{1,0:T(8,128)S(1)}, f32[8,128]{1,0:T(8,128)S(1)}, u32[]{:S(2)}, u32[]{:S(2)}) collective-permute-start(f32[8,128]{1,0:T(8,128)S(1)} %add.111), channel_id=1, source_target_pairs={{0,4},{1,5},{2,6},{3,7},{4,0},{5,1},{6,2},{7,3},{8,12},{9,13},{10,... | collective-permute-start | bytes 12296 | tf_op jit(solution)/shard_map/ppermute | solution.py:388
  266.0 65.2 %collective-permute-start.14 = (bf16[1024,512]{1,0:T(8,128)(2,1)S(1)}, bf16[1024,512]{1,0:T(8,128)(2,1)S(1)}, u32[]{:S(2)}, u32[]{:S(2)}) collective-permute-start(bf16[1024,512]{1,0:T(8,128)(2,1)S(1)} %add_convert_fusion), channel_id=1, source_target_pairs={{0,8},{8,0},{1,9},{9,1},{2,10},{10,2},{3,11},{11,3},{4,12},{12,4},... | collective-permute-start | bytes 3145736 | tf_op jit(solution)/shard_map/ppermute | solution.py:382
  267.2 58.9 %collective-permute-start.10 = (f32[8,128]{1,0:T(8,128)S(1)}, f32[8,128]{1,0:T(8,128)S(1)}, u32[]{:S(2)}, u32[]{:S(2)}) collective-permute-start(f32[8,128]{1,0:T(8,128)S(1)} %add.112), channel_id=1, source_target_pairs={{0,8},{8,0},{1,9},{9,1},{2,10},{10,2},{3,11},{11,3},{4,12},{12,4},... | collective-permute-start | bytes 12296 | tf_op jit(solution)/shard_map/ppermute | solution.py:382
Sparse Core Ops, SparseCore 0:
  59.4 87.2 all-gather.1

commit v6 on v5

--- a/solution.py
+++ b/solution.py
@@ -7,6 +7,7 @@
 from jax.experimental.pallas import tpu as pltpu
 from jax.sharding import PartitionSpec as P
 
+
 EPS_ONE = 1e-30
 EPS_TWO = 1e-3
 F32 = jnp.float32
@@ -27,48 +28,30 @@
     return jnp.sum((v * v).reshape(v.shape[0] // 8, 8, v.shape[1]), axis=0)
 
 
-def cast_kernel(first, w_ref, a_ref, b_ref, s_ref):
-    step = pl.program_id(0)
+def cast_kernel(w_ref, b_ref, s_ref):
     w = w_ref[...]
-
-    @pl.when(step < first)
-    def _():
-        a_ref[...] = w.astype(BF16)
-
-    @pl.when(step >= first)
-    def _():
-        b_ref[...] = w.astype(BF16)
-
-    @pl.when(step == 0)
+    b_ref[...] = w.astype(BF16)
+
+    @pl.when(pl.program_id(0) == 0)
     def _():
         s_ref[...] = jnp.zeros_like(s_ref)
 
     s_ref[...] += fold_squares(w)
 
 
-def cast_weight(w, cut):
+def cast_weight(w):
     rows, cols = w.shape
     tile = 256
-    first = cut // tile
-    a, b, s = pl.pallas_call(
-        functools.partial(cast_kernel, first),
+    return pl.pallas_call(
+        cast_kernel,
         grid=(rows // tile,),
         in_specs=[pl.BlockSpec((tile, cols), lambda i: (i, 0))],
-        out_specs=[
-            pl.BlockSpec((tile, cols), lambda i: (jnp.minimum(i, first - 1), 0)),
-            pl.BlockSpec((tile, cols), lambda i: (jnp.maximum(i - first, 0), 0)),
-            pl.BlockSpec((8, cols), lambda i: (0, 0)),
-        ],
-        out_shape=[
-            jax.ShapeDtypeStruct((cut, cols), BF16),
-            jax.ShapeDtypeStruct((rows - cut, cols), BF16),
-            jax.ShapeDtypeStruct((8, cols), F32),
-        ],
+        out_specs=[pl.BlockSpec((tile, cols), lambda i: (i, 0)), pl.BlockSpec((8, cols), lambda i: (0, 0))],
+        out_shape=[jax.ShapeDtypeStruct((rows, cols), BF16), jax.ShapeDtypeStruct((8, cols), F32)],
         compiler_params=params('arbitrary'),
         cost_estimate=cost(w.size * 1000, w.size * 6),
         name='cast_weight',
     )(w)
-    return a, b, s
 
 
 def grad_block(xt_ref, dy_ref, g_ref, row_ref, col_ref):
@@ -141,12 +124,12 @@
 
 
 def norm_kernel(chunk, start_ref, dyg_ref, dyu_ref, wg_ref, wu_ref, *refs):
-    out, squares, (acc_ref, wb_ref, stage_ref, sems) = refs[:4], refs[4:6], refs[6:]
+    out, squares, (acc_ref, wb_ref, stage_ref, sems) = refs[:-6], refs[-6:-4], refs[-4:]
     step = pl.program_id(0)
     weights = (wg_ref, wu_ref)
     chunks = wg_ref.shape[1] // chunk
     slots = stage_ref.shape[0]
-    per_out = pl.num_programs(0) // 4
+    tile = dyg_ref.shape[0]
 
     def fetch(matrix, c):
         slot = lax.rem(matrix * chunks + c, slots)
@@ -186,23 +169,25 @@
         acc_ref[...] = lax.dot_general(dyg_ref[...], wb_ref[0], NT, preferred_element_type=F32) + lax.dot_general(
             dyu_ref[...], wb_ref[1], NT, preferred_element_type=F32)
 
-    for k in range(4):
-        @pl.when((step >= k * per_out) & (step < (k + 1) * per_out))
-        def _():
-            out[k][...] = acc_ref[...]
-
-
-def norm_partial(first, dyg, dyu, wg, wu):
+    at = 0
+    for ref in out:
+        for lo in range(at - at % tile, at + ref.shape[0], tile):
+            first, last = max(lo, at), min(lo + tile, at + ref.shape[0])
+
+            @pl.when(step == lo // tile)
+            def _():
+                ref[first - at:last - at, :] = acc_ref[first - lo:last - lo, :]
+
+        at += ref.shape[0]
+
+
+def norm_partial(first, dyg, dyu, wg, wu, counts):
     tile, chunk, slots = 512, 1024, 3
     tokens, n = dyg.shape
     m = wg.shape[0]
     tiles = tokens // tile
-    per_out = tiles // 4
     dy_spec = pl.BlockSpec((tile, n), lambda i, start: (lax.rem(i + start[0], tiles), 0))
     any_spec = pl.BlockSpec(memory_space=pl.ANY)
-
-    def block(k):
-        return lambda i, start: (jnp.clip(i - k * per_out, 0, per_out - 1), 0)
 
     out = pl.pallas_call(
         functools.partial(norm_kernel, chunk),
@@ -210,7 +195,7 @@
             num_scalar_prefetch=1,
             grid=(tiles,),
             in_specs=[dy_spec, dy_spec, any_spec, any_spec],
-            out_specs=[pl.BlockSpec((tile, m), block(k)) for k in range(4)]
+            out_specs=[pl.BlockSpec((c, m), lambda i, start: (0, 0)) for c in counts]
             + [pl.BlockSpec((8, chunk), lambda i, start: (0, 0))] * 2,
             scratch_shapes=[
                 pltpu.VMEM((tile, m), F32),
@@ -219,7 +204,7 @@
                 pltpu.SemaphoreType.DMA((slots,)),
             ],
         ),
-        out_shape=[jax.ShapeDtypeStruct((tokens // 4, m), F32)] * 4 + [jax.ShapeDtypeStruct((8, chunk), F32)] * 2,
+        out_shape=[jax.ShapeDtypeStruct((c, m), F32) for c in counts] + [jax.ShapeDtypeStruct((8, chunk), F32)] * 2,
         compiler_params=params('arbitrary'),
         cost_estimate=cost(4 * tokens * m * n, 4 * tokens * n + 8 * m * n + 4 * tokens * m),
         name='norm_partial',
@@ -306,36 +291,44 @@
     return out[:3], out[3], out[4]
 
 
-def act_kernel(parts, total, hyper_ref, dya_ref, dyb_ref, *refs):
-    w_refs, refs = refs[:2 * parts], refs[2 * parts:]
+def act_kernel(pieces, total, row_ref, hyper_ref, dya_ref, *refs):
+    piece_refs, refs = refs[:pieces], refs[pieces:]
+    wa_ref, wb_ref, refs = refs[0], refs[1], refs[2:]
     weights, grads, c_new, (ratio_ref, sum_ref) = refs[:3], refs[3:6], refs[6:9], refs[9:11]
-    out_ref, new, (acc_ref, scale_ref) = refs[11], refs[12:15], refs[15:]
+    out_ref, new, (acc_ref, scale_ref, dyb_ref, sems) = refs[11], refs[12:15], refs[15:]
     step = pl.program_id(0)
+    slot = lax.rem(step, 2)
+
+    def fetch(i):
+        source = lax.bitwise_xor(i, row_ref[0])
+        for k, piece in enumerate(piece_refs):
+            @pl.when(source == k)
+            def _():
+                pltpu.make_async_copy(piece, dyb_ref.at[lax.rem(i, 2)], sems.at[lax.rem(i, 2)]).start()
 
     @pl.when(step == 0)
     def _():
+        fetch(step)
         mean = jnp.sum(sum_ref[...], axis=1, keepdims=True) / total
         for k in range(3):
             rms_u, rms_w = jnp.sqrt(mean[k:k + 1]), jnp.sqrt(mean[3 + k:4 + k])
             scale = hyper_ref[1] * jnp.maximum(EPS_TWO, rms_w) / jnp.maximum(1.0, rms_u / hyper_ref[2])
             scale_ref[k] = jnp.broadcast_to(scale, (8, 128))
 
-    def halves(dy_ref, refs):
-        done = 0
-        for w_ref in refs:
-            yield slice(done, done + w_ref.shape[0]), lax.dot_general(
-                dy_ref[...], w_ref[...], NT, preferred_element_type=F32)
-            done += w_ref.shape[0]
+    @pl.when(step + 1 < pl.num_programs(0))
+    def _():
+        fetch(step + 1)
 
     @pl.when(step >= 0)
     def _():
-        for cols, part in halves(dya_ref, w_refs[:parts]):
-            acc_ref[:, cols] = part
+        acc_ref[...] = lax.dot_general(dya_ref[...], wa_ref[...], NT, preferred_element_type=F32)
+
+    pltpu.make_async_copy(piece_refs[0], dyb_ref.at[slot], sems.at[slot]).wait()
 
     @pl.when(step < pl.num_programs(0))
     def _():
-        for cols, part in halves(dyb_ref, w_refs[parts:]):
-            out_ref[:, cols] = (acc_ref[:, cols] + part).astype(BF16)
+        other = lax.dot_general(dyb_ref[slot], wb_ref[...], NT, preferred_element_type=F32)
+        out_ref[...] = (acc_ref[...] + other).astype(BF16)
 
     start = 0
     for k in range(3):
@@ -352,29 +345,35 @@
         start += tile * pl.num_programs(0)
 
 
-def act_and_update(hyper_params, dya, dyb, wa, wb, weights, grads, c_new, ratio, sums, total):
-    tile = 512
+def act_and_update(hyper_params, row, dya, pieces, wa, wb, weights, grads, c_new, ratio, sums, total):
+    tile = pieces[0].shape[0]
     tokens, n = dya.shape
     steps = tokens // tile
-    m = sum(w.shape[0] for w in wa)
-    dy_spec = pl.BlockSpec((tile, n), lambda i: (i, 0))
+    m = wa.shape[0]
     fixed = lambda v: pl.BlockSpec(v.shape, lambda i: (0, 0), pipeline_mode=pl.Buffered(1))
     rows = lambda v: pl.BlockSpec((v.shape[0] // steps, v.shape[1]), lambda i: (i, 0))
     size = sum(w.size for w in weights)
     out = pl.pallas_call(
-        functools.partial(act_kernel, len(wa), total),
+        functools.partial(act_kernel, len(pieces), total),
         grid=(steps,),
-        in_specs=[pl.BlockSpec(memory_space=pltpu.SMEM), dy_spec, dy_spec]
-        + [fixed(w) for w in (*wa, *wb)]
+        in_specs=[pl.BlockSpec(memory_space=pltpu.SMEM)] * 2
+        + [rows(dya)]
+        + [pl.BlockSpec(memory_space=pl.ANY)] * len(pieces)
+        + [fixed(wa), fixed(wb)]
         + [rows(v) for v in (*weights, *grads)]
         + [fixed(v) for v in (*c_new, ratio, sums)],
         out_specs=[pl.BlockSpec((tile, m), lambda i: (i, 0))] + [rows(w) for w in weights],
         out_shape=[jax.ShapeDtypeStruct((tokens, m), BF16)] + [jax.ShapeDtypeStruct(w.shape, F32) for w in weights],
-        scratch_shapes=[pltpu.VMEM((tile, m), F32), pltpu.VMEM((3, 8, 128), F32)],
+        scratch_shapes=[
+            pltpu.VMEM((tile, m), F32),
+            pltpu.VMEM((3, 8, 128), F32),
+            pltpu.VMEM((2, tile, n), BF16),
+            pltpu.SemaphoreType.DMA((2,)),
+        ],
         compiler_params=params('arbitrary'),
         cost_estimate=cost(4 * tokens * m * n, 4 * tokens * n + 4 * m * n + 2 * tokens * m + 12 * size),
         name='act_and_update',
-    )(hyper_params, dya, dyb, *wa, *wb, *weights, *grads, *c_new, ratio, sums)
+    )(row.astype(jnp.int32).reshape(1), hyper_params, dya, *pieces, wa, wb, *weights, *grads, *c_new, ratio, sums)
     return out[0], out[1:]
 
 
@@ -382,11 +381,15 @@
     return lax.ppermute(v, 'col', [(0, 1), (1, 0)])
 
 
+def swap_row(v, row_size, mask):
+    return lax.ppermute(v, 'row', [(i, i ^ mask) for i in range(row_size)])
+
+
 def sum_row(v, row_size):
-    step = 1
-    while step < row_size:
-        v = v + lax.ppermute(v, 'row', [(i, i ^ step) for i in range(row_size)])
-        step *= 2
+    step = row_size // 2
+    while step:
+        v = v + swap_row(v, row_size, step)
+        step //= 2
     return v
 
 
@@ -408,20 +411,22 @@
 
         share = tokens // row_size
         piece = lax.dynamic_slice_in_dim(dy_down, row * share, share, axis=0)
-        piece = swap_col(piece)
-        dy_down_other = lax.all_gather(piece, 'row', axis=0, tiled=True)
-        b_down_a, b_down_b, w_sq_down = cast_weight(w_down, 768)
-        o_down_a = swap_col(b_down_a)
-
+        pieces = {0: swap_col(piece)}
+        b_down, w_sq_down = cast_weight(w_down)
+        o_down = swap_col(b_down)
         (g_gate, row_gate, col_gate), (g_up, row_up, col_up) = weight_grads(x_norm, [dy_gate, dy_up], 512)
+        for mask in range(2, row_size, 2):
+            pieces[mask] = swap_row(pieces[0], row_size, mask)
+        part = (half // 8, half // 2 - half // 8, half - half // 2)
+        sent_a, sent_b, sent_c, own_ab, own_c, w_sq_gate, w_sq_up = norm_partial(
+            1 - col, dy_gate, dy_up, w_gate, w_up, (*part, half // 2, half // 2))
+        got_a = swap_col(sent_a)
         ((g_down, row_down, col_down),) = weight_grads(x_act, [dy_down], 512)
         row_all = jnp.concatenate([row_gate, row_up, row_down], axis=1)
         row_peer = swap_col(row_all)
-        o_down_b = swap_col(b_down_b)
-        sent0, sent1, own0, own1, w_sq_gate, w_sq_up = norm_partial(1 - col, dy_gate, dy_up, w_gate, w_up)
-        got0 = swap_col(sent0)
-
-        got1 = swap_col(sent1)
+        got_b = swap_col(sent_b)
+        for mask in range(0, row_size, 2):
+            pieces[mask + 1] = swap_row(pieces[mask], row_size, 1)
 
         sizes = [r_gate.shape[0], r_up.shape[0], r_down.shape[0]]
         bounds = [0, sizes[0], sizes[0] + sizes[1], sum(sizes)]
@@ -439,22 +444,23 @@
             [w_sq_gate, w_sq_up, w_sq_down], row_total)
         sums = sum_row(sums, row_size)
         sums_peer = swap_col(sums)
+        got_c = swap_col(sent_c)
         dx_act, new = act_and_update(
-            hyper_params, dy_down, dy_down_other, [b_down_a, b_down_b], [o_down_a, o_down_b],
+            hyper_params, row, dy_down, [pieces[k] for k in range(row_size)], b_down, o_down,
             [w_gate, w_up, w_down], grads, c_new, ratio, sums + sums_peer, float(row_total[0] * col_total[0]))
         r_new = [r_new[0, bounds[k]:bounds[k + 1]] for k in range(3)]
         c_new = [c[0] for c in c_new]
 
-        mine0 = (own0 + got0).astype(BF16)
-        theirs0 = swap_col(mine0)
-        mine1 = (own1 + got1).astype(BF16)
-        theirs1 = swap_col(mine1)
+        mine_ab = (own_ab + jnp.concatenate([got_a, got_b])).astype(BF16)
+        theirs_ab = swap_col(mine_ab)
+        mine_c = (own_c + got_c).astype(BF16)
+        theirs_c = swap_col(mine_c)
         dx_norm = jnp.where(
             col == 0,
-            jnp.concatenate([mine0, mine1, theirs0, theirs0]),
-            jnp.concatenate([theirs0, theirs0, mine0, mine1]),
+            jnp.concatenate([mine_ab, mine_c, theirs_ab, theirs_ab]),
+            jnp.concatenate([theirs_ab, theirs_ab, mine_ab, mine_c]),
         )
-        dx_norm = lax.dynamic_update_slice_in_dim(dx_norm, theirs1, (1 - col) * half + half // 2, axis=0)
+        dx_norm = lax.dynamic_update_slice_in_dim(dx_norm, theirs_c, (1 - col) * half + half // 2, axis=0)
         return (*new, r_new[0], c_new[0], r_new[1], c_new[1], r_new[2], c_new[2], dx_norm, dx_act)
 
     return jax.shard_map(body, mesh=mesh, in_specs=in_specs, out_specs=out_specs, check_vma=False)

time: 406 us -> 491 us (1.21)
  waiting for transfers between devices: 112 us -> 209 us
  between operations: 14.2 us -> 1.03 us
    ppermute x9, waiting for transfers between devices: 104 us -> 154 us  [swap_col(): return lax.ppermute(v, 'col', [(0, 1), (1, 0)])]
    ppermute x6 -> x13, waiting for transfers between devices: 8.08 us -> 55.8 us  [swap_row(): return lax.ppermute(v, 'row', [(i, i ^ mask) for i in range(row_size)])]
    ppermute x6 -> x13, starting transfers between devices: 6.51 us -> 10.6 us  [swap_row(): return lax.ppermute(v, 'row', [(i, i ^ mask) for i in range(row_size)])]
  transfers between devices with their start and end apart: 16 -> 22, of which waited for: 8 -> 11; matrix products, arithmetic and copies ran while one was open for 4% -> 3% of each run, Pallas kernels for 43% -> 35%
where the time goes in v6:
time: 491 us; the launch traced here: 490 us
  Pallas kernels  238 us (48%)
  waiting for transfers between devices  209 us (43%)
  starting transfers between devices  22.3 us (5%)
  other arithmetic  10.9 us (2%)
  local copies, waits for them, and re-layouts  8.11 us (2%)
    ppermute x9, waiting for transfers between devices, swap_col(): return lax.ppermute(v, 'col', [(0, 1), (1, 0)])  154 us
    pallas_call x2, Pallas kernels, weight_grads(): pl.pallas_call(functools.partial(grad_kernel, count, steps), grid=(steps...  90.3 us
    pallas_call x1, Pallas kernels, act_and_update(): pl.pallas_call(functools.partial(act_kernel, len(pieces), total), grid=(s...  65.1 us
    pallas_call x1, Pallas kernels, norm_partial(): pl.pallas_call(functools.partial(norm_kernel, chunk), grid_spec=pltpu.Pre...  59.5 us
    ppermute x13, waiting for transfers between devices, swap_row(): return lax.ppermute(v, 'row', [(i, i ^ mask) for i in range(row_size)])  55.8 us
    pallas_call x1, Pallas kernels, square_sums(): pl.pallas_call(functools.partial(square_kernel, row_total, [g.shape[0] fo...  15.4 us
    ppermute x9, starting transfers between devices, swap_col(): return lax.ppermute(v, 'col', [(0, 1), (1, 0)])  11.7 us
    ppermute x13, starting transfers between devices, swap_row(): return lax.ppermute(v, 'row', [(i, i ^ mask) for i in range(row_size)])  10.6 us
  transfers between devices with their start and end apart: 22, of which 11 were waited for; matrix products, arithmetic and copies ran while one was open for 3% of the time, Pallas kernels for 35%

profile of v6, /device:TPU:0, one launch (start us, length us, event | category | flops | bytes accessed | tf_op | source)
XLA Modules:
  0.0 490.1 jit_solution(5040114519986744056)
XLA Ops:
  0.6 1.8 constant_dynamic-slice_fusion
  2.5 3.3 collective-permute-start
  5.8 59.5 %norm_partial.1 = (f32[256,512]{1,0:T(8,128)}, f32[768,512]{1,0:T(8,128)}, f32[1024,512]{1,0:T(8,128)}, f32[1024,512]{1,0:T(8,128)}, f32[1024,512]{1,0:T(8,128)}, /*index=5*/f32[8,1024]{1,0:T(8,128)}, f32[8,1024]{1,0:T(8,128)}) custom-call(s32[1]{0:T(128)} %bitcast.7.start_ref, bf16[4096,5120]{1,0:T(8,128)(2,1)} %dyg_ref.1, bf16[4096,5120]{1,0:T(8,128)(2,1)} %dyu_ref.1, ...), custom_call_target="tpu_custom_call" | custom-call | flops 42949672960 | bytes 113246208 | tf_op jit(solution)/shard_map/norm_partial/pallas_call | solution.py:192
  65.4 33.3 %weight_grads.3 = (f32[1280,2048]{1,0:T(8,128)}, f32[1,1280]{1,0:T(1,128)}, f32[1,2048]{1,0:T(1,128)}) custom-call(bf16[4096,1280]{1,0:T(8,128)(2,1)} %x_ref.3, bf16[4096,2048]{1,0:T(8,128)(2,1)} %dya_ref.1), custom_call_target="tpu_custom_call" | custom-call | flops 21474836480 | bytes 37748736 | tf_op jit(solution)/shard_map/weight_grads/pallas_call | solution.py:111
  98.8 57.0 %weight_grads.2 = (f32[512,5120]{1,0:T(8,128)}, f32[1,512]{1,0:T(1,128)}, f32[1,5120]{1,0:T(1,128)}, f32[512,5120]{1,0:T(8,128)}, f32[1,512]{1,0:T(1,128)}, /*index=5*/f32[1,5120]{1,0:T(1,128)}) custom-call(bf16[4096,512]{1,0:T(8,128)(2,1)} %x_ref.2, bf16[4096,5120]{1,0:T(8,128)(2,1)} %dyg_ref.1, bf16[4096,5120]{1,0:T(8,128)(2,1)} %dyu_ref.1), custom_call_target="tpu_custom_call" | custom-call | flops 42949672960 | bytes 113246208 | tf_op jit(solution)/shard_map/weight_grads/pallas_call | solution.py:111
  157.2 1.8 collective-permute-start.9
  160.9 1.8 collective-permute-start.10
  162.7 1.6 collective-permute-start.18
  165.1 1.8 collective-permute-start.11
  166.9 2.4 collective-permute-done.11
  169.4 8.0 %cast_weight.1 = (bf16[1280,2048]{1,0:T(8,128)(2,1)}, f32[8,2048]{1,0:T(8,128)}) custom-call(f32[1280,2048]{1,0:T(8,128)} %refs_12_.1), custom_call_target="tpu_custom_call" | custom-call | flops 2621440000 | bytes 15728640 | tf_op jit(solution)/shard_map/cast_weight/pallas_call | solution.py:45
  177.4 1.8 collective-permute-start.8
  179.9 15.4 %square_sums.1 = (f32[1,5120]{1,0:T(1,128)}, f32[1,5120]{1,0:T(1,128)}, f32[1,2048]{1,0:T(1,128)}, f32[2304,128]{1,0:T(8,128)}, f32[8,128]{1,0:T(8,128)}) custom-call(f32[3]{0:T(128)} %hyper_ref.3, f32[512,5120]{1,0:T(8,128)} %get-tuple-element.39.g0.refs_13_, f32[512,5120]{1,0:T(8,128)} %get-tuple-element.40.g1.refs_14_, ...), custom_call_target="tpu_custom_call" | custom-call | flops 7864320000 | bytes 31457280 | tf_op jit(solution)/shard_map/square_sums/pallas_call | solution.py:280
  195.2 1.6 collective-permute-start.13
  196.8 2.3 collective-permute-done.13
  199.8 1.5 collective-permute-start.14
  201.3 2.1 collective-permute-done.14
  203.4 1.2 collective-permute-done.15
  204.8 116.3 %collective-permute-done.17 = f32[256,512]{1,0:T(8,128)S(1)} collective-permute-done((f32[256,512]{1,0:T(8,128)}, f32[256,512]{1,0:T(8,128)S(1)}, u32[]{:S(2)}, u32[]{:S(2)}) %collective-permute-start.17) | collective-permute-done | bytes 524320 | tf_op jit(solution)/shard_map/ppermute | solution.py:381
  321.1 1.2 collective-permute-start.16
  322.3 1.1 copy-done.1
  323.4 2.4 fusion
  326.7 1.4 collective-permute-start.6
  328.1 1.5 collective-permute-start.4
  330.2 2.0 add_convert_fusion
  332.2 16.9 %collective-permute-done.20 = bf16[1024,512]{1,0:T(8,128)(2,1)S(1)} collective-permute-done((bf16[1024,512]{1,0:T(8,128)(2,1)S(1)}, bf16[1024,512]{1,0:T(8,128)(2,1)S(1)}, u32[]{:S(2)}, u32[]{:S(2)}) %collective-permute-start.20) | collective-permute-done | bytes 1048608 | tf_op jit(solution)/shard_map/ppermute | solution.py:381
  349.9 20.2 %collective-permute-done.21 = bf16[1024,512]{1,0:T(8,128)(2,1)S(1)} collective-permute-done((bf16[1024,512]{1,0:T(8,128)(2,1)S(1)}, bf16[1024,512]{1,0:T(8,128)(2,1)S(1)}, u32[]{:S(2)}, u32[]{:S(2)}) %collective-permute-start.21) | collective-permute-done | bytes 1048608 | tf_op jit(solution)/shard_map/ppermute | solution.py:381
  370.1 6.3 %collective-permute-done.6.refs_6_ = bf16[512,2048]{1,0:T(8,128)(2,1)} collective-permute-done((bf16[512,2048]{1,0:T(8,128)(2,1)}, bf16[512,2048]{1,0:T(8,128)(2,1)}, u32[]{:S(2)}, u32[]{:S(2)}) %collective-permute-start.6) | collective-permute-done | bytes 2097184 | tf_op jit(solution)/shard_map/ppermute | solution.py:385
  376.4 40.7 %collective-permute-done.4.refs_4_ = bf16[512,2048]{1,0:T(8,128)(2,1)} collective-permute-done((bf16[512,2048]{1,0:T(8,128)(2,1)}, bf16[512,2048]{1,0:T(8,128)(2,1)}, u32[]{:S(2)}, u32[]{:S(2)}) %collective-permute-start.4) | collective-permute-done | bytes 2097184 | tf_op jit(solution)/shard_map/ppermute | solution.py:385
  419.4 4.4 maximum_select_fusion
  423.8 1.0 constant_dynamic-update-slice_fusion.9
  424.8 65.1 %act_and_update.1 = (bf16[4096,1280]{1,0:T(8,128)(2,1)}, f32[512,5120]{1,0:T(8,128)}, f32[512,5120]{1,0:T(8,128)}, f32[1280,2048]{1,0:T(8,128)}) custom-call(s32[1]{0:T(128)} %bitcast.row_ref, f32[3]{0:T(128)} %hyper_ref.3, bf16[4096,2048]{1,0:T(8,128)(2,1)} %dya_ref.1, bf16[512,2048]{1,0:T(8,128)(2,1)} %collective-permute-done.refs_0_, ...), custom_call_target="tpu_custom_call" | custom-call | flops 42949672960 | bytes 148897792 | tf_op jit(solution)/shard_map/act_and_update/pallas_call | solution.py:356
  (65 shorter events, 10.4 us)
Async XLA Ops:
  2.5 324.2 %collective-permute-start = (bf16[512,2048]{1,0:T(8,128)(2,1)S(1)}, bf16[512,2048]{1,0:T(8,128)(2,1)}, u32[]{:S(2)}, u32[]{:S(2)}) collective-permute-start(bf16[512,2048]{1,0:T(8,128)(2,1)S(1)} %constant_dynamic-slice_fusion), channel_id=1, source_target_pairs={{0,8},{8,0},{1,9},{9,1},{2,10},{10,2},{3,11},{11,3},{4,12},{12,4},... | collective-permute-start | bytes 6291464 | tf_op jit(solution)/shard_map/ppermute | solution.py:381
  65.3 264.3 %collective-permute-start.19 = (f32[1024,512]{1,0:T(8,128)}, f32[1024,512]{1,0:T(8,128)}, u32[]{:S(2)}, u32[]{:S(2)}) collective-permute-start(f32[1024,512]{1,0:T(8,128)} %get-tuple-element.63), channel_id=1, source_target_pairs={{0,8},{8,0},{1,9},{9,1},{2,10},{10,2},{3,11},{11,3},{4,12},{12,4},... | collective-permute-start | bytes 6291464 | tf_op jit(solution)/shard_map/ppermute | solution.py:381
  98.7 58.4 %copy-start.7 = (f32[1,1280]{1,0:T(1,128)S(1)}, f32[1,1280]{1,0:T(1,128)}, u32[]{:S(2)}) copy-start(f32[1,1280]{1,0:T(1,128)} %get-tuple-element.47) | copy-start | bytes 15364
  98.7 61.7 %copy-start.5 = (f32[1,2048]{1,0:T(1,128)S(1)}, f32[1,2048]{1,0:T(1,128)}, u32[]{:S(2)}) copy-start(f32[1,2048]{1,0:T(1,128)} %get-tuple-element.44) | copy-start | bytes 24580
  98.7 61.7 %copy-start.6 = (f32[1280]{0:T(1024)S(1)}, f32[1280]{0:T(1024)}, u32[]{:S(2)}) copy-start(f32[1280]{0:T(1024)} %param.27) | copy-start | bytes 15364
  98.7 61.7 %copy-start.8 = (f32[3]{0:T(128)S(1)}, f32[3]{0:T(128)}, u32[]{:S(2)}) copy-start(f32[3]{0:T(128)} %hyper_ref.3) | copy-start | bytes 40
  98.7 62.1 %copy-start.9 = (f32[512]{0:T(512)S(1)}, f32[512]{0:T(512)}, u32[]{:S(2)}) copy-start(f32[512]{0:T(512)} %param.25) | copy-start | bytes 6148
  98.7 62.1 %copy-start.10 = (f32[512]{0:T(512)S(1)}, f32[512]{0:T(512)}, u32[]{:S(2)}) copy-start(f32[512]{0:T(512)} %param.23) | copy-start | bytes 6148
  157.2 3.7 collective-permute-start.9
  160.9 16.5 %copy-start.3 = (f32[1,2304]{1,0:T(1,128)}, f32[1,2304]{1,0:T(1,128)S(1)}, u32[]{:S(2)}) copy-start(f32[1,2304]{1,0:T(1,128)S(1)} %fusion.4.r_ref) | copy-start | bytes 27652
  160.9 4.1 collective-permute-start.10
  162.7 159.6 %collective-permute-start.18 = (f32[768,512]{1,0:T(8,128)}, f32[768,512]{1,0:T(8,128)S(1)}, u32[]{:S(2)}, u32[]{:S(2)}) collective-permute-start(f32[768,512]{1,0:T(8,128)} %get-tuple-element.61), channel_id=1, source_target_pairs={{0,8},{8,0},{1,9},{9,1},{2,10},{10,2},{3,11},{11,3},{4,12},{12,4},... | collective-permute-start | bytes 4718600 | tf_op jit(solution)/shard_map/ppermute | solution.py:381
  165.1 4.1 collective-permute-start.11
  169.3 9.9 %collective-permute-start.12 = (f32[1,12672]{1,0:T(1,128)S(1)}, f32[1,12672]{1,0:T(1,128)S(1)}, u32[]{:S(2)}, u32[]{:S(2)}) collective-permute-start(f32[1,12672]{1,0:T(1,128)S(1)} %add.108), channel_id=1, source_target_pairs={{0,1},{1,0},{2,3},{3,2},{4,5},{5,4},{6,7},{7,6},{8,9},{9,8},{10,11... | collective-permute-start | bytes 152072 | tf_op jit(solution)/shard_map/ppermute | solution.py:385
  177.4 247.4 %collective-permute-start.8 = (bf16[1280,2048]{1,0:T(8,128)(2,1)}, bf16[1280,2048]{1,0:T(8,128)(2,1)}, u32[]{:S(2)}, u32[]{:S(2)}) collective-permute-start(bf16[1280,2048]{1,0:T(8,128)(2,1)} %get-tuple-element.38.refs_8_), channel_id=1, source_target_pairs={{0,8},{8,0},{1,9},{9,1},{2,10},{10,2},{3,11},{11,3},{4,12},{12,4},... | collective-permute-start | bytes 15728648 | tf_op jit(solution)/shard_map/ppermute | solution.py:381
  195.2 134.9 %copy-start = (f32[1024,512]{1,0:T(8,128)S(1)}, f32[1024,512]{1,0:T(8,128)}, u32[]{:S(2)}) copy-start(f32[1024,512]{1,0:T(8,128)} %get-tuple-element.62) | copy-start | bytes 6291460
  195.2 3.9 collective-permute-start.13
  199.8 3.6 collective-permute-start.14
  203.4 1.2 collective-permute-start.15
  204.6 116.5 %collective-permute-start.17 = (f32[256,512]{1,0:T(8,128)}, f32[256,512]{1,0:T(8,128)S(1)}, u32[]{:S(2)}, u32[]{:S(2)}) collective-permute-start(f32[256,512]{1,0:T(8,128)} %get-tuple-element.60), channel_id=1, source_target_pairs={{0,8},{8,0},{1,9},{9,1},{2,10},{10,2},{3,11},{11,3},{4,12},{12,4},... | collective-permute-start | bytes 1572872 | tf_op jit(solution)/shard_map/ppermute | solution.py:381
  321.1 7.1 %collective-permute-start.16 = (f32[8,128]{1,0:T(8,128)S(1)}, f32[8,128]{1,0:T(8,128)S(1)}, u32[]{:S(2)}, u32[]{:S(2)}) collective-permute-start(f32[8,128]{1,0:T(8,128)S(1)} %add.112), channel_id=1, source_target_pairs={{0,8},{8,0},{1,9},{9,1},{2,10},{10,2},{3,11},{11,3},{4,12},{12,4},... | collective-permute-start | bytes 12296 | tf_op jit(solution)/shard_map/ppermute | solution.py:381
  323.4 94.2 %copy-start.4 = (f32[1,2304]{1,0:T(1,128)S(1)}, f32[1,2304]{1,0:T(1,128)}, u32[]{:S(2)}) copy-start(f32[1,2304]{1,0:T(1,128)} %copy-done.3) | copy-start | bytes 27652
  325.8 23.3 %collective-permute-start.20 = (bf16[1024,512]{1,0:T(8,128)(2,1)S(1)}, bf16[1024,512]{1,0:T(8,128)(2,1)S(1)}, u32[]{:S(2)}, u32[]{:S(2)}) collective-permute-start(bf16[1024,512]{1,0:T(8,128)(2,1)S(1)} %fusion), channel_id=1, source_target_pairs={{0,8},{8,0},{1,9},{9,1},{2,10},{10,2},{3,11},{11,3},{4,12},{12,4},... | collective-permute-start | bytes 3145736 | tf_op jit(solution)/shard_map/ppermute | solution.py:381
  326.7 49.7 %collective-permute-start.6 = (bf16[512,2048]{1,0:T(8,128)(2,1)}, bf16[512,2048]{1,0:T(8,128)(2,1)}, u32[]{:S(2)}, u32[]{:S(2)}) collective-permute-start(bf16[512,2048]{1,0:T(8,128)(2,1)} %collective-permute-done.refs_0_), channel_id=1, source_target_pairs={{0,6},{1,7},{2,4},{3,5},{4,2},{5,3},{6,0},{7,1},{8,14},{9,15},{10,... | collective-permute-start | bytes 6291464 | tf_op jit(solution)/shard_map/ppermute | solution.py:385
  328.1 89.0 %collective-permute-start.4 = (bf16[512,2048]{1,0:T(8,128)(2,1)}, bf16[512,2048]{1,0:T(8,128)(2,1)}, u32[]{:S(2)}, u32[]{:S(2)}) collective-permute-start(bf16[512,2048]{1,0:T(8,128)(2,1)} %collective-permute-done.refs_0_), channel_id=1, source_target_pairs={{0,4},{1,5},{2,6},{3,7},{4,0},{5,1},{6,2},{7,3},{8,12},{9,13},{10,... | collective-permute-start | bytes 6291464 | tf_op jit(solution)/shard_map/ppermute | solution.py:385
  329.6 87.5 %collective-permute-start.2 = (bf16[512,2048]{1,0:T(8,128)(2,1)}, bf16[512,2048]{1,0:T(8,128)(2,1)}, u32[]{:S(2)}, u32[]{:S(2)}) collective-permute-start(bf16[512,2048]{1,0:T(8,128)(2,1)} %collective-permute-done.refs_0_), channel_id=1, source_target_pairs={{0,2},{1,3},{2,0},{3,1},{4,6},{5,7},{6,4},{7,5},{8,10},{9,11},{10,... | collective-permute-start | bytes 6291464 | tf_op jit(solution)/shard_map/ppermute | solution.py:385
  349.1 21.0 %copy-start.2 = (bf16[1024,512]{1,0:T(8,128)(2,1)}, bf16[1024,512]{1,0:T(8,128)(2,1)S(1)}, u32[]{:S(2)}) copy-start(bf16[1024,512]{1,0:T(8,128)(2,1)S(1)} %collective-permute-done.20) | copy-start | bytes 3145732
  349.1 21.0 %collective-permute-start.21 = (bf16[1024,512]{1,0:T(8,128)(2,1)S(1)}, bf16[1024,512]{1,0:T(8,128)(2,1)S(1)}, u32[]{:S(2)}, u32[]{:S(2)}) collective-permute-start(bf16[1024,512]{1,0:T(8,128)(2,1)S(1)} %add_convert_fusion), channel_id=1, source_target_pairs={{0,8},{8,0},{1,9},{9,1},{2,10},{10,2},{3,11},{11,3},{4,12},{12,4},... | collective-permute-start | bytes 3145736 | tf_op jit(solution)/shard_map/ppermute | solution.py:381
  370.1 54.7 %collective-permute-start.1 = (bf16[512,2048]{1,0:T(8,128)(2,1)}, bf16[512,2048]{1,0:T(8,128)(2,1)}, u32[]{:S(2)}, u32[]{:S(2)}) collective-permute-start(bf16[512,2048]{1,0:T(8,128)(2,1)} %collective-permute-done.refs_0_), channel_id=1, source_target_pairs={{0,1},{1,0},{2,3},{3,2},{4,5},{5,4},{6,7},{7,6},{8,9},{9,8},{10,11... | collective-permute-start | bytes 6291464 | tf_op jit(solution)/shard_map/ppermute | solution.py:385
  376.4 48.4 %collective-permute-start.7 = (bf16[512,2048]{1,0:T(8,128)(2,1)}, bf16[512,2048]{1,0:T(8,128)(2,1)}, u32[]{:S(2)}, u32[]{:S(2)}) collective-permute-start(bf16[512,2048]{1,0:T(8,128)(2,1)} %collective-permute-done.6.refs_6_), channel_id=1, source_target_pairs={{0,1},{1,0},{2,3},{3,2},{4,5},{5,4},{6,7},{7,6},{8,9},{9,8},{10,11... | collective-permute-start | bytes 6291464 | tf_op jit(solution)/shard_map/ppermute | solution.py:385
  417.1 7.7 %collective-permute-start.5 = (bf16[512,2048]{1,0:T(8,128)(2,1)}, bf16[512,2048]{1,0:T(8,128)(2,1)}, u32[]{:S(2)}, u32[]{:S(2)}) collective-permute-start(bf16[512,2048]{1,0:T(8,128)(2,1)} %collective-permute-done.4.refs_4_), channel_id=1, source_target_pairs={{0,1},{1,0},{2,3},{3,2},{4,5},{5,4},{6,7},{7,6},{8,9},{9,8},{10,11... | collective-permute-start | bytes 6291464 | tf_op jit(solution)/shard_map/ppermute | solution.py:385
  417.1 7.7 %collective-permute-start.3 = (bf16[512,2048]{1,0:T(8,128)(2,1)}, bf16[512,2048]{1,0:T(8,128)(2,1)}, u32[]{:S(2)}, u32[]{:S(2)}) collective-permute-start(bf16[512,2048]{1,0:T(8,128)(2,1)} %collective-permute-done.2.refs_2_), channel_id=1, source_target_pairs={{0,1},{1,0},{2,3},{3,2},{4,5},{5,4},{6,7},{7,6},{8,9},{9,8},{10,11... | collective-permute-start | bytes 6291464 | tf_op jit(solution)/shard_map/ppermute | solution.py:385
  (1 other events, 1.1 us)

commit v7 on v6

--- a/solution.py
+++ b/solution.py
@@ -265,7 +265,7 @@
 
 
 def square_sums(hyper_params, grads, all_sums, r_new, c_old, w_sq, row_total):
-    steps = 8
+    steps = 4
     whole = lambda v: pl.BlockSpec(v.shape, lambda i: (0, 0))
     in_specs = (
         [pl.BlockSpec(memory_space=pltpu.SMEM)]
@@ -293,9 +293,9 @@
 
 def act_kernel(pieces, total, row_ref, hyper_ref, dya_ref, *refs):
     piece_refs, refs = refs[:pieces], refs[pieces:]
-    wa_ref, wb_ref, refs = refs[0], refs[1], refs[2:]
+    wa_ref, wb_hbm, refs = refs[0], refs[1], refs[2:]
     weights, grads, c_new, (ratio_ref, sum_ref) = refs[:3], refs[3:6], refs[6:9], refs[9:11]
-    out_ref, new, (acc_ref, scale_ref, dyb_ref, sems) = refs[11], refs[12:15], refs[15:]
+    out_ref, new, (acc_ref, scale_ref, dyb_ref, wb_ref, sems, w_sem) = refs[11], refs[12:15], refs[15:]
     step = pl.program_id(0)
     slot = lax.rem(step, 2)
 
@@ -306,9 +306,12 @@
             def _():
                 pltpu.make_async_copy(piece, dyb_ref.at[lax.rem(i, 2)], sems.at[lax.rem(i, 2)]).start()
 
+    w_copy = pltpu.make_async_copy(wb_hbm, wb_ref, w_sem)
+
     @pl.when(step == 0)
     def _():
         fetch(step)
+        w_copy.start()
         mean = jnp.sum(sum_ref[...], axis=1, keepdims=True) / total
         for k in range(3):
             rms_u, rms_w = jnp.sqrt(mean[k:k + 1]), jnp.sqrt(mean[3 + k:4 + k])
@@ -324,6 +327,10 @@
         acc_ref[...] = lax.dot_general(dya_ref[...], wa_ref[...], NT, preferred_element_type=F32)
 
     pltpu.make_async_copy(piece_refs[0], dyb_ref.at[slot], sems.at[slot]).wait()
+
+    @pl.when(step == 0)
+    def _():
+        w_copy.wait()
 
     @pl.when(step < pl.num_programs(0))
     def _():
@@ -359,7 +366,7 @@
         in_specs=[pl.BlockSpec(memory_space=pltpu.SMEM)] * 2
         + [rows(dya)]
         + [pl.BlockSpec(memory_space=pl.ANY)] * len(pieces)
-        + [fixed(wa), fixed(wb)]
+        + [fixed(wa), pl.BlockSpec(memory_space=pl.ANY)]
         + [rows(v) for v in (*weights, *grads)]
         + [fixed(v) for v in (*c_new, ratio, sums)],
         out_specs=[pl.BlockSpec((tile, m), lambda i: (i, 0))] + [rows(w) for w in weights],
@@ -368,7 +375,9 @@
             pltpu.VMEM((tile, m), F32),
             pltpu.VMEM((3, 8, 128), F32),
             pltpu.VMEM((2, tile, n), BF16),
+            pltpu.VMEM((m, n), BF16),
             pltpu.SemaphoreType.DMA((2,)),
+            pltpu.SemaphoreType.DMA,
         ],
         compiler_params=params('arbitrary'),
         cost_estimate=cost(4 * tokens * m * n, 4 * tokens * n + 4 * m * n + 2 * tokens * m + 12 * size),
@@ -386,11 +395,9 @@
 
 
 def sum_row(v, row_size):
-    step = row_size // 2
-    while step:
-        v = v + swap_row(v, row_size, step)
-        step //= 2
-    return v
+    x, y, far = (swap_row(v, row_size, mask) for mask in (2, 4, 6))
+    v = (v + x) + (y + far)
+    return v + swap_row(v, row_size, 1)
 
 
 def solution(mesh):
@@ -417,9 +424,10 @@
         (g_gate, row_gate, col_gate), (g_up, row_up, col_up) = weight_grads(x_norm, [dy_gate, dy_up], 512)
         for mask in range(2, row_size, 2):
             pieces[mask] = swap_row(pieces[0], row_size, mask)
-        part = (half // 8, half // 2 - half // 8, half - half // 2)
+        ahead = 1120
+        part = (256, ahead - 256, half - ahead)
         sent_a, sent_b, sent_c, own_ab, own_c, w_sq_gate, w_sq_up = norm_partial(
-            1 - col, dy_gate, dy_up, w_gate, w_up, (*part, half // 2, half // 2))
+            1 - col, dy_gate, dy_up, w_gate, w_up, (*part, ahead, half - ahead))
         got_a = swap_col(sent_a)
         ((g_down, row_down, col_down),) = weight_grads(x_act, [dy_down], 512)
         row_all = jnp.concatenate([row_gate, row_up, row_down], axis=1)
@@ -457,10 +465,10 @@
         theirs_c = swap_col(mine_c)
         dx_norm = jnp.where(
             col == 0,
-            jnp.concatenate([mine_ab, mine_c, theirs_ab, theirs_ab]),
-            jnp.concatenate([theirs_ab, theirs_ab, mine_ab, mine_c]),
+            jnp.concatenate([mine_ab, mine_c, theirs_ab, mine_c]),
+            jnp.concatenate([theirs_ab, mine_c, mine_ab, mine_c]),
         )
-        dx_norm = lax.dynamic_update_slice_in_dim(dx_norm, theirs_c, (1 - col) * half + half // 2, axis=0)
+        dx_norm = lax.dynamic_update_slice_in_dim(dx_norm, theirs_c, (1 - col) * half + ahead, axis=0)
         return (*new, r_new[0], c_new[0], r_new[1], c_new[1], r_new[2], c_new[2], dx_norm, dx_act)
 
     return jax.shard_map(body, mesh=mesh, in_specs=in_specs, out_specs=out_specs, check_vma=False)

time: 491 us -> 534 us (1.088)
  waiting for transfers between devices: 209 us -> 256 us
    ppermute x9, waiting for transfers between devices: 154 us -> 200 us  [swap_col(): return lax.ppermute(v, 'col', [(0, 1), (1, 0)])]
    ppermute x13 -> x15, starting transfers between devices: 10.6 us -> 14.2 us  [swap_row(): return lax.ppermute(v, 'row', [(i, i ^ mask) for i in range(row_size)])]
    ppermute x13 -> x15, waiting for transfers between devices: 55.8 us -> 55.4 us  [swap_row(): return lax.ppermute(v, 'row', [(i, i ^ mask) for i in range(row_size)])]
  transfers between devices with their start and end apart: 22 -> 24, of which waited for: 11 -> 12; matrix products, arithmetic and copies ran while one was open for 3% -> 3% of each run, Pallas kernels for 35% -> 32%
where the time goes in v7:
time: 534 us; the launch traced here: 533 us
  waiting for transfers between devices  256 us (48%)
  Pallas kernels  237 us (44%)
  starting transfers between devices  21.8 us (4%)
  other arithmetic  8.39 us (2%)
  local copies, waits for them, and re-layouts  8.27 us (2%)
    ppermute x9, waiting for transfers between devices, swap_col(): return lax.ppermute(v, 'col', [(0, 1), (1, 0)])  200 us
    pallas_call x2, Pallas kernels, weight_grads(): pl.pallas_call(functools.partial(grad_kernel, count, steps), grid=(steps...  90.2 us
    pallas_call x1, Pallas kernels, act_and_update(): pl.pallas_call(functools.partial(act_kernel, len(pieces), total), grid=(s...  65 us
    pallas_call x1, Pallas kernels, norm_partial(): pl.pallas_call(functools.partial(norm_kernel, chunk), grid_spec=pltpu.Pre...  59.5 us
    ppermute x15, waiting for transfers between devices, swap_row(): return lax.ppermute(v, 'row', [(i, i ^ mask) for i in range(row_size)])  55.4 us
    pallas_call x1, Pallas kernels, square_sums(): pl.pallas_call(functools.partial(square_kernel, row_total, [g.shape[0] fo...  14.6 us
    ppermute x15, starting transfers between devices, swap_row(): return lax.ppermute(v, 'row', [(i, i ^ mask) for i in range(row_size)])  14.2 us
  transfers between devices with their start and end apart: 24, of which 12 were waited for; matrix products, arithmetic and copies ran while one was open for 3% of the time, Pallas kernels for 32%

profile of v7, /device:TPU:0, one launch (start us, length us, event | category | flops | bytes accessed | tf_op | source)
XLA Modules:
  0.0 532.6 jit_solution(4867858271487005098)
XLA Ops:
  0.6 3.2 constant_dynamic-slice_fusion
  3.8 3.3 collective-permute-start
  7.1 33.1 %weight_grads.3 = (f32[1280,2048]{1,0:T(8,128)}, f32[1,1280]{1,0:T(1,128)}, f32[1,2048]{1,0:T(1,128)}) custom-call(bf16[4096,1280]{1,0:T(8,128)(2,1)} %x_ref.3, bf16[4096,2048]{1,0:T(8,128)(2,1)} %dya_ref.1), custom_call_target="tpu_custom_call" | custom-call | flops 21474836480 | bytes 37748736 | tf_op jit(solution)/shard_map/weight_grads/pallas_call | solution.py:111
  40.3 57.0 %weight_grads.2 = (f32[512,5120]{1,0:T(8,128)}, f32[1,512]{1,0:T(1,128)}, f32[1,5120]{1,0:T(1,128)}, f32[512,5120]{1,0:T(8,128)}, f32[1,512]{1,0:T(1,128)}, /*index=5*/f32[1,5120]{1,0:T(1,128)}) custom-call(bf16[4096,512]{1,0:T(8,128)(2,1)} %x_ref.2, bf16[4096,5120]{1,0:T(8,128)(2,1)} %dyg_ref.1, bf16[4096,5120]{1,0:T(8,128)(2,1)} %dyu_ref.1), custom_call_target="tpu_custom_call" | custom-call | flops 42949672960 | bytes 113246208 | tf_op jit(solution)/shard_map/weight_grads/pallas_call | solution.py:111
  99.4 0.7 constant_dynamic-update-slice_fusion.7
  100.3 2.1 collective-permute-done.9
  102.5 2.5 collective-permute-start.12
  106.0 59.5 %norm_partial.1 = (f32[256,512]{1,0:T(8,128)}, f32[864,512]{1,0:T(8,128)}, f32[928,512]{1,0:T(8,128)}, f32[1120,512]{1,0:T(8,128)}, f32[928,512]{1,0:T(8,128)}, /*index=5*/f32[8,1024]{1,0:T(8,128)}, f32[8,1024]{1,0:T(8,128)}) custom-call(s32[1]{0:T(128)} %bitcast.7.start_ref, bf16[4096,5120]{1,0:T(8,128)(2,1)} %dyg_ref.1, bf16[4096,5120]{1,0:T(8,128)(2,1)} %dyu_ref.1, ...), custom_call_target="tpu_custom_call" | custom-call | flops 42949672960 | bytes 113246208 | tf_op jit(solution)/shard_map/norm_partial/pallas_call | solution.py:192
  165.6 2.0 collective-permute-start.21
  167.7 8.0 %cast_weight.1 = (bf16[1280,2048]{1,0:T(8,128)(2,1)}, f32[8,2048]{1,0:T(8,128)}) custom-call(f32[1280,2048]{1,0:T(8,128)} %refs_12_.1), custom_call_target="tpu_custom_call" | custom-call | flops 2621440000 | bytes 15728640 | tf_op jit(solution)/shard_map/cast_weight/pallas_call | solution.py:45
  176.5 14.6 %square_sums.1 = (f32[1,5120]{1,0:T(1,128)}, f32[1,5120]{1,0:T(1,128)}, f32[1,2048]{1,0:T(1,128)}, f32[2304,128]{1,0:T(8,128)}, f32[8,128]{1,0:T(8,128)}) custom-call(f32[3]{0:T(128)} %hyper_ref.3, f32[512,5120]{1,0:T(8,128)} %get-tuple-element.39.g0.refs_13_, f32[512,5120]{1,0:T(8,128)} %get-tuple-element.40.g1.refs_14_, ...), custom_call_target="tpu_custom_call" | custom-call | flops 7864320000 | bytes 31457280 | tf_op jit(solution)/shard_map/square_sums/pallas_call | solution.py:280
  191.1 2.9 collective-permute-start.16
  194.0 1.9 collective-permute-done.16
  195.9 1.9 collective-permute-start.15
  197.8 1.9 collective-permute-done.15
  199.7 1.9 collective-permute-start.14
  201.6 1.9 collective-permute-done.14
  204.2 1.2 collective-permute-done.17
  205.4 2.0 collective-permute-start.19
  207.4 40.7 %collective-permute-done.21 = f32[928,512]{1,0:T(8,128)} collective-permute-done((f32[928,512]{1,0:T(8,128)}, f32[928,512]{1,0:T(8,128)}, u32[]{:S(2)}, u32[]{:S(2)}) %collective-permute-start.21) | collective-permute-done | bytes 1900576 | tf_op jit(solution)/shard_map/ppermute | solution.py:390
  248.1 1.9 add_convert_fusion
  250.0 119.0 %collective-permute-done.18 = f32[8,128]{1,0:T(8,128)S(1)} collective-permute-done((f32[8,128]{1,0:T(8,128)S(1)}, f32[8,128]{1,0:T(8,128)S(1)}, u32[]{:S(2)}, u32[]{:S(2)}) %collective-permute-start.18) | collective-permute-done | bytes 4128 | tf_op jit(solution)/shard_map/ppermute | solution.py:390
  369.1 2.8 collective-permute-start.6
  372.6 1.9 fusion.3
  374.5 15.6 %collective-permute-done.23 = bf16[928,512]{1,0:T(8,128)(2,1)S(1)} collective-permute-done((bf16[928,512]{1,0:T(8,128)(2,1)S(1)}, bf16[928,512]{1,0:T(8,128)(2,1)S(1)}, u32[]{:S(2)}, u32[]{:S(2)}) %collective-permute-start.23) | collective-permute-done | bytes 950304 | tf_op jit(solution)/shard_map/ppermute | solution.py:390
  390.2 23.0 %collective-permute-done.22 = bf16[1120,512]{1,0:T(8,128)(2,1)S(1)} collective-permute-done((bf16[1120,512]{1,0:T(8,128)(2,1)S(1)}, bf16[1120,512]{1,0:T(8,128)(2,1)S(1)}, u32[]{:S(2)}, u32[]{:S(2)}) %collective-permute-start.22) | collective-permute-done | bytes 1146912 | tf_op jit(solution)/shard_map/ppermute | solution.py:390
  413.2 5.6 %collective-permute-done.6.refs_6_ = bf16[512,2048]{1,0:T(8,128)(2,1)} collective-permute-done((bf16[512,2048]{1,0:T(8,128)(2,1)}, bf16[512,2048]{1,0:T(8,128)(2,1)}, u32[]{:S(2)}, u32[]{:S(2)}) %collective-permute-start.6) | collective-permute-done | bytes 2097184 | tf_op jit(solution)/shard_map/ppermute | solution.py:394
  418.8 41.2 %collective-permute-done.4.refs_4_ = bf16[512,2048]{1,0:T(8,128)(2,1)} collective-permute-done((bf16[512,2048]{1,0:T(8,128)(2,1)}, bf16[512,2048]{1,0:T(8,128)(2,1)}, u32[]{:S(2)}, u32[]{:S(2)}) %collective-permute-start.4) | collective-permute-done | bytes 2097184 | tf_op jit(solution)/shard_map/ppermute | solution.py:394
  462.3 2.5 fusion.2
  464.7 1.0 constant_dynamic-update-slice_fusion.9
  465.8 1.7 collective-permute-done.3.refs_3_
  467.5 65.0 %act_and_update.1 = (bf16[4096,1280]{1,0:T(8,128)(2,1)}, f32[512,5120]{1,0:T(8,128)}, f32[512,5120]{1,0:T(8,128)}, f32[1280,2048]{1,0:T(8,128)}) custom-call(s32[1]{0:T(128)} %bitcast.row_ref, f32[3]{0:T(128)} %hyper_ref.3, bf16[4096,2048]{1,0:T(8,128)(2,1)} %dya_ref.1, bf16[512,2048]{1,0:T(8,128)(2,1)} %collective-permute-done.refs_0_, ...), custom_call_target="tpu_custom_call" | custom-call | flops 42949672960 | bytes 148897792 | tf_op jit(solution)/shard_map/act_and_update/pallas_call | solution.py:363
  (71 shorter events, 8.2 us)
Async XLA Ops:
  3.8 365.3 %collective-permute-start = (bf16[512,2048]{1,0:T(8,128)(2,1)}, bf16[512,2048]{1,0:T(8,128)(2,1)}, u32[]{:S(2)}, u32[]{:S(2)}) collective-permute-start(bf16[512,2048]{1,0:T(8,128)(2,1)} %constant_dynamic-slice_fusion), channel_id=1, source_target_pairs={{0,8},{8,0},{1,9},{9,1},{2,10},{10,2},{3,11},{11,3},{4,12},{12,4},... | collective-permute-start | bytes 6291464 | tf_op jit(solution)/shard_map/ppermute | solution.py:390
  40.2 60.0 %copy-start.7 = (f32[1280]{0:T(1024)S(1)}, f32[1280]{0:T(1024)}, u32[]{:S(2)}) copy-start(f32[1280]{0:T(1024)} %param.27) | copy-start | bytes 15364
  40.2 60.0 %copy-start.9 = (f32[3]{0:T(128)S(1)}, f32[3]{0:T(128)}, u32[]{:S(2)}) copy-start(f32[3]{0:T(128)} %hyper_ref.3) | copy-start | bytes 40
  40.2 62.1 %copy-start.10 = (f32[512]{0:T(512)S(1)}, f32[512]{0:T(512)}, u32[]{:S(2)}) copy-start(f32[512]{0:T(512)} %param.25) | copy-start | bytes 6148
  40.3 62.1 %copy-start.11 = (f32[512]{0:T(512)S(1)}, f32[512]{0:T(512)}, u32[]{:S(2)}) copy-start(f32[512]{0:T(512)} %param.23) | copy-start | bytes 6148
  98.7 3.7 collective-permute-start.9
  102.4 63.1 %copy-start.4 = (f32[1,2304]{1,0:T(1,128)}, f32[1,2304]{1,0:T(1,128)S(1)}, u32[]{:S(2)}) copy-start(f32[1,2304]{1,0:T(1,128)S(1)} %fusion.7.r_ref) | copy-start | bytes 27652
  102.5 63.1 %collective-permute-start.12 = (f32[1,12672]{1,0:T(1,128)S(1)}, f32[1,12672]{1,0:T(1,128)S(1)}, u32[]{:S(2)}, u32[]{:S(2)}) collective-permute-start(f32[1,12672]{1,0:T(1,128)S(1)} %constant_dynamic-update-slice_fusion.3), channel_id=1, source_target_pairs={{0,6},{1,7},{2,4},{3,5},{4,2},{5,3},{6,0},{7,1},{8,14},{9,15},{10,... | collective-permute-start | bytes 152072 | tf_op jit(solution)/shard_map/ppermute | solution.py:394
  105.0 62.6 %collective-permute-start.11 = (f32[1,12672]{1,0:T(1,128)S(1)}, f32[1,12672]{1,0:T(1,128)S(1)}, u32[]{:S(2)}, u32[]{:S(2)}) collective-permute-start(f32[1,12672]{1,0:T(1,128)S(1)} %constant_dynamic-update-slice_fusion.3), channel_id=1, source_target_pairs={{0,4},{1,5},{2,6},{3,7},{4,0},{5,1},{6,2},{7,3},{8,12},{9,13},{10,... | collective-permute-start | bytes 152072 | tf_op jit(solution)/shard_map/ppermute | solution.py:394
  105.5 62.1 %collective-permute-start.10 = (f32[1,12672]{1,0:T(1,128)S(1)}, f32[1,12672]{1,0:T(1,128)S(1)}, u32[]{:S(2)}, u32[]{:S(2)}) collective-permute-start(f32[1,12672]{1,0:T(1,128)S(1)} %constant_dynamic-update-slice_fusion.3), channel_id=1, source_target_pairs={{0,2},{1,3},{2,0},{3,1},{4,6},{5,7},{6,4},{7,5},{8,10},{9,11},{10,... | collective-permute-start | bytes 152072 | tf_op jit(solution)/shard_map/ppermute | solution.py:394
  165.5 206.8 %collective-permute-start.20 = (f32[864,512]{1,0:T(8,128)}, f32[864,512]{1,0:T(8,128)}, u32[]{:S(2)}, u32[]{:S(2)}) collective-permute-start(f32[864,512]{1,0:T(8,128)} %get-tuple-element.61), channel_id=1, source_target_pairs={{0,8},{8,0},{1,9},{9,1},{2,10},{10,2},{3,11},{11,3},{4,12},{12,4},... | collective-permute-start | bytes 5308424 | tf_op jit(solution)/shard_map/ppermute | solution.py:390
  165.6 82.5 %collective-permute-start.21 = (f32[928,512]{1,0:T(8,128)}, f32[928,512]{1,0:T(8,128)}, u32[]{:S(2)}, u32[]{:S(2)}) collective-permute-start(f32[928,512]{1,0:T(8,128)} %get-tuple-element.63), channel_id=1, source_target_pairs={{0,8},{8,0},{1,9},{9,1},{2,10},{10,2},{3,11},{11,3},{4,12},{12,4},... | collective-permute-start | bytes 5701640 | tf_op jit(solution)/shard_map/ppermute | solution.py:390
  167.7 8.1 %collective-permute-start.13 = (f32[1,12672]{1,0:T(1,128)S(1)}, f32[1,12672]{1,0:T(1,128)S(1)}, u32[]{:S(2)}, u32[]{:S(2)}) collective-permute-start(f32[1,12672]{1,0:T(1,128)S(1)} %add_add_fusion), channel_id=1, source_target_pairs={{0,1},{1,0},{2,3},{3,2},{4,5},{5,4},{6,7},{7,6},{8,9},{9,8},{10,11... | collective-permute-start | bytes 152072 | tf_op jit(solution)/shard_map/ppermute | solution.py:394
  175.7 290.0 %collective-permute-start.8 = (bf16[1280,2048]{1,0:T(8,128)(2,1)}, bf16[1280,2048]{1,0:T(8,128)(2,1)}, u32[]{:S(2)}, u32[]{:S(2)}) collective-permute-start(bf16[1280,2048]{1,0:T(8,128)(2,1)} %get-tuple-element.38.refs_8_), channel_id=1, source_target_pairs={{0,8},{8,0},{1,9},{9,1},{2,10},{10,2},{3,11},{11,3},{4,12},{12,4},... | collective-permute-start | bytes 15728648 | tf_op jit(solution)/shard_map/ppermute | solution.py:390
  176.5 71.6 %copy-start.1 = (f32[928,512]{1,0:T(8,128)S(1)}, f32[928,512]{1,0:T(8,128)}, u32[]{:S(2)}) copy-start(f32[928,512]{1,0:T(8,128)} %get-tuple-element.62) | copy-start | bytes 5701636
  191.1 181.4 %copy-start = (f32[1120,512]{1,0:T(8,128)S(1)}, f32[1120,512]{1,0:T(8,128)}, u32[]{:S(2)}) copy-start(f32[1120,512]{1,0:T(8,128)} %get-tuple-element.59) | copy-start | bytes 6881284
  191.1 4.8 collective-permute-start.16
  195.9 3.8 collective-permute-start.15
  199.7 3.8 collective-permute-start.14
  204.2 1.2 collective-permute-start.17
  205.4 166.5 %collective-permute-start.19 = (f32[256,512]{1,0:T(8,128)S(1)}, f32[256,512]{1,0:T(8,128)S(1)}, u32[]{:S(2)}, u32[]{:S(2)}) collective-permute-start(f32[256,512]{1,0:T(8,128)S(1)} %copy-done.12), channel_id=1, source_target_pairs={{0,8},{8,0},{1,9},{9,1},{2,10},{10,2},{3,11},{11,3},{4,12},{12,4},... | collective-permute-start | bytes 1572872 | tf_op jit(solution)/shard_map/ppermute | solution.py:390
  248.1 120.9 %collective-permute-start.18 = (f32[8,128]{1,0:T(8,128)S(1)}, f32[8,128]{1,0:T(8,128)S(1)}, u32[]{:S(2)}, u32[]{:S(2)}) collective-permute-start(f32[8,128]{1,0:T(8,128)S(1)} %add.120), channel_id=1, source_target_pairs={{0,8},{8,0},{1,9},{9,1},{2,10},{10,2},{3,11},{11,3},{4,12},{12,4},... | collective-permute-start | bytes 12296 | tf_op jit(solution)/shard_map/ppermute | solution.py:390
  248.1 212.4 %copy-start.5 = (f32[1,2304]{1,0:T(1,128)S(1)}, f32[1,2304]{1,0:T(1,128)}, u32[]{:S(2)}) copy-start(f32[1,2304]{1,0:T(1,128)} %copy-done.4) | copy-start | bytes 27652
  369.0 21.1 %collective-permute-start.23 = (bf16[928,512]{1,0:T(8,128)(2,1)S(1)}, bf16[928,512]{1,0:T(8,128)(2,1)S(1)}, u32[]{:S(2)}, u32[]{:S(2)}) collective-permute-start(bf16[928,512]{1,0:T(8,128)(2,1)S(1)} %add_convert_fusion), channel_id=1, source_target_pairs={{0,8},{8,0},{1,9},{9,1},{2,10},{10,2},{3,11},{11,3},{4,12},{12,4},... | collective-permute-start | bytes 2850824 | tf_op jit(solution)/shard_map/ppermute | solution.py:390
  369.1 49.7 %collective-permute-start.6 = (bf16[512,2048]{1,0:T(8,128)(2,1)}, bf16[512,2048]{1,0:T(8,128)(2,1)}, u32[]{:S(2)}, u32[]{:S(2)}) collective-permute-start(bf16[512,2048]{1,0:T(8,128)(2,1)} %collective-permute-done.refs_0_), channel_id=1, source_target_pairs={{0,6},{1,7},{2,4},{3,5},{4,2},{5,3},{6,0},{7,1},{8,14},{9,15},{10,... | collective-permute-start | bytes 6291464 | tf_op jit(solution)/shard_map/ppermute | solution.py:394
  371.9 88.1 %collective-permute-start.4 = (bf16[512,2048]{1,0:T(8,128)(2,1)}, bf16[512,2048]{1,0:T(8,128)(2,1)}, u32[]{:S(2)}, u32[]{:S(2)}) collective-permute-start(bf16[512,2048]{1,0:T(8,128)(2,1)} %collective-permute-done.refs_0_), channel_id=1, source_target_pairs={{0,4},{1,5},{2,6},{3,7},{4,0},{5,1},{6,2},{7,3},{8,12},{9,13},{10,... | collective-permute-start | bytes 6291464 | tf_op jit(solution)/shard_map/ppermute | solution.py:394
  372.4 87.6 %collective-permute-start.2 = (bf16[512,2048]{1,0:T(8,128)(2,1)}, bf16[512,2048]{1,0:T(8,128)(2,1)}, u32[]{:S(2)}, u32[]{:S(2)}) collective-permute-start(bf16[512,2048]{1,0:T(8,128)(2,1)} %collective-permute-done.refs_0_), channel_id=1, source_target_pairs={{0,2},{1,3},{2,0},{3,1},{4,6},{5,7},{6,4},{7,5},{8,10},{9,11},{10,... | collective-permute-start | bytes 6291464 | tf_op jit(solution)/shard_map/ppermute | solution.py:394
  390.1 23.1 %collective-permute-start.22 = (bf16[1120,512]{1,0:T(8,128)(2,1)S(1)}, bf16[1120,512]{1,0:T(8,128)(2,1)S(1)}, u32[]{:S(2)}, u32[]{:S(2)}) collective-permute-start(bf16[1120,512]{1,0:T(8,128)(2,1)S(1)} %fusion.3), channel_id=1, source_target_pairs={{0,8},{8,0},{1,9},{9,1},{2,10},{10,2},{3,11},{11,3},{4,12},{12,4},... | collective-permute-start | bytes 3440648 | tf_op jit(solution)/shard_map/ppermute | solution.py:390
  413.2 52.5 %collective-permute-start.1 = (bf16[512,2048]{1,0:T(8,128)(2,1)}, bf16[512,2048]{1,0:T(8,128)(2,1)}, u32[]{:S(2)}, u32[]{:S(2)}) collective-permute-start(bf16[512,2048]{1,0:T(8,128)(2,1)} %collective-permute-done.refs_0_), channel_id=1, source_target_pairs={{0,1},{1,0},{2,3},{3,2},{4,5},{5,4},{6,7},{7,6},{8,9},{9,8},{10,11... | collective-permute-start | bytes 6291464 | tf_op jit(solution)/shard_map/ppermute | solution.py:394
  418.8 47.0 %collective-permute-start.7 = (bf16[512,2048]{1,0:T(8,128)(2,1)}, bf16[512,2048]{1,0:T(8,128)(2,1)}, u32[]{:S(2)}, u32[]{:S(2)}) collective-permute-start(bf16[512,2048]{1,0:T(8,128)(2,1)} %collective-permute-done.6.refs_6_), channel_id=1, source_target_pairs={{0,1},{1,0},{2,3},{3,2},{4,5},{5,4},{6,7},{7,6},{8,9},{9,8},{10,11... | collective-permute-start | bytes 6291464 | tf_op jit(solution)/shard_map/ppermute | solution.py:394
  460.0 5.8 %collective-permute-start.5 = (bf16[512,2048]{1,0:T(8,128)(2,1)}, bf16[512,2048]{1,0:T(8,128)(2,1)}, u32[]{:S(2)}, u32[]{:S(2)}) collective-permute-start(bf16[512,2048]{1,0:T(8,128)(2,1)} %collective-permute-done.4.refs_4_), channel_id=1, source_target_pairs={{0,1},{1,0},{2,3},{3,2},{4,5},{5,4},{6,7},{7,6},{8,9},{9,8},{10,11... | collective-permute-start | bytes 6291464 | tf_op jit(solution)/shard_map/ppermute | solution.py:394
  460.0 7.5 %collective-permute-start.3 = (bf16[512,2048]{1,0:T(8,128)(2,1)}, bf16[512,2048]{1,0:T(8,128)(2,1)}, u32[]{:S(2)}, u32[]{:S(2)}) collective-permute-start(bf16[512,2048]{1,0:T(8,128)(2,1)} %collective-permute-done.2.refs_2_), channel_id=1, source_target_pairs={{0,1},{1,0},{2,3},{3,2},{4,5},{5,4},{6,7},{7,6},{8,9},{9,8},{10,11... | collective-permute-start | bytes 6291464 | tf_op jit(solution)/shard_map/ppermute | solution.py:394
  (5 other events, 174.7 us)

commit v8 on v7

--- a/solution.py
+++ b/solution.py
@@ -66,7 +66,7 @@
 
 
 def grad_kernel(count, steps, x_ref, *refs):
-    dy, out, xt_ref, part_ref = refs[:count], refs[count:-2], refs[-2], refs[-1]
+    dy, grads, (row_ref, col_ref, xt_ref, part_ref) = refs[:count], refs[count:-4], refs[-4:]
     step = pl.program_id(0)
 
     @pl.when(step == 0)
@@ -80,11 +80,11 @@
 
         @pl.when((step >= k * steps) & (step < (k + 1) * steps))
         def _():
-            grad_block(xt_ref, dy[k], out[3 * k], part_ref, out[3 * k + 2])
+            grad_block(xt_ref, dy[k], grads[k], part_ref, col_ref)
 
         @pl.when(step == (k + 1) * steps - 1)
         def _():
-            out[3 * k + 1][...] = jnp.sum(part_ref[...].T, axis=0, keepdims=True)
+            row_ref[...] = jnp.sum(part_ref[...].T, axis=0, keepdims=True)
 
 
 def weight_grads(x, dys, tile):
@@ -96,19 +96,15 @@
     def block(k):
         return lambda j: (0, jnp.clip(j - k * steps, 0, steps - 1))
 
-    out_specs, out_shape = [], []
-    for k in range(count):
-        out_specs += [
-            pl.BlockSpec((m, tile), block(k)),
-            pl.BlockSpec((1, m), lambda j: (0, 0)),
-            pl.BlockSpec((1, tile), block(k)),
-        ]
-        out_shape += [
-            jax.ShapeDtypeStruct((m, n), F32),
-            jax.ShapeDtypeStruct((1, m), F32),
-            jax.ShapeDtypeStruct((1, n), F32),
-        ]
-    out = pl.pallas_call(
+    out_specs = [pl.BlockSpec((m, tile), block(k)) for k in range(count)] + [
+        pl.BlockSpec((1, m), lambda j: (0, j // steps)),
+        pl.BlockSpec((1, tile), lambda j: (0, j)),
+    ]
+    out_shape = [jax.ShapeDtypeStruct((m, n), F32)] * count + [
+        jax.ShapeDtypeStruct((1, m * count), F32),
+        jax.ShapeDtypeStruct((1, n * count), F32),
+    ]
+    return pl.pallas_call(
         functools.partial(grad_kernel, count, steps),
         grid=(steps * count,),
         in_specs=[pl.BlockSpec((tokens, m), lambda j: (0, 0), pipeline_mode=pl.Buffered(1))]
@@ -120,7 +116,6 @@
         cost_estimate=cost(2 * count * tokens * m * n, count * (2 * tokens * (m + n) + 4 * m * n)),
         name='weight_grads',
     )(x, *dys)
-    return [tuple(out[3 * k:3 * k + 3]) for k in range(count)]
 
 
 def norm_kernel(chunk, start_ref, dyg_ref, dyu_ref, wg_ref, wu_ref, *refs):
@@ -421,16 +416,16 @@
         pieces = {0: swap_col(piece)}
         b_down, w_sq_down = cast_weight(w_down)
         o_down = swap_col(b_down)
-        (g_gate, row_gate, col_gate), (g_up, row_up, col_up) = weight_grads(x_norm, [dy_gate, dy_up], 512)
+        g_gate, g_up, row_in, col_in = weight_grads(x_norm, [dy_gate, dy_up], 512)
         for mask in range(2, row_size, 2):
             pieces[mask] = swap_row(pieces[0], row_size, mask)
-        ahead = 1120
-        part = (256, ahead - 256, half - ahead)
+        ahead = 992
+        part = (224, ahead - 224, half - ahead)
         sent_a, sent_b, sent_c, own_ab, own_c, w_sq_gate, w_sq_up = norm_partial(
             1 - col, dy_gate, dy_up, w_gate, w_up, (*part, ahead, half - ahead))
         got_a = swap_col(sent_a)
-        ((g_down, row_down, col_down),) = weight_grads(x_act, [dy_down], 512)
-        row_all = jnp.concatenate([row_gate, row_up, row_down], axis=1)
+        g_down, row_down, col_down = weight_grads(x_act, [dy_down], 512)
+        row_all = jnp.concatenate([row_in, row_down], axis=1)
         row_peer = swap_col(row_all)
         got_b = swap_col(sent_b)
         for mask in range(0, row_size, 2):
@@ -445,7 +440,7 @@
         r_old = jnp.concatenate([r_gate, r_up, r_down])[None]
         r_new = beta_two * r_old + (1.0 - beta_two) * ((row_all + row_peer) / length.astype(F32))
         r_part = [lane_fold(r_new[:, bounds[k]:bounds[k + 1]]) for k in range(3)]
-        all_sums = sum_row(jnp.concatenate([col_gate, col_up, col_down, *r_part], axis=1), row_size)
+        all_sums = sum_row(jnp.concatenate([col_in, col_down, *r_part], axis=1), row_size)
         grads = [g_gate, g_up, g_down]
         c_new, ratio, sums = square_sums(
             hyper_params, grads, all_sums, r_new, [c_gate[None], c_up[None], c_down[None]],

time: 534 us -> 536 us (level)
  transfers between devices with their start and end apart: 24 -> 24, of which waited for: 12 -> 12; matrix products, arithmetic and copies ran while one was open for 3% -> 2% of each run, Pallas kernels for 32% -> 32%
where the time goes in v8:
time: 536 us; the launch traced here: 535 us
  waiting for transfers between devices  254 us (47%)
  Pallas kernels  237 us (44%)
  starting transfers between devices  25.3 us (5%)
  other arithmetic  9.46 us (2%)
  local copies, waits for them, and re-layouts  8.1 us (2%)
    ppermute x9, waiting for transfers between devices, swap_col(): return lax.ppermute(v, 'col', [(0, 1), (1, 0)])  199 us
    pallas_call x2, Pallas kernels, weight_grads(): pl.pallas_call(functools.partial(grad_kernel, count, steps), grid=(steps...  90.3 us
    pallas_call x1, Pallas kernels, act_and_update(): pl.pallas_call(functools.partial(act_kernel, len(pieces), total), grid=(s...  65 us
    pallas_call x1, Pallas kernels, norm_partial(): pl.pallas_call(functools.partial(norm_kernel, chunk), grid_spec=pltpu.Pre...  59.6 us
    ppermute x15, waiting for transfers between devices, swap_row(): return lax.ppermute(v, 'row', [(i, i ^ mask) for i in range(row_size)])  54.8 us
    pallas_call x1, Pallas kernels, square_sums(): pl.pallas_call(functools.partial(square_kernel, row_total, [g.shape[0] fo...  14.6 us
    ppermute x15, starting transfers between devices, swap_row(): return lax.ppermute(v, 'row', [(i, i ^ mask) for i in range(row_size)])  14.2 us
    ppermute x9, starting transfers between devices, swap_col(): return lax.ppermute(v, 'col', [(0, 1), (1, 0)])  11.2 us
  transfers between devices with their start and end apart: 24, of which 12 were waited for; matrix products, arithmetic and copies ran while one was open for 2% of the time, Pallas kernels for 32%

profile of v8, /device:TPU:0, one launch (start us, length us, event | category | flops | bytes accessed | tf_op | source)
XLA Modules:
  0.0 535.1 jit_solution(14820584843742039572)
XLA Ops:
  0.6 3.2 constant_dynamic-slice_fusion
  3.8 3.3 collective-permute-start
  7.1 33.2 %weight_grads.3 = (f32[1280,2048]{1,0:T(8,128)}, f32[1,1280]{1,0:T(1,128)}, f32[1,2048]{1,0:T(1,128)}) custom-call(bf16[4096,1280]{1,0:T(8,128)(2,1)} %x_ref.3, bf16[4096,2048]{1,0:T(8,128)(2,1)} %dya_ref.1), custom_call_target="tpu_custom_call" | custom-call | flops 21474836480 | bytes 37748736 | tf_op jit(solution)/shard_map/weight_grads/pallas_call | solution.py:107
  40.4 57.0 %weight_grads.2 = (f32[512,5120]{1,0:T(8,128)}, f32[512,5120]{1,0:T(8,128)}, f32[1,1024]{1,0:T(1,128)}, f32[1,10240]{1,0:T(1,128)}) custom-call(bf16[4096,512]{1,0:T(8,128)(2,1)} %x_ref.2, bf16[4096,5120]{1,0:T(8,128)(2,1)} %dyg_ref.1, bf16[4096,5120]{1,0:T(8,128)(2,1)} %dyu_ref.1), custom_call_target="tpu_custom_call" | custom-call | flops 42949672960 | bytes 113246208 | tf_op jit(solution)/shard_map/weight_grads/pallas_call | solution.py:107
  99.0 2.8 collective-permute-done.9
  101.9 2.5 collective-permute-start.12
  105.4 59.6 %norm_partial.1 = (f32[224,512]{1,0:T(8,128)}, f32[768,512]{1,0:T(8,128)}, f32[1056,512]{1,0:T(8,128)}, f32[992,512]{1,0:T(8,128)}, f32[1056,512]{1,0:T(8,128)}, /*index=5*/f32[8,1024]{1,0:T(8,128)}, f32[8,1024]{1,0:T(8,128)}) custom-call(s32[1]{0:T(128)} %bitcast.7.start_ref, bf16[4096,5120]{1,0:T(8,128)(2,1)} %dyg_ref.1, bf16[4096,5120]{1,0:T(8,128)(2,1)} %dyu_ref.1, ...), custom_call_target="tpu_custom_call" | custom-call | flops 42949672960 | bytes 113246208 | tf_op jit(solution)/shard_map/norm_partial/pallas_call | solution.py:187
  165.1 2.0 collective-permute-start.21
  167.2 8.0 %cast_weight.1 = (bf16[1280,2048]{1,0:T(8,128)(2,1)}, f32[8,2048]{1,0:T(8,128)}) custom-call(f32[1280,2048]{1,0:T(8,128)} %refs_12_.1), custom_call_target="tpu_custom_call" | custom-call | flops 2621440000 | bytes 15728640 | tf_op jit(solution)/shard_map/cast_weight/pallas_call | solution.py:45
  176.0 14.6 %square_sums.1 = (f32[1,5120]{1,0:T(1,128)}, f32[1,5120]{1,0:T(1,128)}, f32[1,2048]{1,0:T(1,128)}, f32[2304,128]{1,0:T(8,128)}, f32[8,128]{1,0:T(8,128)}) custom-call(f32[3]{0:T(128)} %hyper_ref.3, f32[512,5120]{1,0:T(8,128)} %get-tuple-element.37.g0.refs_13_, f32[512,5120]{1,0:T(8,128)} %get-tuple-element.38.g1.refs_14_, ...), custom_call_target="tpu_custom_call" | custom-call | flops 7864320000 | bytes 31457280 | tf_op jit(solution)/shard_map/square_sums/pallas_call | solution.py:275
  190.6 2.9 collective-permute-start.16
  193.5 1.9 collective-permute-done.16
  195.4 1.9 collective-permute-start.15
  197.3 1.9 collective-permute-done.15
  199.2 1.9 collective-permute-start.14
  201.1 1.9 collective-permute-done.14
  203.7 1.2 collective-permute-done.17
  204.9 2.0 collective-permute-start.19
  206.9 160.8 %collective-permute-done.19 = f32[224,512]{1,0:T(8,128)S(1)} collective-permute-done((f32[224,512]{1,0:T(8,128)}, f32[224,512]{1,0:T(8,128)S(1)}, u32[]{:S(2)}, u32[]{:S(2)}) %collective-permute-start.19) | collective-permute-done | bytes 458784 | tf_op jit(solution)/shard_map/ppermute | solution.py:385
  368.0 1.1 copy-done.2
  369.2 1.8 fusion.3
  370.9 1.7 collective-permute-start.22
  372.7 2.4 collective-permute-start.6
  376.2 2.0 add_convert_fusion
  378.2 15.3 %collective-permute-done.22 = bf16[992,512]{1,0:T(8,128)(2,1)S(1)} collective-permute-done((bf16[992,512]{1,0:T(8,128)(2,1)S(1)}, bf16[992,512]{1,0:T(8,128)(2,1)S(1)}, u32[]{:S(2)}, u32[]{:S(2)}) %collective-permute-start.22) | collective-permute-done | bytes 1015840 | tf_op jit(solution)/shard_map/ppermute | solution.py:385
  393.5 1.7 collective-permute-start.23
  395.2 20.0 %collective-permute-done.23 = bf16[1056,512]{1,0:T(8,128)(2,1)S(1)} collective-permute-done((bf16[1056,512]{1,0:T(8,128)(2,1)S(1)}, bf16[1056,512]{1,0:T(8,128)(2,1)S(1)}, u32[]{:S(2)}, u32[]{:S(2)}) %collective-permute-start.23) | collective-permute-done | bytes 1081376 | tf_op jit(solution)/shard_map/ppermute | solution.py:385
  415.2 7.2 %collective-permute-done.6.refs_6_ = bf16[512,2048]{1,0:T(8,128)(2,1)} collective-permute-done((bf16[512,2048]{1,0:T(8,128)(2,1)}, bf16[512,2048]{1,0:T(8,128)(2,1)}, u32[]{:S(2)}, u32[]{:S(2)}) %collective-permute-start.6) | collective-permute-done | bytes 2097184 | tf_op jit(solution)/shard_map/ppermute | solution.py:389
  422.4 40.1 %collective-permute-done.4.refs_4_ = bf16[512,2048]{1,0:T(8,128)(2,1)} collective-permute-done((bf16[512,2048]{1,0:T(8,128)(2,1)}, bf16[512,2048]{1,0:T(8,128)(2,1)}, u32[]{:S(2)}, u32[]{:S(2)}) %collective-permute-start.4) | collective-permute-done | bytes 2097184 | tf_op jit(solution)/shard_map/ppermute | solution.py:389
  464.8 3.5 fusion.2
  468.4 1.0 constant_dynamic-update-slice_fusion.7
  470.0 65.0 %act_and_update.1 = (bf16[4096,1280]{1,0:T(8,128)(2,1)}, f32[512,5120]{1,0:T(8,128)}, f32[512,5120]{1,0:T(8,128)}, f32[1280,2048]{1,0:T(8,128)}) custom-call(s32[1]{0:T(128)} %bitcast.row_ref, f32[3]{0:T(128)} %hyper_ref.3, bf16[4096,2048]{1,0:T(8,128)(2,1)} %dya_ref.1, bf16[512,2048]{1,0:T(8,128)(2,1)} %collective-permute-done.refs_0_, ...), custom_call_target="tpu_custom_call" | custom-call | flops 42949672960 | bytes 148897792 | tf_op jit(solution)/shard_map/act_and_update/pallas_call | solution.py:358
  (67 shorter events, 8.6 us)
Async XLA Ops:
  3.8 368.9 %collective-permute-start = (bf16[512,2048]{1,0:T(8,128)(2,1)}, bf16[512,2048]{1,0:T(8,128)(2,1)}, u32[]{:S(2)}, u32[]{:S(2)}) collective-permute-start(bf16[512,2048]{1,0:T(8,128)(2,1)} %constant_dynamic-slice_fusion), channel_id=1, source_target_pairs={{0,8},{8,0},{1,9},{9,1},{2,10},{10,2},{3,11},{11,3},{4,12},{12,4},... | collective-permute-start | bytes 6291464 | tf_op jit(solution)/shard_map/ppermute | solution.py:385
  40.3 58.6 %copy-start.7 = (f32[1280]{0:T(1024)S(1)}, f32[1280]{0:T(1024)}, u32[]{:S(2)}) copy-start(f32[1280]{0:T(1024)} %param.27) | copy-start | bytes 15364
  40.3 58.6 %copy-start.9 = (f32[3]{0:T(128)S(1)}, f32[3]{0:T(128)}, u32[]{:S(2)}) copy-start(f32[3]{0:T(128)} %hyper_ref.3) | copy-start | bytes 40
  40.4 61.4 %copy-start.10 = (f32[512]{0:T(512)S(1)}, f32[512]{0:T(512)}, u32[]{:S(2)}) copy-start(f32[512]{0:T(512)} %param.25) | copy-start | bytes 6148
  40.4 61.4 %copy-start.11 = (f32[512]{0:T(512)S(1)}, f32[512]{0:T(512)}, u32[]{:S(2)}) copy-start(f32[512]{0:T(512)} %param.23) | copy-start | bytes 6148
  98.1 3.7 collective-permute-start.9
  101.9 63.1 %copy-start.4 = (f32[1,2304]{1,0:T(1,128)}, f32[1,2304]{1,0:T(1,128)S(1)}, u32[]{:S(2)}) copy-start(f32[1,2304]{1,0:T(1,128)S(1)} %fusion.7.r_ref) | copy-start | bytes 27652
  101.9 63.2 %collective-permute-start.12 = (f32[1,12672]{1,0:T(1,128)S(1)}, f32[1,12672]{1,0:T(1,128)S(1)}, u32[]{:S(2)}, u32[]{:S(2)}) collective-permute-start(f32[1,12672]{1,0:T(1,128)S(1)} %constant_dynamic-update-slice_fusion.2), channel_id=1, source_target_pairs={{0,6},{1,7},{2,4},{3,5},{4,2},{5,3},{6,0},{7,1},{8,14},{9,15},{10,... | collective-permute-start | bytes 152072 | tf_op jit(solution)/shard_map/ppermute | solution.py:389
  104.4 62.7 %collective-permute-start.11 = (f32[1,12672]{1,0:T(1,128)S(1)}, f32[1,12672]{1,0:T(1,128)S(1)}, u32[]{:S(2)}, u32[]{:S(2)}) collective-permute-start(f32[1,12672]{1,0:T(1,128)S(1)} %constant_dynamic-update-slice_fusion.2), channel_id=1, source_target_pairs={{0,4},{1,5},{2,6},{3,7},{4,0},{5,1},{6,2},{7,3},{8,12},{9,13},{10,... | collective-permute-start | bytes 152072 | tf_op jit(solution)/shard_map/ppermute | solution.py:389
  104.9 62.2 %collective-permute-start.10 = (f32[1,12672]{1,0:T(1,128)S(1)}, f32[1,12672]{1,0:T(1,128)S(1)}, u32[]{:S(2)}, u32[]{:S(2)}) collective-permute-start(f32[1,12672]{1,0:T(1,128)S(1)} %constant_dynamic-update-slice_fusion.2), channel_id=1, source_target_pairs={{0,2},{1,3},{2,0},{3,1},{4,6},{5,7},{6,4},{7,5},{8,10},{9,11},{10,... | collective-permute-start | bytes 152072 | tf_op jit(solution)/shard_map/ppermute | solution.py:389
  165.0 203.0 %collective-permute-start.20 = (f32[768,512]{1,0:T(8,128)}, f32[768,512]{1,0:T(8,128)S(1)}, u32[]{:S(2)}, u32[]{:S(2)}) collective-permute-start(f32[768,512]{1,0:T(8,128)} %get-tuple-element.57), channel_id=1, source_target_pairs={{0,8},{8,0},{1,9},{9,1},{2,10},{10,2},{3,11},{11,3},{4,12},{12,4},... | collective-permute-start | bytes 4718600 | tf_op jit(solution)/shard_map/ppermute | solution.py:385
  165.1 210.6 %collective-permute-start.21 = (f32[1056,512]{1,0:T(8,128)}, f32[1056,512]{1,0:T(8,128)}, u32[]{:S(2)}, u32[]{:S(2)}) collective-permute-start(f32[1056,512]{1,0:T(8,128)} %get-tuple-element.59), channel_id=1, source_target_pairs={{0,8},{8,0},{1,9},{9,1},{2,10},{10,2},{3,11},{11,3},{4,12},{12,4},... | collective-permute-start | bytes 6488072 | tf_op jit(solution)/shard_map/ppermute | solution.py:385
  167.2 8.1 %collective-permute-start.13 = (f32[1,12672]{1,0:T(1,128)S(1)}, f32[1,12672]{1,0:T(1,128)S(1)}, u32[]{:S(2)}, u32[]{:S(2)}) collective-permute-start(f32[1,12672]{1,0:T(1,128)S(1)} %add_add_fusion), channel_id=1, source_target_pairs={{0,1},{1,0},{2,3},{3,2},{4,5},{5,4},{6,7},{7,6},{8,9},{9,8},{10,11... | collective-permute-start | bytes 152072 | tf_op jit(solution)/shard_map/ppermute | solution.py:389
  175.3 294.1 %collective-permute-start.8 = (bf16[1280,2048]{1,0:T(8,128)(2,1)}, bf16[1280,2048]{1,0:T(8,128)(2,1)}, u32[]{:S(2)}, u32[]{:S(2)}) collective-permute-start(bf16[1280,2048]{1,0:T(8,128)(2,1)} %get-tuple-element.36.refs_8_), channel_id=1, source_target_pairs={{0,8},{8,0},{1,9},{9,1},{2,10},{10,2},{3,11},{11,3},{4,12},{12,4},... | collective-permute-start | bytes 15728648 | tf_op jit(solution)/shard_map/ppermute | solution.py:385
  176.0 193.2 %copy-start.1 = (f32[992,512]{1,0:T(8,128)S(1)}, f32[992,512]{1,0:T(8,128)}, u32[]{:S(2)}) copy-start(f32[992,512]{1,0:T(8,128)} %get-tuple-element.55) | copy-start | bytes 6094852
  190.6 185.6 %copy-start = (f32[1056,512]{1,0:T(8,128)S(1)}, f32[1056,512]{1,0:T(8,128)}, u32[]{:S(2)}) copy-start(f32[1056,512]{1,0:T(8,128)} %get-tuple-element.58) | copy-start | bytes 6488068
  190.6 4.8 collective-permute-start.16
  195.4 3.8 collective-permute-start.15
  199.2 3.8 collective-permute-start.14
  203.7 1.2 collective-permute-start.17
  204.9 162.8 %collective-permute-start.19 = (f32[224,512]{1,0:T(8,128)}, f32[224,512]{1,0:T(8,128)S(1)}, u32[]{:S(2)}, u32[]{:S(2)}) collective-permute-start(f32[224,512]{1,0:T(8,128)} %get-tuple-element.56), channel_id=1, source_target_pairs={{0,8},{8,0},{1,9},{9,1},{2,10},{10,2},{3,11},{11,3},{4,12},{12,4},... | collective-permute-start | bytes 1376264 | tf_op jit(solution)/shard_map/ppermute | solution.py:385
  367.7 7.4 %collective-permute-start.18 = (f32[8,128]{1,0:T(8,128)S(1)}, f32[8,128]{1,0:T(8,128)S(1)}, u32[]{:S(2)}, u32[]{:S(2)}) collective-permute-start(f32[8,128]{1,0:T(8,128)S(1)} %add.120), channel_id=1, source_target_pairs={{0,8},{8,0},{1,9},{9,1},{2,10},{10,2},{3,11},{11,3},{4,12},{12,4},... | collective-permute-start | bytes 12296 | tf_op jit(solution)/shard_map/ppermute | solution.py:385
  369.2 93.8 %copy-start.5 = (f32[1,2304]{1,0:T(1,128)S(1)}, f32[1,2304]{1,0:T(1,128)}, u32[]{:S(2)}) copy-start(f32[1,2304]{1,0:T(1,128)} %copy-done.4) | copy-start | bytes 27652
  370.9 22.5 %collective-permute-start.22 = (bf16[992,512]{1,0:T(8,128)(2,1)S(1)}, bf16[992,512]{1,0:T(8,128)(2,1)S(1)}, u32[]{:S(2)}, u32[]{:S(2)}) collective-permute-start(bf16[992,512]{1,0:T(8,128)(2,1)S(1)} %fusion.3), channel_id=1, source_target_pairs={{0,8},{8,0},{1,9},{9,1},{2,10},{10,2},{3,11},{11,3},{4,12},{12,4},... | collective-permute-start | bytes 3047432 | tf_op jit(solution)/shard_map/ppermute | solution.py:385
  372.7 49.7 %collective-permute-start.6 = (bf16[512,2048]{1,0:T(8,128)(2,1)}, bf16[512,2048]{1,0:T(8,128)(2,1)}, u32[]{:S(2)}, u32[]{:S(2)}) collective-permute-start(bf16[512,2048]{1,0:T(8,128)(2,1)} %collective-permute-done.refs_0_), channel_id=1, source_target_pairs={{0,6},{1,7},{2,4},{3,5},{4,2},{5,3},{6,0},{7,1},{8,14},{9,15},{10,... | collective-permute-start | bytes 6291464 | tf_op jit(solution)/shard_map/ppermute | solution.py:389
  375.1 87.4 %collective-permute-start.4 = (bf16[512,2048]{1,0:T(8,128)(2,1)}, bf16[512,2048]{1,0:T(8,128)(2,1)}, u32[]{:S(2)}, u32[]{:S(2)}) collective-permute-start(bf16[512,2048]{1,0:T(8,128)(2,1)} %collective-permute-done.refs_0_), channel_id=1, source_target_pairs={{0,4},{1,5},{2,6},{3,7},{4,0},{5,1},{6,2},{7,3},{8,12},{9,13},{10,... | collective-permute-start | bytes 6291464 | tf_op jit(solution)/shard_map/ppermute | solution.py:389
  375.7 86.9 %collective-permute-start.2 = (bf16[512,2048]{1,0:T(8,128)(2,1)}, bf16[512,2048]{1,0:T(8,128)(2,1)}, u32[]{:S(2)}, u32[]{:S(2)}) collective-permute-start(bf16[512,2048]{1,0:T(8,128)(2,1)} %collective-permute-done.refs_0_), channel_id=1, source_target_pairs={{0,2},{1,3},{2,0},{3,1},{4,6},{5,7},{6,4},{7,5},{8,10},{9,11},{10,... | collective-permute-start | bytes 6291464 | tf_op jit(solution)/shard_map/ppermute | solution.py:389
  393.5 21.7 %collective-permute-start.23 = (bf16[1056,512]{1,0:T(8,128)(2,1)S(1)}, bf16[1056,512]{1,0:T(8,128)(2,1)S(1)}, u32[]{:S(2)}, u32[]{:S(2)}) collective-permute-start(bf16[1056,512]{1,0:T(8,128)(2,1)S(1)} %add_convert_fusion), channel_id=1, source_target_pairs={{0,8},{8,0},{1,9},{9,1},{2,10},{10,2},{3,11},{11,3},{4,12},{12,4},... | collective-permute-start | bytes 3244040 | tf_op jit(solution)/shard_map/ppermute | solution.py:385
  415.2 54.2 %collective-permute-start.1 = (bf16[512,2048]{1,0:T(8,128)(2,1)}, bf16[512,2048]{1,0:T(8,128)(2,1)}, u32[]{:S(2)}, u32[]{:S(2)}) collective-permute-start(bf16[512,2048]{1,0:T(8,128)(2,1)} %collective-permute-done.refs_0_), channel_id=1, source_target_pairs={{0,1},{1,0},{2,3},{3,2},{4,5},{5,4},{6,7},{7,6},{8,9},{9,8},{10,11... | collective-permute-start | bytes 6291464 | tf_op jit(solution)/shard_map/ppermute | solution.py:389
  422.4 47.0 %collective-permute-start.7 = (bf16[512,2048]{1,0:T(8,128)(2,1)}, bf16[512,2048]{1,0:T(8,128)(2,1)}, u32[]{:S(2)}, u32[]{:S(2)}) collective-permute-start(bf16[512,2048]{1,0:T(8,128)(2,1)} %collective-permute-done.6.refs_6_), channel_id=1, source_target_pairs={{0,1},{1,0},{2,3},{3,2},{4,5},{5,4},{6,7},{7,6},{8,9},{9,8},{10,11... | collective-permute-start | bytes 6291464 | tf_op jit(solution)/shard_map/ppermute | solution.py:389
  462.5 6.9 %collective-permute-start.5 = (bf16[512,2048]{1,0:T(8,128)(2,1)}, bf16[512,2048]{1,0:T(8,128)(2,1)}, u32[]{:S(2)}, u32[]{:S(2)}) collective-permute-start(bf16[512,2048]{1,0:T(8,128)(2,1)} %collective-permute-done.4.refs_4_), channel_id=1, source_target_pairs={{0,1},{1,0},{2,3},{3,2},{4,5},{5,4},{6,7},{7,6},{8,9},{9,8},{10,11... | collective-permute-start | bytes 6291464 | tf_op jit(solution)/shard_map/ppermute | solution.py:389
  462.6 7.4 %collective-permute-start.3 = (bf16[512,2048]{1,0:T(8,128)(2,1)}, bf16[512,2048]{1,0:T(8,128)(2,1)}, u32[]{:S(2)}, u32[]{:S(2)}) collective-permute-start(bf16[512,2048]{1,0:T(8,128)(2,1)} %collective-permute-done.2.refs_2_), channel_id=1, source_target_pairs={{0,1},{1,0},{2,3},{3,2},{4,5},{5,4},{6,7},{7,6},{8,9},{9,8},{10,11... | collective-permute-start | bytes 6291464 | tf_op jit(solution)/shard_map/ppermute | solution.py:389
  (4 other events, 139.3 us)
